TPU v7x, 32 devices: a whole 2x2x4 slice. The times are simulated.
32 devices in a mesh: scen: 8 (over y, x, core), base: 4 (over z).
Axes of the slice: x: 2, y: 2, z: 4, core: 2. Of those that a mesh axis runs over, the one named last changes fastest.
Arguments:
- right_sides: float32 [32, 8192], P(None, 'scen'), may hold values from -6 to 6
- base_hessian: float32 [8192], P('scen'), may hold values from 0.05 to 1
- sensitivity: float32 [16, 8192, 128], P('base', 'scen'), may hold values from -0.1875 to 0.1875
- weights: float32 [16, 128], P('base'), may hold values from 0.1 to 10
- outage_factors: float32 [16, 128], P('base'), may hold values from -1 to 1
- outaged: int32 [16], P('base'), may hold values from 0 to 127
Outputs:
- step: float32 [32, 8192], P(None, 'scen')
- flow_step: float32 [16, 32, 128], P('base')
All inputs are finite; a program needn't handle non-finite values.
Results may differ from a plain program's by a relative error of at most 0.0003.
Values sent between devices are 32-bit elements; how exact they have to be, the bound alone decides.
No kernel may reach another device: no remote copies, remote signals or barrier semaphores. Data moves between devices by JAX's collectives and lax.ppermute only.
A program may use at most 64 MiB of HBM per device.

v0:
```python
import jax
import jax.numpy as jnp
from jax import lax
from jax.sharding import PartitionSpec as P

ITERS = 5


HIGHEST_PREC = lax.Precision.HIGHEST


def contingency_terms(flows_sum, weights, selector, factors):
    outaged_flow = jnp.sum(flows_sum * selector[:, None, :], axis=2, keepdims=True)
    post_flows = flows_sum + factors[:, None, :] * outaged_flow
    weighted = weights[:, None, :] * post_flows
    outaged_sum = jnp.sum(factors[:, None, :] * weighted, axis=2, keepdims=True)
    spread_back = weighted + selector[:, None, :] * outaged_sum
    return (post_flows, weighted, spread_back)


def per_device(right_sides, base_hessian, sensitivity, weights, outage_factors, outaged):
    chosen = lax.broadcasted_iota(jnp.int32, weights.shape, 1) == outaged[:, None]
    selector = chosen.astype(jnp.float32)
    factors = jnp.where(chosen, -1.0, outage_factors)

    def squares(vector):
        return lax.psum(jnp.sum(vector * vector, axis=1), "scen")

    residual = right_sides
    direction_share = residual
    direction_full = right_sides
    solution = jnp.zeros_like(residual)
    norm_now = squares(residual)
    for iteration in range(ITERS):
        apply_partial_value = jnp.einsum(
            "knm,rn->krm", sensitivity, direction_full, precision=HIGHEST_PREC
        )
        base_term = jnp.sum(base_hessian[None, :] * direction_full * direction_full, axis=1)
        apply_flows_sum, base_curv = lax.psum((apply_partial_value, base_term), "scen")
        apply_post_flows, apply_weighted, apply_spread_back = contingency_terms(
            apply_flows_sum, weights, selector, factors
        )
        partial_image = jnp.einsum(
            "knm,krm->rn", sensitivity, apply_spread_back, precision=HIGHEST_PREC
        )
        contingent_term = jnp.sum(apply_post_flows * apply_weighted, axis=(0, 2))
        product, contingent = lax.psum((partial_image, contingent_term), "base")
        product = product + base_hessian[None, :] * direction_full
        curvature = base_curv + contingent
        product, curvature = (product, curvature)
        step_len = norm_now / curvature
        solution = solution + step_len[:, None] * direction_share
        residual = residual - step_len[:, None] * product
        if iteration + 1 < ITERS:
            norm_next = squares(residual)
            direction_share = residual + (norm_next / norm_now)[:, None] * direction_share
            direction_full = direction_share
            norm_now = norm_next
    partial_value = jnp.einsum("knm,rn->krm", sensitivity, solution, precision=HIGHEST_PREC)
    flows_sum = lax.psum(partial_value, "scen")
    post_flows, weighted, spread_back = contingency_terms(flows_sum, weights, selector, factors)
    return (solution, weighted)


def solution(mesh):
    placed = (
        P(None, "scen"),
        P("scen"),
        P("base", "scen", None),
        P("base", None),
        P("base", None),
        P("base"),
    )
    return jax.shard_map(
        per_device,
        mesh=mesh,
        in_specs=placed,
        out_specs=(P(None, "scen"), P("base", None, None)),
        check_vma=False,
    )
```

profile of v0, /device:TPU:0, one launch (start us, length us, event | category | flops | bytes accessed | tf_op | source)
XLA Modules:
  0.0 599.1 jit_solution(15261414494149478442)
XLA Ops:
  12.0 15.2 %all-reduce = (f32[32]{0:T(128)S(1)}, f32[32]{0:T(128)S(1)}) all-reduce(f32[32]{0:T(128)S(1)} %get-tuple-element.3, f32[32]{0:T(128)S(1)} %get-tuple-element.2), channel_id=1, replica_groups=mesh['scen'=8,'base'=4] {'scen'}, use_global_device_ids=true, to_apply=%region_1.2 | all-reduce | flops 64 | bytes 512 | tf_op jit(solution)/shard_map/psum | solution.py:27
  27.1 40.6 %all-reduce.12.cloned.1.call-done = f32[4,32,128]{2,1,0:T(8,128)} async-done(((f32[4,32,128]{2,1,0:T(8,128)}), f32[4,32,128]{2,1,0:T(8,128)}) %all-reduce.12.cloned.1.call-update) | async-done | bytes 65552 | tf_op jit(solution)/shard_map/psum | solution.py:39
  68.9 11.7 %psum.178 = f32[32]{0:T(128)S(1)} all-reduce(f32[32]{0:T(128)S(1)} %get-tuple-element.10), channel_id=1, replica_groups=mesh['scen'=8,'base'=4] {'base'}, use_global_device_ids=true, to_apply=%region_7.8 | all-reduce | flops 32 | bytes 256 | tf_op jit(solution)/shard_map/psum | solution.py:47
  83.4 31.4 %all-reduce.14.cloned.1.call-done = f32[32,1024]{1,0:T(8,128)} async-done(((f32[32,1024]{1,0:T(8,128)}), f32[32,1024]{1,0:T(8,128)}) %all-reduce.14.cloned.1.call-update) | async-done | bytes 131088 | tf_op jit(solution)/shard_map/psum | solution.py:47
  115.9 11.8 %psum.180 = f32[32]{0:T(128)S(1)} all-reduce(f32[32]{0:T(128)S(1)} %multiply_reduce_fusion.3), channel_id=1, replica_groups=mesh['scen'=8,'base'=4] {'scen'}, use_global_device_ids=true, to_apply=%region_11.12 | all-reduce | flops 32 | bytes 256 | tf_op jit(solution)/shard_map/psum | solution.py:27
  130.9 11.8 %psum.181 = f32[32]{0:T(128)S(1)} all-reduce(f32[32]{0:T(128)S(1)} %fusion.22), channel_id=1, replica_groups=mesh['scen'=8,'base'=4] {'scen'}, use_global_device_ids=true, to_apply=%region_13.14 | all-reduce | flops 32 | bytes 256 | tf_op jit(solution)/shard_map/psum | solution.py:39
  142.7 40.1 %all-reduce.16.cloned.1.call-done = f32[4,32,128]{2,1,0:T(8,128)} async-done(((f32[4,32,128]{2,1,0:T(8,128)}), f32[4,32,128]{2,1,0:T(8,128)}) %all-reduce.16.cloned.1.call-update) | async-done | bytes 65552 | tf_op jit(solution)/shard_map/psum | solution.py:39
  184.0 11.7 %psum.183 = f32[32]{0:T(128)S(1)} all-reduce(f32[32]{0:T(128)S(1)} %get-tuple-element.8), channel_id=1, replica_groups=mesh['scen'=8,'base'=4] {'base'}, use_global_device_ids=true, to_apply=%region_17.18 | all-reduce | flops 32 | bytes 256 | tf_op jit(solution)/shard_map/psum | solution.py:47
  198.5 31.4 %all-reduce.18.cloned.1.call-done = f32[32,1024]{1,0:T(8,128)} async-done(((f32[32,1024]{1,0:T(8,128)}), f32[32,1024]{1,0:T(8,128)}) %all-reduce.18.cloned.1.call-update) | async-done | bytes 131088 | tf_op jit(solution)/shard_map/psum | solution.py:47
  231.0 11.8 %psum.185 = f32[32]{0:T(128)S(1)} all-reduce(f32[32]{0:T(128)S(1)} %get-tuple-element.22), channel_id=1, replica_groups=mesh['scen'=8,'base'=4] {'scen'}, use_global_device_ids=true, to_apply=%region_21.22 | all-reduce | flops 32 | bytes 256 | tf_op jit(solution)/shard_map/psum | solution.py:27
  245.1 11.8 %psum.186 = f32[32]{0:T(128)S(1)} all-reduce(f32[32]{0:T(128)S(1)} %get-tuple-element.20), channel_id=1, replica_groups=mesh['scen'=8,'base'=4] {'scen'}, use_global_device_ids=true, to_apply=%region_23.24 | all-reduce | flops 32 | bytes 256 | tf_op jit(solution)/shard_map/psum | solution.py:39
  256.9 40.2 %all-reduce.20.cloned.1.call-done = f32[4,32,128]{2,1,0:T(8,128)} async-done(((f32[4,32,128]{2,1,0:T(8,128)}), f32[4,32,128]{2,1,0:T(8,128)}) %all-reduce.20.cloned.1.call-update) | async-done | bytes 65552 | tf_op jit(solution)/shard_map/psum | solution.py:39
  298.3 11.7 %psum.188 = f32[32]{0:T(128)S(1)} all-reduce(f32[32]{0:T(128)S(1)} %get-tuple-element.6), channel_id=1, replica_groups=mesh['scen'=8,'base'=4] {'base'}, use_global_device_ids=true, to_apply=%region_27.28 | all-reduce | flops 32 | bytes 256 | tf_op jit(solution)/shard_map/psum | solution.py:47
  312.8 31.4 %all-reduce.22.cloned.1.call-done = f32[32,1024]{1,0:T(8,128)} async-done(((f32[32,1024]{1,0:T(8,128)}), f32[32,1024]{1,0:T(8,128)}) %all-reduce.22.cloned.1.call-update) | async-done | bytes 131088 | tf_op jit(solution)/shard_map/psum | solution.py:47
  345.3 11.8 %psum.190 = f32[32]{0:T(128)S(1)} all-reduce(f32[32]{0:T(128)S(1)} %get-tuple-element.18), channel_id=1, replica_groups=mesh['scen'=8,'base'=4] {'scen'}, use_global_device_ids=true, to_apply=%region_31.32 | all-reduce | flops 32 | bytes 256 | tf_op jit(solution)/shard_map/psum | solution.py:27
  359.3 11.8 %psum.191 = f32[32]{0:T(128)S(1)} all-reduce(f32[32]{0:T(128)S(1)} %get-tuple-element.16), channel_id=1, replica_groups=mesh['scen'=8,'base'=4] {'scen'}, use_global_device_ids=true, to_apply=%region_33.34 | all-reduce | flops 32 | bytes 256 | tf_op jit(solution)/shard_map/psum | solution.py:39
  371.1 40.3 %all-reduce.24.cloned.1.call-done = f32[4,32,128]{2,1,0:T(8,128)} async-done(((f32[4,32,128]{2,1,0:T(8,128)}), f32[4,32,128]{2,1,0:T(8,128)}) %all-reduce.24.cloned.1.call-update) | async-done | bytes 65552 | tf_op jit(solution)/shard_map/psum | solution.py:39
  412.6 11.9 %psum.193 = f32[32]{0:T(128)S(1)} all-reduce(f32[32]{0:T(128)S(1)} %get-tuple-element.4), channel_id=1, replica_groups=mesh['scen'=8,'base'=4] {'base'}, use_global_device_ids=true, to_apply=%region_37.38 | all-reduce | flops 32 | bytes 256 | tf_op jit(solution)/shard_map/psum | solution.py:47
  427.3 31.4 %all-reduce.26.cloned.1.call-done = f32[32,1024]{1,0:T(8,128)} async-done(((f32[32,1024]{1,0:T(8,128)}), f32[32,1024]{1,0:T(8,128)}) %all-reduce.26.cloned.1.call-update) | async-done | bytes 131088 | tf_op jit(solution)/shard_map/psum | solution.py:47
  459.8 11.8 %psum.195 = f32[32]{0:T(128)S(1)} all-reduce(f32[32]{0:T(128)S(1)} %get-tuple-element.14), channel_id=1, replica_groups=mesh['scen'=8,'base'=4] {'scen'}, use_global_device_ids=true, to_apply=%region_41.42 | all-reduce | flops 32 | bytes 256 | tf_op jit(solution)/shard_map/psum | solution.py:27
  473.8 11.8 %psum.196 = f32[32]{0:T(128)S(1)} all-reduce(f32[32]{0:T(128)S(1)} %fusion.31), channel_id=1, replica_groups=mesh['scen'=8,'base'=4] {'scen'}, use_global_device_ids=true, to_apply=%region_43.44 | all-reduce | flops 32 | bytes 256 | tf_op jit(solution)/shard_map/psum | solution.py:39
  485.7 40.0 %all-reduce.28.cloned.1.call-done = f32[4,32,128]{2,1,0:T(8,128)} async-done(((f32[4,32,128]{2,1,0:T(8,128)}), f32[4,32,128]{2,1,0:T(8,128)}) %all-reduce.28.cloned.1.call-update) | async-done | bytes 65552 | tf_op jit(solution)/shard_map/psum | solution.py:39
  526.8 11.7 %psum.198 = f32[32]{0:T(128)S(1)} all-reduce(f32[32]{0:T(128)S(1)} %fusion.79), channel_id=1, replica_groups=mesh['scen'=8,'base'=4] {'base'}, use_global_device_ids=true, to_apply=%region_47.48 | all-reduce | flops 32 | bytes 256 | tf_op jit(solution)/shard_map/psum | solution.py:47
  540.6 50.0 %all-reduce.30.cloned.1.call-done = f32[4,32,128]{2,1,0:T(8,128)} async-done(((f32[4,32,128]{2,1,0:T(8,128)}), f32[4,32,128]{2,1,0:T(8,128)}) %all-reduce.30.cloned.1.call-update) | async-done | bytes 65552 | tf_op jit(solution)/shard_map/psum | solution.py:60
  (73 shorter events, 39.8 us)
Async XLA Ops:
  7.2 1.6 copy-start
  7.2 4.7 copy-start.1
  7.2 4.5 copy-start.6
  7.2 4.6 copy-start.7
  7.2 4.6 copy-start.4
  7.2 60.5 %copy-start.5 = (f32[4,128]{1,0:T(4,128)S(1)}, f32[4,128]{1,0:T(4,128)}, u32[]{:S(2)}) copy-start(f32[4,128]{1,0:T(4,128)} %param.9) | copy-start | bytes 6148
  7.2 60.5 %all-reduce.12.cloned.1.call-start = ((), (), s32[]{:S(2)}) async-start(), calls=%async_computation | async-start | bytes 131072 | tf_op jit(solution)/shard_map/psum | solution.py:39
  11.6 103.1 %all-reduce.14.cloned.1.call-start = ((), (), s32[]{:S(2)}) async-start(), calls=%async_computation.1 | async-start | bytes 262144 | tf_op jit(solution)/shard_map/psum | solution.py:47
  83.3 99.5 %all-reduce.16.cloned.1.call-start = ((), (), s32[]{:S(2)}) async-start(), calls=%async_computation.2 | async-start | bytes 131072 | tf_op jit(solution)/shard_map/psum | solution.py:39
  114.8 15.9 %copy-start.2 = (f32[32,1024]{1,0:T(8,128)S(1)}, f32[32,1024]{1,0:T(8,128)}, u32[]{:S(2)}) copy-start(f32[32,1024]{1,0:T(8,128)} %all-reduce.14.cloned.1.call-done) | copy-start | bytes 393220
  130.6 99.2 %all-reduce.18.cloned.1.call-start = ((), (), s32[]{:S(2)}) async-start(), calls=%async_computation.3 | async-start | bytes 262144 | tf_op jit(solution)/shard_map/psum | solution.py:47
  198.4 98.7 %all-reduce.20.cloned.1.call-start = ((), (), s32[]{:S(2)}) async-start(), calls=%async_computation.4 | async-start | bytes 131072 | tf_op jit(solution)/shard_map/psum | solution.py:39
  245.0 99.2 %all-reduce.22.cloned.1.call-start = ((), (), s32[]{:S(2)}) async-start(), calls=%async_computation.5 | async-start | bytes 262144 | tf_op jit(solution)/shard_map/psum | solution.py:47
  312.7 98.7 %all-reduce.24.cloned.1.call-start = ((), (), s32[]{:S(2)}) async-start(), calls=%async_computation.6 | async-start | bytes 131072 | tf_op jit(solution)/shard_map/psum | solution.py:39
  359.2 99.4 %all-reduce.26.cloned.1.call-start = ((), (), s32[]{:S(2)}) async-start(), calls=%async_computation.7 | async-start | bytes 262144 | tf_op jit(solution)/shard_map/psum | solution.py:47
  427.2 98.5 %all-reduce.28.cloned.1.call-start = ((), (), s32[]{:S(2)}) async-start(), calls=%async_computation.8 | async-start | bytes 131072 | tf_op jit(solution)/shard_map/psum | solution.py:39
  473.6 117.0 %all-reduce.30.cloned.1.call-start = ((), (), s32[]{:S(2)}) async-start(), calls=%async_computation.9 | async-start | bytes 131072 | tf_op jit(solution)/shard_map/psum | solution.py:60
  538.7 53.6 %copy-start.3 = (f32[32,1024]{1,0:T(8,128)}, f32[32,1024]{1,0:T(8,128)S(1)}, u32[]{:S(2)}) copy-start(f32[32,1024]{1,0:T(8,128)S(1)} %multiply_add_fusion.4) | copy-start | bytes 393220
Sparse Core Ops, SparseCore 0:
  11.8 55.8 all-reduce.11
  83.4 31.2 all-reduce.13
  130.8 51.9 all-reduce.15
  198.6 31.2 all-reduce.17
  245.1 51.9 all-reduce.19
  312.9 31.2 all-reduce.21
  359.4 51.9 all-reduce.23
  427.3 31.2 all-reduce.25
  473.7 51.9 all-reduce.27
  540.8 49.8 all-reduce.29
where the time goes:
time: 600 us; the launch traced here: 599 us
  waiting for transfers between devices  377 us (63%)
  blocking collectives  168 us (28%)
  matrix products  24.3 us (4%)
  between operations  14.3 us (2%)
  other arithmetic  13.3 us (2%)
    psum x5, waiting for transfers between devices, per_device(): lax.psum((apply_partial_value, base_term), 'scen')  201 us
    psum x4, waiting for transfers between devices, per_device(): product, contingent = lax.psum((partial_image, contingent_term), 'base')  125 us
    psum x5, blocking collectives, squares(): return lax.psum(jnp.sum(vector * vector, axis=1), 'scen')  62.4 us
    psum x5, blocking collectives, per_device(): product, contingent = lax.psum((partial_image, contingent_term), 'base')  58.7 us
    psum x1, waiting for transfers between devices, per_device(): flows_sum = lax.psum(partial_value, 'scen')  50 us
    psum x4, blocking collectives, per_device(): lax.psum((apply_partial_value, base_term), 'scen')  47.3 us
  transfers between devices with their start and end apart: 10, of which 10 were waited for; matrix products, arithmetic and copies ran while one was open for 0% of the time, Pallas kernels for 0%

commit v1 on v0

v1 whole, which is shorter than its diff:
```python
import functools

import jax
import jax.numpy as jnp
from jax import lax
from jax.experimental import pallas as pl
from jax.experimental.pallas import tpu as pltpu
from jax.sharding import PartitionSpec as P

ITERS = 5
LANE = 128
F32 = jnp.float32
BF16 = jnp.bfloat16
VM = pl.BlockSpec(memory_space=pltpu.VMEM)
SM = pl.BlockSpec(memory_space=pltpu.SMEM)
PARAMS = pltpu.CompilerParams(vmem_limit_bytes=24 * 1024 * 1024)


def call(body, out_shape, name, *args, scalars=0):
    specs = [VM] * (len(args) - scalars) + [SM] * scalars
    many = isinstance(out_shape, (list, tuple))
    return pl.pallas_call(
        body,
        out_shape=out_shape,
        in_specs=specs,
        out_specs=[VM] * len(out_shape) if many else VM,
        compiler_params=PARAMS,
        name=name,
    )(*args)


def struct(shape, dtype=F32):
    return jax.ShapeDtypeStruct(shape, dtype)


def split(value):
    high = value.astype(BF16)
    low = (value - high.astype(F32)).astype(BF16)
    return high, low


def stacked(value):
    high, low = split(value)
    return jnp.concatenate([high, low], axis=0)


def lane_index(shape):
    return lax.broadcasted_iota(jnp.int32, shape, 1)


def convert_body(a_ref, high_ref, low_ref):
    for k in range(a_ref.shape[0]):
        high, low = split(a_ref[k])
        high_ref[:, k * LANE:(k + 1) * LANE] = high
        low_ref[:, k * LANE:(k + 1) * LANE] = low


def convert(a):
    k, n, m = a.shape
    shape = struct((n, k * m), BF16)
    return call(convert_body, [shape, shape], "convert", a)


def dot(lhs, rhs, rhs_dim):
    return lax.dot_general(lhs, rhs, (((1,), (rhs_dim,)), ((), ())), preferred_element_type=F32)


def to_lines(vector, mats):
    rows, n = vector.shape[0], vector.shape[1] // 2
    total = None
    for half in range(2):
        pair = stacked(vector[:, half * n:(half + 1) * n])
        for part in range(2):
            out = dot(pair, mats[2 * half + part][...], 0)
            total = out if total is None else total + out
    return total[:rows] + total[rows:]


def from_lines(lines, mats):
    rows = lines.shape[0]
    pair = stacked(lines)
    halves = []
    for half in range(2):
        out = dot(pair, mats[2 * half][...], 1) + dot(pair, mats[2 * half + 1][...], 1)
        halves.append(out[:rows] + out[rows:])
    return halves


def store_flows(vector, hess, previous, mats, payload_ref):
    rows = vector.shape[0]
    lines = to_lines(vector, mats)
    conts = lines.shape[1] // LANE
    for k in range(conts):
        payload_ref[k * rows:(k + 1) * rows, :] = lines[:, k * LANE:(k + 1) * LANE]
    scaled = hess * vector
    first = jnp.sum(vector * vector, axis=1, keepdims=True)
    second = jnp.sum(scaled * vector, axis=1, keepdims=True)
    lane = lane_index((rows, LANE))
    packed = jnp.where(lane == 0, first, 0.0) + jnp.where(lane == 1, second, 0.0)
    if previous is not None:
        third = jnp.sum(scaled * previous, axis=1, keepdims=True)
        packed = packed + jnp.where(lane == 2, third, 0.0)
    payload_ref[conts * rows:(conts + 1) * rows, :] = packed


def first_body(r_ref, hess_ref, a0, a1, a2, a3, payload_ref):
    store_flows(r_ref[...], hess_ref[...], None, (a0, a1, a2, a3), payload_ref)


def step_body(za_ref, zb_ref, r_ref, p_ref, x_ref, sc_ref, hess_ref, a0, a1, a2, a3,
              payload_ref, rn_ref, pn_ref, xn_ref, alpha_ref, *, first):
    n = r_ref.shape[1]
    r = r_ref[...]
    hess = hess_ref[...]
    curved = za_ref[:, n:n + 1] + zb_ref[:, n:n + 1] + sc_ref[:, 1:2]
    alpha = sc_ref[:, 0:1] / curved
    if first:
        p = r
        xn_ref[...] = alpha * p
    else:
        p = r + sc_ref[:, 2:3] * p_ref[...]
        xn_ref[...] = x_ref[...] + alpha * p
    pn_ref[...] = p
    image = za_ref[:, :n] + zb_ref[:, :n] + hess * p
    r = r - alpha * image
    rn_ref[...] = r
    alpha_ref[...] = jnp.broadcast_to(alpha, alpha_ref.shape)
    store_flows(r, hess, p, (a0, a1, a2, a3), payload_ref)


def contingency(flows, k, w_ref, f_ref, out_ref):
    lane = lane_index((1, LANE))
    chosen = lane == out_ref[k]
    factors = jnp.where(chosen, -1.0, f_ref[k:k + 1, :])
    hit = jnp.sum(jnp.where(chosen, flows, 0.0), axis=1, keepdims=True)
    post = flows + factors * hit
    weighted = w_ref[k:k + 1, :] * post
    return chosen, factors, post, weighted


def lines_body(*refs, first, last):
    fa_ref, fb_ref, fp_ref, fx_ref, sc_ref, alpha_ref, w_ref, f_ref = refs[:8]
    mats = () if last else refs[8:12]
    out_ref = refs[8 if last else 12]
    z_ref, fpn_ref, fxn_ref, scn_ref = refs[9 if last else 13:]
    conts = w_ref.shape[0]
    rows = fa_ref.shape[0] // (conts + 1)
    top = conts * rows
    sums = fa_ref[top:, :] + fb_ref[top:, :]
    rr, base = sums[:, 0:1], sums[:, 1:2]
    if not first:
        beta = rr / sc_ref[:, 0:1]
        base = base + beta * (2.0 * sums[:, 2:3] + beta * sc_ref[:, 1:2])
        alpha = alpha_ref[:, 0:1]
    lane = lane_index((rows, LANE))
    packed = jnp.where(lane == 0, rr, 0.0) + jnp.where(lane == 1, base, 0.0)
    if not first:
        packed = packed + jnp.where(lane == 2, beta, 0.0)
    scn_ref[...] = packed
    curv = jnp.zeros((rows, 1), F32)
    backs = []
    for k in range(conts):
        span = slice(k * rows, (k + 1) * rows)
        flows = fa_ref[span, :] + fb_ref[span, :]
        if not first:
            before = fp_ref[span, :]
            fxn_ref[span, :] = fx_ref[span, :] + alpha * before
            flows = flows + beta * before
        else:
            fxn_ref[span, :] = jnp.zeros((rows, LANE), F32)
        fpn_ref[span, :] = flows
        chosen, factors, post, weighted = contingency(flows, k, w_ref, f_ref, out_ref)
        curv = curv + jnp.sum(post * weighted, axis=1, keepdims=True)
        if not last:
            total = jnp.sum(factors * weighted, axis=1, keepdims=True)
            backs.append(weighted + jnp.where(chosen, total, 0.0))
    if last:
        z_ref[...] = jnp.broadcast_to(curv, z_ref.shape)
    else:
        halves = from_lines(jnp.concatenate(backs, axis=1), mats)
        n = halves[0].shape[1]
        z_ref[:, :n] = halves[0]
        z_ref[:, n:2 * n] = halves[1]
        z_ref[:, 2 * n:] = jnp.broadcast_to(curv, (rows, LANE))


def finish_body(ca_ref, cb_ref, r_ref, p_ref, x_ref, sc_ref, fp_ref, fx_ref, w_ref, f_ref, out_ref,
                own_ref, send_ref):
    n = r_ref.shape[1] // 2
    rows = r_ref.shape[0]
    alpha = sc_ref[:, 0:1] / (ca_ref[:, 0:1] + cb_ref[:, 0:1] + sc_ref[:, 1:2])
    p = r_ref[...] + sc_ref[:, 2:3] * p_ref[...]
    x = x_ref[...] + alpha * p
    own_ref[:, :n] = x[:, :n]
    send_ref[:, :n] = x[:, n:]
    for k in range(w_ref.shape[0]):
        span = slice(k * rows, (k + 1) * rows)
        flows = fx_ref[span, :] + alpha * fp_ref[span, :]
        weighted = contingency(flows, k, w_ref, f_ref, out_ref)[3]
        own_ref[:, n + k * LANE:n + (k + 1) * LANE] = weighted
        send_ref[:, n + k * LANE:n + (k + 1) * LANE] = weighted


def place_body(own_ref, other_ref, side_ref, x_ref, w_ref):
    rows = own_ref.shape[0]
    n = x_ref.shape[1]
    side = side_ref[0]
    for which, ref in ((side, own_ref), (1 - side, other_ref)):
        at = pl.ds(pl.multiple_of(which * rows, 8), rows)
        x_ref[at, :] = ref[:, :n]
        for k in range(w_ref.shape[0]):
            w_ref[k, at, :] = ref[:, n + k * LANE:n + (k + 1) * LANE]


def per_device(right_sides, base_hessian, sensitivity, weights, outage_factors, outaged, *, scen, base):
    conts, n, lines = sensitivity.shape
    rhs = right_sides.shape[0]
    rows = rhs // 2
    outaged = outaged.astype(jnp.int32)

    def swap(value, axis, size, distance):
        return lax.ppermute(value, axis, [(i, i ^ distance) for i in range(size)])

    def butterfly(value, axis, size, distance):
        while 2 * distance < size:
            value = value + swap(value, axis, size, distance)
            distance *= 2
        return value, swap(value, axis, size, distance)

    side = lax.axis_index("scen") % 2
    other_a = swap(sensitivity, "scen", scen, 1)
    mine = lax.dynamic_slice_in_dim(right_sides, side * rows, rows, 0)
    theirs = lax.dynamic_slice_in_dim(right_sides, (1 - side) * rows, rows, 0)
    extra = jnp.concatenate([theirs, jnp.broadcast_to(base_hessian[None, :], (8, n))], axis=0)
    other = swap(extra, "scen", scen, 1)
    r = jnp.concatenate([mine, other[:rows]], axis=1)
    hess = jnp.concatenate([base_hessian[None, :], other[rows:rows + 1]], axis=1)
    mats = convert(sensitivity) + convert(other_a)

    flat = struct((conts * rows, LANE))
    state = struct((rows, 2 * n))
    scal = struct((rows, LANE))
    payload = struct(((conts + 1) * rows, LANE))
    wide = struct((rows, 2 * n + LANE))

    pay = call(first_body, payload, "first", r, hess, *mats)
    p = x = r
    fp = fx = jnp.zeros(flat.shape, F32)
    sc = alpha = jnp.zeros(scal.shape, F32)
    for it in range(ITERS):
        first, last = it == 0, it + 1 == ITERS
        fa, fb = butterfly(pay, "scen", scen, 2)
        tail = () if last else tuple(mats)
        z, fp, fx, sc = call(
            functools.partial(lines_body, first=first, last=last),
            [scal if last else wide, flat, flat, scal], "lines",
            fa, fb, fp, fx, sc, alpha, weights, outage_factors, *tail, outaged, scalars=1)
        za, zb = butterfly(z, "base", base, 1)
        if not last:
            pay, r, p, x, alpha = call(
                functools.partial(step_body, first=first),
                [payload, state, state, state, scal], "step",
                za, zb, r, p, x, sc, hess, *mats)
    both = struct((rows, n + conts * LANE))
    own, send = call(finish_body, [both, both], "finish", za, zb, r, p, x, sc, fp, fx,
                     weights, outage_factors, outaged, scalars=1)
    recv = swap(send, "scen", scen, 1)
    step, flow = call(place_body, [struct((rhs, n)), struct((conts, rhs, lines))], "place",
                      own, recv, side.astype(jnp.int32).reshape(1), scalars=1)
    return step, flow


def solution(mesh):
    placed = (
        P(None, "scen"),
        P("scen"),
        P("base", "scen", None),
        P("base", None),
        P("base", None),
        P("base"),
    )
    body = functools.partial(per_device, scen=mesh.shape["scen"], base=mesh.shape["base"])
    return jax.shard_map(
        body,
        mesh=mesh,
        in_specs=placed,
        out_specs=(P(None, "scen"), P("base", None, None)),
        check_vma=False,
    )
```

time: 600 us -> 122 us (0.20)
  waiting for transfers between devices: 377 us -> 73.3 us
  blocking collectives: 168 us -> 0 us
  starting transfers between devices: 0.41 us -> 29 us
  matrix products: 24.3 us -> 0 us
  Pallas kernels: 0 us -> 15.7 us
  between operations: 14.3 us -> 0.81 us
  other arithmetic: 13.3 us -> 0.14 us
    psum x10 -> x0, waiting for transfers between devices: 377 us -> none  [the longest x5 201 us: per_device(): lax.psum((apply_partial_value, base_term), 'scen')]
    psum x14 -> x0, blocking collectives: 168 us -> none  [the longest x5 62.4 us: squares(): return lax.psum(jnp.sum(vector * vector, axis=1), 'scen')]
    ppermute x0 -> x23, waiting for transfers between devices: none -> 73.3 us  [swap(): return lax.ppermute(value, axis, [(i, i ^ distance) for i in range(size)])]
    ppermute x0 -> x23, starting transfers between devices: none -> 29 us  [swap(): return lax.ppermute(value, axis, [(i, i ^ distance) for i in range(size)])]
    dot_general x10 -> x0, matrix products: 24.3 us -> none  [the longest x5 11.6 us: per_device(): jnp.einsum('knm,rn->krm', sensitivity, direction_full, precision=HIGHEST_...]
    pallas_call x0 -> x14, Pallas kernels: none -> 15.7 us  [call(): pl.pallas_call(body, out_shape=out_shape, in_specs=specs, out_specs=[VM]...]
    mul x6 -> x0, other arithmetic: 7.53 us -> none  [contingency_terms(): post_flows = flows_sum + factors[:, None, :] * outaged_flow]
  transfers between devices with their start and end apart: 10 -> 23, of which waited for: 10 -> 22; matrix products, arithmetic and copies ran while one was open for 0% -> 1% of each run, Pallas kernels for 0% -> 0%
where the time goes in v1:
time: 122 us
  waiting for transfers between devices  73.3 us (60%)
  starting transfers between devices  29 us (24%)
  Pallas kernels  15.7 us (13%)
  local copies, waits for them, and re-layouts  3.2 us (3%)
    ppermute x23, waiting for transfers between devices, swap(): return lax.ppermute(value, axis, [(i, i ^ distance) for i in range(size)])  73.3 us
    ppermute x23, starting transfers between devices, swap(): return lax.ppermute(value, axis, [(i, i ^ distance) for i in range(size)])  29 us
    pallas_call x14, Pallas kernels, call(): pl.pallas_call(body, out_shape=out_shape, in_specs=specs, out_specs=[VM]...  15.7 us
  transfers between devices with their start and end apart: 23, of which 22 were waited for; matrix products, arithmetic and copies ran while one was open for 1% of the time, Pallas kernels for 0%

profile of v1, /device:TPU:0, one launch (start us, length us, event | category | flops | bytes accessed | tf_op | source)
XLA Modules:
  0.0 122.2 jit_solution(16379725730934713362)
XLA Ops:
  6.7 2.9 %collective-permute-start.2 = (f32[80,128]{1,0:T(8,128)S(1)}, f32[80,128]{1,0:T(8,128)S(1)}, u32[]{:S(2)}, u32[]{:S(2)}) collective-permute-start(f32[80,128]{1,0:T(8,128)S(1)} %first.1), channel_id=1, source_target_pairs={{0,8},{4,12},{8,0},{12,4},{16,24},{20,28},{24,16},{28,20},{1,9},{5... | collective-permute-start | bytes 122888 | tf_op jit(solution)/shard_map/ppermute | solution.py:222
  11.5 2.1 %collective-permute-start.3 = (f32[80,128]{1,0:T(8,128)S(1)}, f32[80,128]{1,0:T(8,128)S(1)}, u32[]{:S(2)}, u32[]{:S(2)}) collective-permute-start(f32[80,128]{1,0:T(8,128)S(1)} %add.43.refs_0_), channel_id=1, source_target_pairs={{0,16},{4,20},{8,24},{12,28},{16,0},{20,4},{24,8},{28,12},{1,17},{... | collective-permute-start | bytes 122888 | tf_op jit(solution)/shard_map/ppermute | solution.py:222
  17.5 2.1 %collective-permute-start.4 = (f32[16,2176]{1,0:T(8,128)S(1)}, f32[16,2176]{1,0:T(8,128)S(1)}, u32[]{:S(2)}, u32[]{:S(2)}) collective-permute-start(f32[16,2176]{1,0:T(8,128)S(1)} %get-tuple-element.52), channel_id=1, source_target_pairs={{0,1},{1,0},{2,3},{3,2},{4,5},{5,4},{6,7},{7,6},{8,9},{9,8},{10,11... | collective-permute-start | bytes 417800 | tf_op jit(solution)/shard_map/ppermute | solution.py:222
  19.6 3.0 %collective-permute-done.4 = f32[16,2176]{1,0:T(8,128)S(1)} collective-permute-done((f32[16,2176]{1,0:T(8,128)S(1)}, f32[16,2176]{1,0:T(8,128)S(1)}, u32[]{:S(2)}, u32[]{:S(2)}) %collective-permute-start.4) | collective-permute-done | bytes 139296 | tf_op jit(solution)/shard_map/ppermute | solution.py:222
  22.7 3.8 %collective-permute-start.5 = (f32[16,2176]{1,0:T(8,128)S(1)}, f32[16,2176]{1,0:T(8,128)S(1)}, u32[]{:S(2)}, u32[]{:S(2)}) collective-permute-start(f32[16,2176]{1,0:T(8,128)S(1)} %add.44.za_ref), channel_id=1, source_target_pairs={{0,2},{1,3},{2,0},{3,1},{4,6},{5,7},{6,4},{7,5},{8,10},{9,11},{10,... | collective-permute-start | bytes 417800 | tf_op jit(solution)/shard_map/ppermute | solution.py:222
  26.5 4.5 %collective-permute-done.5.zb_ref = f32[16,2176]{1,0:T(8,128)S(1)} collective-permute-done((f32[16,2176]{1,0:T(8,128)S(1)}, f32[16,2176]{1,0:T(8,128)S(1)}, u32[]{:S(2)}, u32[]{:S(2)}) %collective-permute-start.5) | collective-permute-done | bytes 139296 | tf_op jit(solution)/shard_map/ppermute | solution.py:222
  33.5 2.5 %collective-permute-done.6 = f32[80,128]{1,0:T(8,128)S(1)} collective-permute-done((f32[80,128]{1,0:T(8,128)S(1)}, f32[80,128]{1,0:T(8,128)S(1)}, u32[]{:S(2)}, u32[]{:S(2)}) %collective-permute-start.6) | collective-permute-done | bytes 40992 | tf_op jit(solution)/shard_map/ppermute | solution.py:222
  37.5 2.5 %collective-permute-done.7.refs_1_ = f32[80,128]{1,0:T(8,128)S(1)} collective-permute-done((f32[80,128]{1,0:T(8,128)S(1)}, f32[80,128]{1,0:T(8,128)S(1)}, u32[]{:S(2)}, u32[]{:S(2)}) %collective-permute-start.7) | collective-permute-done | bytes 40992 | tf_op jit(solution)/shard_map/ppermute | solution.py:222
  42.4 4.7 %collective-permute-done.8 = f32[16,2176]{1,0:T(8,128)S(1)} collective-permute-done((f32[16,2176]{1,0:T(8,128)S(1)}, f32[16,2176]{1,0:T(8,128)S(1)}, u32[]{:S(2)}, u32[]{:S(2)}) %collective-permute-start.8) | collective-permute-done | bytes 139296 | tf_op jit(solution)/shard_map/ppermute | solution.py:222
  48.9 5.7 %collective-permute-done.9.zb_ref = f32[16,2176]{1,0:T(8,128)S(1)} collective-permute-done((f32[16,2176]{1,0:T(8,128)S(1)}, f32[16,2176]{1,0:T(8,128)S(1)}, u32[]{:S(2)}, u32[]{:S(2)}) %collective-permute-start.9) | collective-permute-done | bytes 139296 | tf_op jit(solution)/shard_map/ppermute | solution.py:222
  57.0 2.5 %collective-permute-done.10 = f32[80,128]{1,0:T(8,128)S(1)} collective-permute-done((f32[80,128]{1,0:T(8,128)S(1)}, f32[80,128]{1,0:T(8,128)S(1)}, u32[]{:S(2)}, u32[]{:S(2)}) %collective-permute-start.10) | collective-permute-done | bytes 40992 | tf_op jit(solution)/shard_map/ppermute | solution.py:222
  61.1 2.5 %collective-permute-done.11.refs_1_ = f32[80,128]{1,0:T(8,128)S(1)} collective-permute-done((f32[80,128]{1,0:T(8,128)S(1)}, f32[80,128]{1,0:T(8,128)S(1)}, u32[]{:S(2)}, u32[]{:S(2)}) %collective-permute-start.11) | collective-permute-done | bytes 40992 | tf_op jit(solution)/shard_map/ppermute | solution.py:222
  63.5 2.0 %lines.7 = (f32[16,2176]{1,0:T(8,128)S(1)}, f32[64,128]{1,0:T(8,128)S(1)}, f32[64,128]{1,0:T(8,128)S(1)}, f32[16,128]{1,0:T(8,128)S(1)}) custom-call(f32[80,128]{1,0:T(8,128)S(1)} %add.47.refs_0_, f32[80,128]{1,0:T(8,128)S(1)} %collective-permute-done.11.refs_1_, f32[64,128]{1,0:T(8,128)S(1)} %get-tuple-element.64.refs_2_, ...), custom_call_target="tpu_custom_call" | custom-call | tf_op jit(solution)/shard_map/lines/pallas_call | solution.py:22
  65.6 5.1 %collective-permute-done.12 = f32[16,2176]{1,0:T(8,128)S(1)} collective-permute-done((f32[16,2176]{1,0:T(8,128)S(1)}, f32[16,2176]{1,0:T(8,128)S(1)}, u32[]{:S(2)}, u32[]{:S(2)}) %collective-permute-start.12) | collective-permute-done | bytes 139296 | tf_op jit(solution)/shard_map/ppermute | solution.py:222
  71.9 6.1 %collective-permute-done.13.zb_ref = f32[16,2176]{1,0:T(8,128)S(1)} collective-permute-done((f32[16,2176]{1,0:T(8,128)S(1)}, f32[16,2176]{1,0:T(8,128)S(1)}, u32[]{:S(2)}, u32[]{:S(2)}) %collective-permute-start.13) | collective-permute-done | bytes 139296 | tf_op jit(solution)/shard_map/ppermute | solution.py:222
  80.4 2.5 %collective-permute-done.14 = f32[80,128]{1,0:T(8,128)S(1)} collective-permute-done((f32[80,128]{1,0:T(8,128)S(1)}, f32[80,128]{1,0:T(8,128)S(1)}, u32[]{:S(2)}, u32[]{:S(2)}) %collective-permute-start.14) | collective-permute-done | bytes 40992 | tf_op jit(solution)/shard_map/ppermute | solution.py:222
  84.5 2.5 %collective-permute-done.15.refs_1_ = f32[80,128]{1,0:T(8,128)S(1)} collective-permute-done((f32[80,128]{1,0:T(8,128)S(1)}, f32[80,128]{1,0:T(8,128)S(1)}, u32[]{:S(2)}, u32[]{:S(2)}) %collective-permute-start.15) | collective-permute-done | bytes 40992 | tf_op jit(solution)/shard_map/ppermute | solution.py:222
  86.9 2.0 %lines.8 = (f32[16,2176]{1,0:T(8,128)S(1)}, f32[64,128]{1,0:T(8,128)S(1)}, f32[64,128]{1,0:T(8,128)S(1)}, f32[16,128]{1,0:T(8,128)S(1)}) custom-call(f32[80,128]{1,0:T(8,128)S(1)} %add.49.refs_0_, f32[80,128]{1,0:T(8,128)S(1)} %collective-permute-done.15.refs_1_, f32[64,128]{1,0:T(8,128)S(1)} %get-tuple-element.73.refs_2_, ...), custom_call_target="tpu_custom_call" | custom-call | tf_op jit(solution)/shard_map/lines/pallas_call | solution.py:22
  89.0 5.1 %collective-permute-done.16 = f32[16,2176]{1,0:T(8,128)S(1)} collective-permute-done((f32[16,2176]{1,0:T(8,128)S(1)}, f32[16,2176]{1,0:T(8,128)S(1)}, u32[]{:S(2)}, u32[]{:S(2)}) %collective-permute-start.16) | collective-permute-done | bytes 139296 | tf_op jit(solution)/shard_map/ppermute | solution.py:222
  95.0 6.2 %collective-permute-done.17.zb_ref = f32[16,2176]{1,0:T(8,128)S(1)} collective-permute-done((f32[16,2176]{1,0:T(8,128)S(1)}, f32[16,2176]{1,0:T(8,128)S(1)}, u32[]{:S(2)}, u32[]{:S(2)}) %collective-permute-start.17) | collective-permute-done | bytes 139296 | tf_op jit(solution)/shard_map/ppermute | solution.py:222
  103.6 2.5 %collective-permute-done.18 = f32[80,128]{1,0:T(8,128)S(1)} collective-permute-done((f32[80,128]{1,0:T(8,128)S(1)}, f32[80,128]{1,0:T(8,128)S(1)}, u32[]{:S(2)}, u32[]{:S(2)}) %collective-permute-start.18) | collective-permute-done | bytes 40992 | tf_op jit(solution)/shard_map/ppermute | solution.py:222
  107.6 2.5 %collective-permute-done.19.refs_1_ = f32[80,128]{1,0:T(8,128)S(1)} collective-permute-done((f32[80,128]{1,0:T(8,128)S(1)}, f32[80,128]{1,0:T(8,128)S(1)}, u32[]{:S(2)}, u32[]{:S(2)}) %collective-permute-start.19) | collective-permute-done | bytes 40992 | tf_op jit(solution)/shard_map/ppermute | solution.py:222
  111.1 3.6 %collective-permute-done.20 = f32[16,128]{1,0:T(8,128)S(1)} collective-permute-done((f32[16,128]{1,0:T(8,128)S(1)}, f32[16,128]{1,0:T(8,128)S(1)}, u32[]{:S(2)}, u32[]{:S(2)}) %collective-permute-start.20) | collective-permute-done | bytes 8224 | tf_op jit(solution)/shard_map/ppermute | solution.py:222
  115.7 3.7 %collective-permute-done.21.cb_ref = f32[16,128]{1,0:T(8,128)S(1)} collective-permute-done((f32[16,128]{1,0:T(8,128)S(1)}, f32[16,128]{1,0:T(8,128)S(1)}, u32[]{:S(2)}, u32[]{:S(2)}) %collective-permute-start.21) | collective-permute-done | bytes 8224 | tf_op jit(solution)/shard_map/ppermute | solution.py:222
  (65 shorter events, 38.8 us)
Async XLA Ops:
  0.6 4.8 %collective-permute-start.1 = (f32[4,1024,128]{2,1,0:T(8,128)}, f32[4,1024,128]{2,1,0:T(8,128)S(1)}, u32[]{:S(2)}, u32[]{:S(2)}) collective-permute-start(f32[4,1024,128]{2,1,0:T(8,128)} %a_ref.1), channel_id=1, source_target_pairs={{0,4},{4,0},{8,12},{12,8},{16,20},{20,16},{24,28},{28,24},{1,5},{5... | collective-permute-start | bytes 6291464 | tf_op jit(solution)/shard_map/ppermute | solution.py:222
  2.8 2.6 %collective-permute-start = (f32[24,1024]{1,0:T(8,128)S(1)}, f32[24,1024]{1,0:T(8,128)S(1)}, u32[]{:S(2)}, u32[]{:S(2)}) collective-permute-start(f32[24,1024]{1,0:T(8,128)S(1)} %pad_maximum_fusion.1), channel_id=1, source_target_pairs={{0,4},{4,0},{8,12},{12,8},{16,20},{20,16},{24,28},{28,24},{1,5},{5... | collective-permute-start | bytes 294920 | tf_op jit(solution)/shard_map/ppermute | solution.py:222
  5.9 9.7 %copy-start.1 = (f32[4,128]{1,0:T(4,128)S(1)}, f32[4,128]{1,0:T(4,128)}, u32[]{:S(2)}) copy-start(f32[4,128]{1,0:T(4,128)} %w_ref.1) | copy-start | bytes 6148
  6.7 4.8 %collective-permute-start.2 = (f32[80,128]{1,0:T(8,128)S(1)}, f32[80,128]{1,0:T(8,128)S(1)}, u32[]{:S(2)}, u32[]{:S(2)}) collective-permute-start(f32[80,128]{1,0:T(8,128)S(1)} %first.1), channel_id=1, source_target_pairs={{0,8},{4,12},{8,0},{12,4},{16,24},{20,28},{24,16},{28,20},{1,9},{5... | collective-permute-start | bytes 122888 | tf_op jit(solution)/shard_map/ppermute | solution.py:222
  11.5 4.0 %collective-permute-start.3 = (f32[80,128]{1,0:T(8,128)S(1)}, f32[80,128]{1,0:T(8,128)S(1)}, u32[]{:S(2)}, u32[]{:S(2)}) collective-permute-start(f32[80,128]{1,0:T(8,128)S(1)} %add.43.refs_0_), channel_id=1, source_target_pairs={{0,16},{4,20},{8,24},{12,28},{16,0},{20,4},{24,8},{28,12},{1,17},{... | collective-permute-start | bytes 122888 | tf_op jit(solution)/shard_map/ppermute | solution.py:222
  17.5 5.1 %collective-permute-start.4 = (f32[16,2176]{1,0:T(8,128)S(1)}, f32[16,2176]{1,0:T(8,128)S(1)}, u32[]{:S(2)}, u32[]{:S(2)}) collective-permute-start(f32[16,2176]{1,0:T(8,128)S(1)} %get-tuple-element.52), channel_id=1, source_target_pairs={{0,1},{1,0},{2,3},{3,2},{4,5},{5,4},{6,7},{7,6},{8,9},{9,8},{10,11... | collective-permute-start | bytes 417800 | tf_op jit(solution)/shard_map/ppermute | solution.py:222
  22.7 8.4 %collective-permute-start.5 = (f32[16,2176]{1,0:T(8,128)S(1)}, f32[16,2176]{1,0:T(8,128)S(1)}, u32[]{:S(2)}, u32[]{:S(2)}) collective-permute-start(f32[16,2176]{1,0:T(8,128)S(1)} %add.44.za_ref), channel_id=1, source_target_pairs={{0,2},{1,3},{2,0},{3,1},{4,6},{5,7},{6,4},{7,5},{8,10},{9,11},{10,... | collective-permute-start | bytes 417800 | tf_op jit(solution)/shard_map/ppermute | solution.py:222
  31.9 4.0 %collective-permute-start.6 = (f32[80,128]{1,0:T(8,128)S(1)}, f32[80,128]{1,0:T(8,128)S(1)}, u32[]{:S(2)}, u32[]{:S(2)}) collective-permute-start(f32[80,128]{1,0:T(8,128)S(1)} %get-tuple-element.54), channel_id=1, source_target_pairs={{0,8},{4,12},{8,0},{12,4},{16,24},{20,28},{24,16},{28,20},{1,9},{5... | collective-permute-start | bytes 122888 | tf_op jit(solution)/shard_map/ppermute | solution.py:222
  36.0 4.0 %collective-permute-start.7 = (f32[80,128]{1,0:T(8,128)S(1)}, f32[80,128]{1,0:T(8,128)S(1)}, u32[]{:S(2)}, u32[]{:S(2)}) collective-permute-start(f32[80,128]{1,0:T(8,128)S(1)} %add.45.refs_0_), channel_id=1, source_target_pairs={{0,16},{4,20},{8,24},{12,28},{16,0},{20,4},{24,8},{28,12},{1,17},{... | collective-permute-start | bytes 122888 | tf_op jit(solution)/shard_map/ppermute | solution.py:222
  42.0 5.1 %collective-permute-start.8 = (f32[16,2176]{1,0:T(8,128)S(1)}, f32[16,2176]{1,0:T(8,128)S(1)}, u32[]{:S(2)}, u32[]{:S(2)}) collective-permute-start(f32[16,2176]{1,0:T(8,128)S(1)} %get-tuple-element.58), channel_id=1, source_target_pairs={{0,1},{1,0},{2,3},{3,2},{4,5},{5,4},{6,7},{7,6},{8,9},{9,8},{10,11... | collective-permute-start | bytes 417800 | tf_op jit(solution)/shard_map/ppermute | solution.py:222
  47.1 7.5 %collective-permute-start.9 = (f32[16,2176]{1,0:T(8,128)S(1)}, f32[16,2176]{1,0:T(8,128)S(1)}, u32[]{:S(2)}, u32[]{:S(2)}) collective-permute-start(f32[16,2176]{1,0:T(8,128)S(1)} %add.46.za_ref), channel_id=1, source_target_pairs={{0,2},{1,3},{2,0},{3,1},{4,6},{5,7},{6,4},{7,5},{8,10},{9,11},{10,... | collective-permute-start | bytes 417800 | tf_op jit(solution)/shard_map/ppermute | solution.py:222
  55.5 4.0 %collective-permute-start.10 = (f32[80,128]{1,0:T(8,128)S(1)}, f32[80,128]{1,0:T(8,128)S(1)}, u32[]{:S(2)}, u32[]{:S(2)}) collective-permute-start(f32[80,128]{1,0:T(8,128)S(1)} %get-tuple-element.63), channel_id=1, source_target_pairs={{0,8},{4,12},{8,0},{12,4},{16,24},{20,28},{24,16},{28,20},{1,9},{5... | collective-permute-start | bytes 122888 | tf_op jit(solution)/shard_map/ppermute | solution.py:222
  59.5 4.0 %collective-permute-start.11 = (f32[80,128]{1,0:T(8,128)S(1)}, f32[80,128]{1,0:T(8,128)S(1)}, u32[]{:S(2)}, u32[]{:S(2)}) collective-permute-start(f32[80,128]{1,0:T(8,128)S(1)} %add.47.refs_0_), channel_id=1, source_target_pairs={{0,16},{4,20},{8,24},{12,28},{16,0},{20,4},{24,8},{28,12},{1,17},{... | collective-permute-start | bytes 122888 | tf_op jit(solution)/shard_map/ppermute | solution.py:222
  65.6 5.1 %collective-permute-start.12 = (f32[16,2176]{1,0:T(8,128)S(1)}, f32[16,2176]{1,0:T(8,128)S(1)}, u32[]{:S(2)}, u32[]{:S(2)}) collective-permute-start(f32[16,2176]{1,0:T(8,128)S(1)} %get-tuple-element.67), channel_id=1, source_target_pairs={{0,1},{1,0},{2,3},{3,2},{4,5},{5,4},{6,7},{7,6},{8,9},{9,8},{10,11... | collective-permute-start | bytes 417800 | tf_op jit(solution)/shard_map/ppermute | solution.py:222
  70.7 7.3 %collective-permute-start.13 = (f32[16,2176]{1,0:T(8,128)S(1)}, f32[16,2176]{1,0:T(8,128)S(1)}, u32[]{:S(2)}, u32[]{:S(2)}) collective-permute-start(f32[16,2176]{1,0:T(8,128)S(1)} %add.48.za_ref), channel_id=1, source_target_pairs={{0,2},{1,3},{2,0},{3,1},{4,6},{5,7},{6,4},{7,5},{8,10},{9,11},{10,... | collective-permute-start | bytes 417800 | tf_op jit(solution)/shard_map/ppermute | solution.py:222
  78.9 4.0 %collective-permute-start.14 = (f32[80,128]{1,0:T(8,128)S(1)}, f32[80,128]{1,0:T(8,128)S(1)}, u32[]{:S(2)}, u32[]{:S(2)}) collective-permute-start(f32[80,128]{1,0:T(8,128)S(1)} %get-tuple-element.72), channel_id=1, source_target_pairs={{0,8},{4,12},{8,0},{12,4},{16,24},{20,28},{24,16},{28,20},{1,9},{5... | collective-permute-start | bytes 122888 | tf_op jit(solution)/shard_map/ppermute | solution.py:222
  82.9 4.0 %collective-permute-start.15 = (f32[80,128]{1,0:T(8,128)S(1)}, f32[80,128]{1,0:T(8,128)S(1)}, u32[]{:S(2)}, u32[]{:S(2)}) collective-permute-start(f32[80,128]{1,0:T(8,128)S(1)} %add.49.refs_0_), channel_id=1, source_target_pairs={{0,16},{4,20},{8,24},{12,28},{16,0},{20,4},{24,8},{28,12},{1,17},{... | collective-permute-start | bytes 122888 | tf_op jit(solution)/shard_map/ppermute | solution.py:222
  89.0 5.1 %collective-permute-start.16 = (f32[16,2176]{1,0:T(8,128)S(1)}, f32[16,2176]{1,0:T(8,128)S(1)}, u32[]{:S(2)}, u32[]{:S(2)}) collective-permute-start(f32[16,2176]{1,0:T(8,128)S(1)} %get-tuple-element.76), channel_id=1, source_target_pairs={{0,1},{1,0},{2,3},{3,2},{4,5},{5,4},{6,7},{7,6},{8,9},{9,8},{10,11... | collective-permute-start | bytes 417800 | tf_op jit(solution)/shard_map/ppermute | solution.py:222
  94.1 7.1 %collective-permute-start.17 = (f32[16,2176]{1,0:T(8,128)S(1)}, f32[16,2176]{1,0:T(8,128)S(1)}, u32[]{:S(2)}, u32[]{:S(2)}) collective-permute-start(f32[16,2176]{1,0:T(8,128)S(1)} %add.50.za_ref), channel_id=1, source_target_pairs={{0,2},{1,3},{2,0},{3,1},{4,6},{5,7},{6,4},{7,5},{8,10},{9,11},{10,... | collective-permute-start | bytes 417800 | tf_op jit(solution)/shard_map/ppermute | solution.py:222
  102.1 4.0 %collective-permute-start.18 = (f32[80,128]{1,0:T(8,128)S(1)}, f32[80,128]{1,0:T(8,128)S(1)}, u32[]{:S(2)}, u32[]{:S(2)}) collective-permute-start(f32[80,128]{1,0:T(8,128)S(1)} %get-tuple-element.81), channel_id=1, source_target_pairs={{0,8},{4,12},{8,0},{12,4},{16,24},{20,28},{24,16},{28,20},{1,9},{5... | collective-permute-start | bytes 122888 | tf_op jit(solution)/shard_map/ppermute | solution.py:222
  106.1 4.0 %collective-permute-start.19 = (f32[80,128]{1,0:T(8,128)S(1)}, f32[80,128]{1,0:T(8,128)S(1)}, u32[]{:S(2)}, u32[]{:S(2)}) collective-permute-start(f32[80,128]{1,0:T(8,128)S(1)} %add.51.refs_0_), channel_id=1, source_target_pairs={{0,16},{4,20},{8,24},{12,28},{16,0},{20,4},{24,8},{28,12},{1,17},{... | collective-permute-start | bytes 122888 | tf_op jit(solution)/shard_map/ppermute | solution.py:222
  111.1 3.7 %collective-permute-start.20 = (f32[16,128]{1,0:T(8,128)S(1)}, f32[16,128]{1,0:T(8,128)S(1)}, u32[]{:S(2)}, u32[]{:S(2)}) collective-permute-start(f32[16,128]{1,0:T(8,128)S(1)} %get-tuple-element.85), channel_id=1, source_target_pairs={{0,1},{1,0},{2,3},{3,2},{4,5},{5,4},{6,7},{7,6},{8,9},{9,8},{10,11... | collective-permute-start | bytes 24584 | tf_op jit(solution)/shard_map/ppermute | solution.py:222
  114.8 4.5 %collective-permute-start.21 = (f32[16,128]{1,0:T(8,128)S(1)}, f32[16,128]{1,0:T(8,128)S(1)}, u32[]{:S(2)}, u32[]{:S(2)}) collective-permute-start(f32[16,128]{1,0:T(8,128)S(1)} %add.52.ca_ref), channel_id=1, source_target_pairs={{0,2},{1,3},{2,0},{3,1},{4,6},{5,7},{6,4},{7,5},{8,10},{9,11},{10,... | collective-permute-start | bytes 24584 | tf_op jit(solution)/shard_map/ppermute | solution.py:222
  120.1 1.4 %collective-permute-start.22 = (f32[16,1536]{1,0:T(8,128)S(1)}, f32[16,1536]{1,0:T(8,128)S(1)}, u32[]{:S(2)}, u32[]{:S(2)}) collective-permute-start(f32[16,1536]{1,0:T(8,128)S(1)} %get-tuple-element.93), channel_id=1, source_target_pairs={{0,4},{4,0},{8,12},{12,8},{16,20},{20,16},{24,28},{28,24},{1,5},{5... | collective-permute-start | bytes 294920 | tf_op jit(solution)/shard_map/ppermute | solution.py:222
  (4 other events, 25.7 us)

commit v2 on v1

v2 whole, which is shorter than its diff:
```python
import functools

import jax
import jax.numpy as jnp
from jax import lax
from jax.experimental import pallas as pl
from jax.experimental.pallas import tpu as pltpu
from jax.sharding import PartitionSpec as P

ITERS = 5
LANE = 128
F32 = jnp.float32
BF16 = jnp.bfloat16
VM = pl.BlockSpec(memory_space=pltpu.VMEM)
PARAMS = pltpu.CompilerParams(vmem_limit_bytes=24 * 1024 * 1024)


def call(body, out_shape, name, *args):
    many = isinstance(out_shape, (list, tuple))
    return pl.pallas_call(
        body,
        out_shape=out_shape,
        in_specs=[VM] * len(args),
        out_specs=[VM] * len(out_shape) if many else VM,
        compiler_params=PARAMS,
        name=name,
    )(*args)


def struct(shape, dtype=F32):
    return jax.ShapeDtypeStruct(shape, dtype)


def split(value):
    high = value.astype(BF16)
    low = (value - high.astype(F32)).astype(BF16)
    return high, low


def stacked(value):
    high, low = split(value)
    return jnp.concatenate([high, low], axis=0)


def lane_index(shape):
    return lax.broadcasted_iota(jnp.int32, shape, 1)


def convert_body(a_ref, high_ref, low_ref):
    for k in range(a_ref.shape[0]):
        high, low = split(a_ref[k])
        high_ref[:, k * LANE:(k + 1) * LANE] = high
        low_ref[:, k * LANE:(k + 1) * LANE] = low


def convert(a):
    k, n, m = a.shape
    shape = struct((n, k * m), BF16)
    return call(convert_body, [shape, shape], "convert", a)


def dot(lhs, rhs, rhs_dim):
    return lax.dot_general(lhs, rhs, (((1,), (rhs_dim,)), ((), ())), preferred_element_type=F32)


def to_lines(vector, mats):
    rows, n = vector.shape[0], vector.shape[1] // 2
    total = None
    for half in range(2):
        pair = stacked(vector[:, half * n:(half + 1) * n])
        for part in range(2):
            out = dot(pair, mats[2 * half + part][...], 0)
            total = out if total is None else total + out
    return total[:rows] + total[rows:]


def from_lines(lines, mats):
    rows = lines.shape[0]
    pair = stacked(lines)
    halves = []
    for half in range(2):
        out = dot(pair, mats[2 * half][...], 0) + dot(pair, mats[2 * half + 1][...], 0)
        halves.append(out[:rows] + out[rows:])
    return halves


def operator(w, f, out):
    row = lax.broadcasted_iota(jnp.int32, (LANE, LANE), 0)
    col = lax.broadcasted_iota(jnp.int32, (LANE, LANE), 1)
    lane = lane_index((1, LANE))
    kept = jnp.where(lane == out, 0.0, f)
    gain = w * kept
    corner = jnp.sum(gain * kept, axis=1, keepdims=True)
    edge = jnp.where(row == out, gain, 0.0)
    inner = jnp.where(row == col, jnp.where(col == out, corner, w), 0.0)
    return inner + edge + edge.T


def fold_body(high_ref, low_ref, w_ref, f_ref, out_ref, bh_ref, bl_ref):
    for k in range(w_ref.shape[0]):
        span = slice(k * LANE, (k + 1) * LANE)
        op = operator(w_ref[k:k + 1, :], f_ref[k:k + 1, :], out_ref[k:k + 1, :])
        pair = stacked(op)
        main = dot(pair, high_ref[:, span], 1)
        rest = dot(pair[:LANE], low_ref[:, span], 1)
        high, low = split(main[:LANE] + (main[LANE:] + rest))
        bh_ref[span, :] = high
        bl_ref[span, :] = low


def fold(pair, w, f, out):
    n, m = pair[0].shape
    shape = struct((m, n), BF16)
    return call(fold_body, [shape, shape], "fold", *pair, w, f, out)


def store_flows(vector, hess, previous, mats, payload_ref):
    rows = vector.shape[0]
    lines = to_lines(vector, mats)
    conts = lines.shape[1] // LANE
    for k in range(conts):
        payload_ref[k * rows:(k + 1) * rows, :] = lines[:, k * LANE:(k + 1) * LANE]
    scaled = hess * vector
    first = jnp.sum(vector * vector, axis=1, keepdims=True)
    second = jnp.sum(scaled * vector, axis=1, keepdims=True)
    lane = lane_index((rows, LANE))
    packed = jnp.where(lane == 0, first, 0.0) + jnp.where(lane == 1, second, 0.0)
    if previous is not None:
        third = jnp.sum(scaled * previous, axis=1, keepdims=True)
        packed = packed + jnp.where(lane == 2, third, 0.0)
    payload_ref[conts * rows:(conts + 1) * rows, :] = packed


def first_body(r_ref, hess_ref, a0, a1, a2, a3, payload_ref):
    store_flows(r_ref[...], hess_ref[...], None, (a0, a1, a2, a3), payload_ref)


def merged(za_ref, zb_ref, rows, chunks):
    def block(ref, at):
        return ref[at * rows:(at + 1) * rows, :]

    own = [block(za_ref, c) + block(zb_ref, chunks + c) for c in range(chunks)]
    other = [block(za_ref, chunks + c) + block(zb_ref, c) for c in range(chunks)]
    curved = block(za_ref, 2 * chunks) + block(zb_ref, 2 * chunks)
    return jnp.concatenate(own + other, axis=1), curved


def step_body(za_ref, zb_ref, r_ref, p_ref, x_ref, sc_ref, hess_ref, a0, a1, a2, a3,
              payload_ref, rn_ref, pn_ref, xn_ref, alpha_ref, *, first):
    rows, n = r_ref.shape
    r = r_ref[...]
    hess = hess_ref[...]
    image, curved = merged(za_ref, zb_ref, rows, n // 2 // LANE)
    alpha = sc_ref[:, 0:1] / (curved[:, 0:1] + sc_ref[:, 1:2])
    if first:
        p = r
        xn_ref[...] = alpha * p
    else:
        p = r + sc_ref[:, 2:3] * p_ref[...]
        xn_ref[...] = x_ref[...] + alpha * p
    pn_ref[...] = p
    r = r - alpha * (image + hess * p)
    rn_ref[...] = r
    alpha_ref[...] = jnp.broadcast_to(alpha, alpha_ref.shape)
    store_flows(r, hess, p, (a0, a1, a2, a3), payload_ref)


def weigh(flows, k, w_ref, f_ref, out_ref):
    chosen = lane_index((1, LANE)) == out_ref[k:k + 1, :]
    factors = jnp.where(chosen, -1.0, f_ref[k:k + 1, :])
    hit = jnp.sum(jnp.where(chosen, flows, 0.0), axis=1, keepdims=True)
    post = flows + factors * hit
    return post, w_ref[k:k + 1, :] * post


def lines_body(*refs, count, first, last):
    parts, refs = refs[:count], refs[count:]
    fp_ref, fx_ref, sc_ref, alpha_ref, w_ref, f_ref, out_ref = refs[:7]
    mats = () if last else refs[7:11]
    z_ref, fpn_ref, fxn_ref, scn_ref = refs[7 if last else 11:]
    conts = w_ref.shape[0]
    rows = parts[0].shape[0] // (conts + 1)

    def total(at):
        values = [ref[at:at + rows, :] for ref in parts]
        while len(values) > 1:
            values = [values[i] + values[i + 1] for i in range(0, len(values), 2)]
        return values[0]

    sums = total(conts * rows)
    rr, base = sums[:, 0:1], sums[:, 1:2]
    if not first:
        beta = rr / sc_ref[:, 0:1]
        base = base + beta * (2.0 * sums[:, 2:3] + beta * sc_ref[:, 1:2])
        alpha = alpha_ref[:, 0:1]
    lane = lane_index((rows, LANE))
    packed = jnp.where(lane == 0, rr, 0.0) + jnp.where(lane == 1, base, 0.0)
    if not first:
        packed = packed + jnp.where(lane == 2, beta, 0.0)
    scn_ref[...] = packed
    curv = jnp.zeros((rows, LANE), F32)
    flat = []
    for k in range(conts):
        span = slice(k * rows, (k + 1) * rows)
        flows = total(k * rows)
        if not first:
            before = fp_ref[span, :]
            fxn_ref[span, :] = fx_ref[span, :] + alpha * before
            flows = flows + beta * before
        else:
            fxn_ref[span, :] = jnp.zeros((rows, LANE), F32)
        fpn_ref[span, :] = flows
        post, weighted = weigh(flows, k, w_ref, f_ref, out_ref)
        curv = curv + post * weighted
        flat.append(flows)
    curv = jnp.broadcast_to(jnp.sum(curv, axis=1, keepdims=True), (rows, LANE))
    if last:
        z_ref[...] = curv
    else:
        halves = from_lines(jnp.concatenate(flat, axis=1), mats)
        chunks = halves[0].shape[1] // LANE
        for half in range(2):
            for c in range(chunks):
                at = (half * chunks + c) * rows
                z_ref[at:at + rows, :] = halves[half][:, c * LANE:(c + 1) * LANE]
        z_ref[2 * chunks * rows:, :] = curv


def finish_body(ca_ref, cb_ref, r_ref, p_ref, x_ref, sc_ref, fp_ref, fx_ref, w_ref, f_ref, out_ref,
                own_ref, send_ref):
    n = r_ref.shape[1] // 2
    rows = r_ref.shape[0]
    alpha = sc_ref[:, 0:1] / (ca_ref[:, 0:1] + cb_ref[:, 0:1] + sc_ref[:, 1:2])
    p = r_ref[...] + sc_ref[:, 2:3] * p_ref[...]
    x = x_ref[...] + alpha * p
    own_ref[:, :n] = x[:, :n]
    send_ref[:, :n] = x[:, n:]
    for k in range(w_ref.shape[0]):
        span = slice(k * rows, (k + 1) * rows)
        flows = fx_ref[span, :] + alpha * fp_ref[span, :]
        weighted = weigh(flows, k, w_ref, f_ref, out_ref)[1]
        own_ref[:, n + k * LANE:n + (k + 1) * LANE] = weighted
        send_ref[:, n + k * LANE:n + (k + 1) * LANE] = weighted


def place_body(own_ref, other_ref, part_ref, x_ref, w_ref):
    rows = own_ref.shape[0]
    n = x_ref.shape[1]
    upper = part_ref[0:1, 0:1] > 0
    for low in range(2):
        one, two = (other_ref, own_ref) if low == 0 else (own_ref, other_ref)
        value = jnp.where(upper, one[...], two[...])
        at = slice(low * rows, (low + 1) * rows)
        x_ref[at, :] = value[:, :n]
        for k in range(w_ref.shape[0]):
            w_ref[k, at, :] = value[:, n + k * LANE:n + (k + 1) * LANE]


def per_device(right_sides, base_hessian, sensitivity, weights, outage_factors, outaged, *, scen, base):
    conts, n, lines = sensitivity.shape
    rhs = right_sides.shape[0]
    rows = rhs // 2
    half = n // LANE * rows
    spread = jnp.broadcast_to(outaged.astype(jnp.int32)[:, None], (conts, lines))

    def half_of(s, b):
        return (s.bit_count() + b.bit_count()) & 1

    def swap(value, *steps):
        pairs = []
        for s in range(scen):
            for b in range(base):
                along, across = steps[half_of(s, b) % len(steps)]
                pairs.append((s * base + b, (s ^ along) * base + (b ^ across)))
        return lax.ppermute(value, ("scen", "base"), pairs)

    def over_scen(value):
        bit = 2
        while 4 * bit < scen:
            value = value + swap(value, (bit | 1, 0))
            bit *= 2
        if 2 * bit < scen:
            one, two = (bit | 1, 0), (2 * bit | 1, 0)
            return [value, swap(value, one, two), swap(value, two, one), swap(value, (3 * bit, 0))]
        return [value, swap(value, (bit | 1, 0))]

    def over_base(value):
        bits = [1 << i for i in range((base - 1).bit_length())]
        for i, bit in enumerate(bits):
            got = swap(value, (1, bit), (1, bits[(i + 1) % len(bits)]))
            if i + 1 == len(bits):
                return value, got
            if got.shape[0] > 2 * half:
                got = jnp.concatenate([got[half:2 * half], got[:half], got[2 * half:]], axis=0)
            value = value + got

    place = lax.axis_index("scen") * base + lax.axis_index("base")
    bits = (scen * base - 1).bit_length()
    part = sum((place >> i) & 1 for i in range(bits)) & 1
    other_a = swap(sensitivity, (1, 0))
    mine = lax.dynamic_slice_in_dim(right_sides, part * rows, rows, 0)
    theirs = lax.dynamic_slice_in_dim(right_sides, (1 - part) * rows, rows, 0)
    extra = jnp.concatenate([theirs, jnp.broadcast_to(base_hessian[None, :], (8, n))], axis=0)
    other = swap(extra, (1, 0))
    r = jnp.concatenate([mine, other[:rows]], axis=1)
    hess = jnp.concatenate([base_hessian[None, :], other[rows:rows + 1]], axis=1)
    pairs = convert(sensitivity), convert(other_a)
    mats = [*pairs[0], *pairs[1]]

    flat = struct((conts * rows, LANE))
    state = struct((rows, 2 * n))
    scal = struct((rows, LANE))
    payload = struct(((conts + 1) * rows, LANE))
    wide = struct((2 * half + rows, LANE))

    pay = call(first_body, payload, "first", r, hess, *mats)
    table = (weights, outage_factors, spread)
    folded = [*fold(pairs[0], *table), *fold(pairs[1], *table)]
    p = x = r
    fp = fx = jnp.zeros(flat.shape, F32)
    sc = alpha = jnp.zeros(scal.shape, F32)
    for it in range(ITERS):
        first, last = it == 0, it + 1 == ITERS
        sent = over_scen(pay)
        tail = () if last else tuple(folded)
        z, fp, fx, sc = call(
            functools.partial(lines_body, count=len(sent), first=first, last=last),
            [scal if last else wide, flat, flat, scal], "lines",
            *sent, fp, fx, sc, alpha, *table, *tail)
        za, zb = over_base(z)
        if not last:
            pay, r, p, x, alpha = call(
                functools.partial(step_body, first=first),
                [payload, state, state, state, scal], "step",
                za, zb, r, p, x, sc, hess, *mats)
    both = struct((rows, n + conts * LANE))
    own, send = call(finish_body, [both, both], "finish", za, zb, r, p, x, sc, fp, fx, *table)
    recv = swap(send, (1, 0))
    which = jnp.broadcast_to(part.astype(jnp.int32), (8, LANE))
    step, flow = call(place_body, [struct((rhs, n)), struct((conts, rhs, lines))], "place", own, recv, which)
    return step, flow


def solution(mesh):
    placed = (
        P(None, "scen"),
        P("scen"),
        P("base", "scen", None),
        P("base", None),
        P("base", None),
        P("base"),
    )
    body = functools.partial(per_device, scen=mesh.shape["scen"], base=mesh.shape["base"])
    return jax.shard_map(
        body,
        mesh=mesh,
        in_specs=placed,
        out_specs=(P(None, "scen"), P("base", None, None)),
        check_vma=False,
    )
```

time: 122 us -> 109 us (0.89)
  waiting for transfers between devices: 73.3 us -> 66.6 us
  Pallas kernels: 15.7 us -> 12 us
  starting transfers between devices: 29 us -> 25.7 us
    ppermute x23 -> x28, waiting for transfers between devices: 73.3 us -> 66.6 us  [swap(): return lax.ppermute(value, ('scen', 'base'), pairs)]
    pallas_call x14 -> x16, Pallas kernels: 15.7 us -> 12 us  [call(): pl.pallas_call(body, out_shape=out_shape, in_specs=[VM] * len(args), out_...]
    ppermute x23 -> x28, starting transfers between devices: 29 us -> 25.7 us  [swap(): return lax.ppermute(value, ('scen', 'base'), pairs)]
  transfers between devices with their start and end apart: 23 -> 28, of which waited for: 22 -> 25; matrix products, arithmetic and copies ran while one was open for 1% -> 2% of each run, Pallas kernels for 0% -> 2%
where the time goes in v2:
time: 109 us
  waiting for transfers between devices  66.6 us (61%)
  starting transfers between devices  25.7 us (24%)
  Pallas kernels  12 us (11%)
  local copies, waits for them, and re-layouts  3.32 us (3%)
    ppermute x28, waiting for transfers between devices, swap(): return lax.ppermute(value, ('scen', 'base'), pairs)  66.6 us
    ppermute x28, starting transfers between devices, swap(): return lax.ppermute(value, ('scen', 'base'), pairs)  25.7 us
    pallas_call x16, Pallas kernels, call(): pl.pallas_call(body, out_shape=out_shape, in_specs=[VM] * len(args), out_...  12 us
  transfers between devices with their start and end apart: 28, of which 25 were waited for; matrix products, arithmetic and copies ran while one was open for 2% of the time, Pallas kernels for 2%

profile of v2, /device:TPU:0, one launch (start us, length us, event | category | flops | bytes accessed | tf_op | source)
XLA Modules:
  0.0 108.6 jit_solution(13804100021000886201)
XLA Ops:
  2.9 1.6 %copy-done = f32[4,1024,128]{2,1,0:T(8,128)S(1)} copy-done((f32[4,1024,128]{2,1,0:T(8,128)S(1)}, f32[4,1024,128]{2,1,0:T(8,128)}, u32[]{:S(2)}) %copy-start) | copy-done | bytes 2097176
  6.7 2.6 %collective-permute-start.2 = (f32[80,128]{1,0:T(8,128)S(1)}, f32[80,128]{1,0:T(8,128)S(1)}, u32[]{:S(2)}, u32[]{:S(2)}) collective-permute-start(f32[80,128]{1,0:T(8,128)S(1)} %first.1.refs_0_), channel_id=1, source_target_pairs={{0,12},{1,21},{2,22},{3,15},{4,16},{5,9},{6,10},{7,19},{8,28},{9,5... | collective-permute-start | bytes 122888 | tf_op jit(solution)/shard_map/ppermute | solution.py:275
  13.0 2.7 %collective-permute-done.4.refs_3_ = f32[80,128]{1,0:T(8,128)S(1)} collective-permute-done((f32[80,128]{1,0:T(8,128)S(1)}, f32[80,128]{1,0:T(8,128)S(1)}, u32[]{:S(2)}, u32[]{:S(2)}) %collective-permute-start.4) | collective-permute-done | bytes 40992 | tf_op jit(solution)/shard_map/ppermute | solution.py:275
  16.6 5.2 %collective-permute-done.5 = f32[272,128]{1,0:T(8,128)S(1)} collective-permute-done((f32[272,128]{1,0:T(8,128)S(1)}, f32[272,128]{1,0:T(8,128)S(1)}, u32[]{:S(2)}, u32[]{:S(2)}) %collective-permute-start.5) | collective-permute-done | bytes 139296 | tf_op jit(solution)/shard_map/ppermute | solution.py:275
  21.9 2.6 %collective-permute-start.6 = (f32[272,128]{1,0:T(8,128)S(1)}, f32[272,128]{1,0:T(8,128)S(1)}, u32[]{:S(2)}, u32[]{:S(2)}) collective-permute-start(f32[272,128]{1,0:T(8,128)S(1)} %maximum_add_fusion.za_ref), channel_id=1, source_target_pairs={{0,6},{1,4},{2,7},{3,5},{4,1},{5,3},{6,0},{7,2},{8,13},{9,15},{10,... | collective-permute-start | bytes 417800 | tf_op jit(solution)/shard_map/ppermute | solution.py:275
  24.4 3.8 %collective-permute-done.6.zb_ref = f32[272,128]{1,0:T(8,128)S(1)} collective-permute-done((f32[272,128]{1,0:T(8,128)S(1)}, f32[272,128]{1,0:T(8,128)S(1)}, u32[]{:S(2)}, u32[]{:S(2)}) %collective-permute-start.6) | collective-permute-done | bytes 139296 | tf_op jit(solution)/shard_map/ppermute | solution.py:275
  30.6 1.8 %collective-permute-start.9 = (f32[80,128]{1,0:T(8,128)S(1)}, f32[80,128]{1,0:T(8,128)S(1)}, u32[]{:S(2)}, u32[]{:S(2)}) collective-permute-start(f32[80,128]{1,0:T(8,128)S(1)} %get-tuple-element.62.refs_0_), channel_id=1, source_target_pairs={{0,24},{1,25},{2,26},{3,27},{4,28},{5,29},{6,30},{7,31},{8,16},{9,... | collective-permute-start | bytes 122888 | tf_op jit(solution)/shard_map/ppermute | solution.py:275
  33.9 1.6 %collective-permute-done.9.refs_3_ = f32[80,128]{1,0:T(8,128)S(1)} collective-permute-done((f32[80,128]{1,0:T(8,128)S(1)}, f32[80,128]{1,0:T(8,128)S(1)}, u32[]{:S(2)}, u32[]{:S(2)}) %collective-permute-start.9) | collective-permute-done | bytes 40992 | tf_op jit(solution)/shard_map/ppermute | solution.py:275
  36.3 6.0 %collective-permute-done.10 = f32[272,128]{1,0:T(8,128)S(1)} collective-permute-done((f32[272,128]{1,0:T(8,128)S(1)}, f32[272,128]{1,0:T(8,128)S(1)}, u32[]{:S(2)}, u32[]{:S(2)}) %collective-permute-start.10) | collective-permute-done | bytes 139296 | tf_op jit(solution)/shard_map/ppermute | solution.py:275
  42.3 1.7 %collective-permute-start.11 = (f32[272,128]{1,0:T(8,128)S(1)}, f32[272,128]{1,0:T(8,128)S(1)}, u32[]{:S(2)}, u32[]{:S(2)}) collective-permute-start(f32[272,128]{1,0:T(8,128)S(1)} %maximum_add_fusion.1.za_ref), channel_id=1, source_target_pairs={{0,6},{1,4},{2,7},{3,5},{4,1},{5,3},{6,0},{7,2},{8,13},{9,15},{10,... | collective-permute-start | bytes 417800 | tf_op jit(solution)/shard_map/ppermute | solution.py:275
  44.0 4.6 %collective-permute-done.11.zb_ref = f32[272,128]{1,0:T(8,128)S(1)} collective-permute-done((f32[272,128]{1,0:T(8,128)S(1)}, f32[272,128]{1,0:T(8,128)S(1)}, u32[]{:S(2)}, u32[]{:S(2)}) %collective-permute-start.11) | collective-permute-done | bytes 139296 | tf_op jit(solution)/shard_map/ppermute | solution.py:275
  49.6 1.7 %collective-permute-start.12 = (f32[80,128]{1,0:T(8,128)S(1)}, f32[80,128]{1,0:T(8,128)S(1)}, u32[]{:S(2)}, u32[]{:S(2)}) collective-permute-start(f32[80,128]{1,0:T(8,128)S(1)} %get-tuple-element.71.refs_0_), channel_id=1, source_target_pairs={{0,12},{1,21},{2,22},{3,15},{4,16},{5,9},{6,10},{7,19},{8,28},{9,5... | collective-permute-start | bytes 122888 | tf_op jit(solution)/shard_map/ppermute | solution.py:275
  53.0 1.7 %collective-permute-done.13.refs_2_ = f32[80,128]{1,0:T(8,128)S(1)} collective-permute-done((f32[80,128]{1,0:T(8,128)S(1)}, f32[80,128]{1,0:T(8,128)S(1)}, u32[]{:S(2)}, u32[]{:S(2)}) %collective-permute-start.13) | collective-permute-done | bytes 40992 | tf_op jit(solution)/shard_map/ppermute | solution.py:275
  54.7 1.9 %collective-permute-done.14.refs_3_ = f32[80,128]{1,0:T(8,128)S(1)} collective-permute-done((f32[80,128]{1,0:T(8,128)S(1)}, f32[80,128]{1,0:T(8,128)S(1)}, u32[]{:S(2)}, u32[]{:S(2)}) %collective-permute-start.14) | collective-permute-done | bytes 40992 | tf_op jit(solution)/shard_map/ppermute | solution.py:275
  57.6 5.8 %collective-permute-done.15 = f32[272,128]{1,0:T(8,128)S(1)} collective-permute-done((f32[272,128]{1,0:T(8,128)S(1)}, f32[272,128]{1,0:T(8,128)S(1)}, u32[]{:S(2)}, u32[]{:S(2)}) %collective-permute-start.15) | collective-permute-done | bytes 139296 | tf_op jit(solution)/shard_map/ppermute | solution.py:275
  65.0 5.0 %collective-permute-done.16.zb_ref = f32[272,128]{1,0:T(8,128)S(1)} collective-permute-done((f32[272,128]{1,0:T(8,128)S(1)}, f32[272,128]{1,0:T(8,128)S(1)}, u32[]{:S(2)}, u32[]{:S(2)}) %collective-permute-start.16) | collective-permute-done | bytes 139296 | tf_op jit(solution)/shard_map/ppermute | solution.py:275
  72.1 2.0 %collective-permute-start.19 = (f32[80,128]{1,0:T(8,128)S(1)}, f32[80,128]{1,0:T(8,128)S(1)}, u32[]{:S(2)}, u32[]{:S(2)}) collective-permute-start(f32[80,128]{1,0:T(8,128)S(1)} %get-tuple-element.80.refs_0_), channel_id=1, source_target_pairs={{0,24},{1,25},{2,26},{3,27},{4,28},{5,29},{6,30},{7,31},{8,16},{9,... | collective-permute-start | bytes 122888 | tf_op jit(solution)/shard_map/ppermute | solution.py:275
  74.4 2.6 %collective-permute-done.19.refs_3_ = f32[80,128]{1,0:T(8,128)S(1)} collective-permute-done((f32[80,128]{1,0:T(8,128)S(1)}, f32[80,128]{1,0:T(8,128)S(1)}, u32[]{:S(2)}, u32[]{:S(2)}) %collective-permute-start.19) | collective-permute-done | bytes 40992 | tf_op jit(solution)/shard_map/ppermute | solution.py:275
  77.8 6.0 %collective-permute-done.20 = f32[272,128]{1,0:T(8,128)S(1)} collective-permute-done((f32[272,128]{1,0:T(8,128)S(1)}, f32[272,128]{1,0:T(8,128)S(1)}, u32[]{:S(2)}, u32[]{:S(2)}) %collective-permute-start.20) | collective-permute-done | bytes 139296 | tf_op jit(solution)/shard_map/ppermute | solution.py:275
  84.5 6.2 %collective-permute-done.21.zb_ref = f32[272,128]{1,0:T(8,128)S(1)} collective-permute-done((f32[272,128]{1,0:T(8,128)S(1)}, f32[272,128]{1,0:T(8,128)S(1)}, u32[]{:S(2)}, u32[]{:S(2)}) %collective-permute-start.21) | collective-permute-done | bytes 139296 | tf_op jit(solution)/shard_map/ppermute | solution.py:275
  91.6 2.3 %collective-permute-start.23 = (f32[80,128]{1,0:T(8,128)S(1)}, f32[80,128]{1,0:T(8,128)S(1)}, u32[]{:S(2)}, u32[]{:S(2)}) collective-permute-start(f32[80,128]{1,0:T(8,128)S(1)} %get-tuple-element.89.refs_0_), channel_id=1, source_target_pairs={{0,20},{1,13},{2,14},{3,23},{4,8},{5,17},{6,18},{7,11},{8,4},{9,29... | collective-permute-start | bytes 122888 | tf_op jit(solution)/shard_map/ppermute | solution.py:275
  95.6 3.2 %collective-permute-done.24.refs_3_ = f32[80,128]{1,0:T(8,128)S(1)} collective-permute-done((f32[80,128]{1,0:T(8,128)S(1)}, f32[80,128]{1,0:T(8,128)S(1)}, u32[]{:S(2)}, u32[]{:S(2)}) %collective-permute-start.24) | collective-permute-done | bytes 40992 | tf_op jit(solution)/shard_map/ppermute | solution.py:275
  99.2 3.1 %collective-permute-done.25 = f32[16,128]{1,0:T(8,128)S(1)} collective-permute-done((f32[16,128]{1,0:T(8,128)S(1)}, f32[16,128]{1,0:T(8,128)S(1)}, u32[]{:S(2)}, u32[]{:S(2)}) %collective-permute-start.25) | collective-permute-done | bytes 8224 | tf_op jit(solution)/shard_map/ppermute | solution.py:275
  103.3 3.0 %collective-permute-done.26.cb_ref = f32[16,128]{1,0:T(8,128)S(1)} collective-permute-done((f32[16,128]{1,0:T(8,128)S(1)}, f32[16,128]{1,0:T(8,128)S(1)}, u32[]{:S(2)}, u32[]{:S(2)}) %collective-permute-start.26) | collective-permute-done | bytes 8224 | tf_op jit(solution)/shard_map/ppermute | solution.py:275
  (82 shorter events, 29.3 us)
Async XLA Ops:
  0.6 4.8 %collective-permute-start.1 = (f32[4,1024,128]{2,1,0:T(8,128)}, f32[4,1024,128]{2,1,0:T(8,128)S(1)}, u32[]{:S(2)}, u32[]{:S(2)}) collective-permute-start(f32[4,1024,128]{2,1,0:T(8,128)} %a_ref.1), channel_id=1, source_target_pairs={{0,4},{1,5},{2,6},{3,7},{4,0},{5,1},{6,2},{7,3},{8,12},{9,13},{10,... | collective-permute-start | bytes 6291464 | tf_op jit(solution)/shard_map/ppermute | solution.py:275
  6.7 6.3 %collective-permute-start.2 = (f32[80,128]{1,0:T(8,128)S(1)}, f32[80,128]{1,0:T(8,128)S(1)}, u32[]{:S(2)}, u32[]{:S(2)}) collective-permute-start(f32[80,128]{1,0:T(8,128)S(1)} %first.1.refs_0_), channel_id=1, source_target_pairs={{0,12},{1,21},{2,22},{3,15},{4,16},{5,9},{6,10},{7,19},{8,28},{9,5... | collective-permute-start | bytes 122888 | tf_op jit(solution)/shard_map/ppermute | solution.py:275
  9.3 3.7 %collective-permute-start.3 = (f32[80,128]{1,0:T(8,128)S(1)}, f32[80,128]{1,0:T(8,128)S(1)}, u32[]{:S(2)}, u32[]{:S(2)}) collective-permute-start(f32[80,128]{1,0:T(8,128)S(1)} %first.1.refs_0_), channel_id=1, source_target_pairs={{0,20},{1,13},{2,14},{3,23},{4,8},{5,17},{6,18},{7,11},{8,4},{9,29... | collective-permute-start | bytes 122888 | tf_op jit(solution)/shard_map/ppermute | solution.py:275
  10.8 4.9 %collective-permute-start.4 = (f32[80,128]{1,0:T(8,128)S(1)}, f32[80,128]{1,0:T(8,128)S(1)}, u32[]{:S(2)}, u32[]{:S(2)}) collective-permute-start(f32[80,128]{1,0:T(8,128)S(1)} %first.1.refs_0_), channel_id=1, source_target_pairs={{0,24},{1,25},{2,26},{3,27},{4,28},{5,29},{6,30},{7,31},{8,16},{9,... | collective-permute-start | bytes 122888 | tf_op jit(solution)/shard_map/ppermute | solution.py:275
  16.4 5.4 %collective-permute-start.5 = (f32[272,128]{1,0:T(8,128)S(1)}, f32[272,128]{1,0:T(8,128)S(1)}, u32[]{:S(2)}, u32[]{:S(2)}) collective-permute-start(f32[272,128]{1,0:T(8,128)S(1)} %get-tuple-element.60), channel_id=1, source_target_pairs={{0,5},{1,7},{2,4},{3,6},{4,2},{5,0},{6,3},{7,1},{8,14},{9,12},{10,... | collective-permute-start | bytes 417800 | tf_op jit(solution)/shard_map/ppermute | solution.py:275
  21.9 6.4 %collective-permute-start.6 = (f32[272,128]{1,0:T(8,128)S(1)}, f32[272,128]{1,0:T(8,128)S(1)}, u32[]{:S(2)}, u32[]{:S(2)}) collective-permute-start(f32[272,128]{1,0:T(8,128)S(1)} %maximum_add_fusion.za_ref), channel_id=1, source_target_pairs={{0,6},{1,4},{2,7},{3,5},{4,1},{5,3},{6,0},{7,2},{8,13},{9,15},{10,... | collective-permute-start | bytes 417800 | tf_op jit(solution)/shard_map/ppermute | solution.py:275
  29.2 3.4 %collective-permute-start.7 = (f32[80,128]{1,0:T(8,128)S(1)}, f32[80,128]{1,0:T(8,128)S(1)}, u32[]{:S(2)}, u32[]{:S(2)}) collective-permute-start(f32[80,128]{1,0:T(8,128)S(1)} %get-tuple-element.62.refs_0_), channel_id=1, source_target_pairs={{0,12},{1,21},{2,22},{3,15},{4,16},{5,9},{6,10},{7,19},{8,28},{9,5... | collective-permute-start | bytes 122888 | tf_op jit(solution)/shard_map/ppermute | solution.py:275
  30.6 4.9 %collective-permute-start.9 = (f32[80,128]{1,0:T(8,128)S(1)}, f32[80,128]{1,0:T(8,128)S(1)}, u32[]{:S(2)}, u32[]{:S(2)}) collective-permute-start(f32[80,128]{1,0:T(8,128)S(1)} %get-tuple-element.62.refs_0_), channel_id=1, source_target_pairs={{0,24},{1,25},{2,26},{3,27},{4,28},{5,29},{6,30},{7,31},{8,16},{9,... | collective-permute-start | bytes 122888 | tf_op jit(solution)/shard_map/ppermute | solution.py:275
  36.3 6.0 %collective-permute-start.10 = (f32[272,128]{1,0:T(8,128)S(1)}, f32[272,128]{1,0:T(8,128)S(1)}, u32[]{:S(2)}, u32[]{:S(2)}) collective-permute-start(f32[272,128]{1,0:T(8,128)S(1)} %get-tuple-element.66), channel_id=1, source_target_pairs={{0,5},{1,7},{2,4},{3,6},{4,2},{5,0},{6,3},{7,1},{8,14},{9,12},{10,... | collective-permute-start | bytes 417800 | tf_op jit(solution)/shard_map/ppermute | solution.py:275
  42.3 6.3 %collective-permute-start.11 = (f32[272,128]{1,0:T(8,128)S(1)}, f32[272,128]{1,0:T(8,128)S(1)}, u32[]{:S(2)}, u32[]{:S(2)}) collective-permute-start(f32[272,128]{1,0:T(8,128)S(1)} %maximum_add_fusion.1.za_ref), channel_id=1, source_target_pairs={{0,6},{1,4},{2,7},{3,5},{4,1},{5,3},{6,0},{7,2},{8,13},{9,15},{10,... | collective-permute-start | bytes 417800 | tf_op jit(solution)/shard_map/ppermute | solution.py:275
  49.6 3.4 %collective-permute-start.12 = (f32[80,128]{1,0:T(8,128)S(1)}, f32[80,128]{1,0:T(8,128)S(1)}, u32[]{:S(2)}, u32[]{:S(2)}) collective-permute-start(f32[80,128]{1,0:T(8,128)S(1)} %get-tuple-element.71.refs_0_), channel_id=1, source_target_pairs={{0,12},{1,21},{2,22},{3,15},{4,16},{5,9},{6,10},{7,19},{8,28},{9,5... | collective-permute-start | bytes 122888 | tf_op jit(solution)/shard_map/ppermute | solution.py:275
  51.2 3.4 %collective-permute-start.13 = (f32[80,128]{1,0:T(8,128)S(1)}, f32[80,128]{1,0:T(8,128)S(1)}, u32[]{:S(2)}, u32[]{:S(2)}) collective-permute-start(f32[80,128]{1,0:T(8,128)S(1)} %get-tuple-element.71.refs_0_), channel_id=1, source_target_pairs={{0,20},{1,13},{2,14},{3,23},{4,8},{5,17},{6,18},{7,11},{8,4},{9,29... | collective-permute-start | bytes 122888 | tf_op jit(solution)/shard_map/ppermute | solution.py:275
  51.6 4.9 %collective-permute-start.14 = (f32[80,128]{1,0:T(8,128)S(1)}, f32[80,128]{1,0:T(8,128)S(1)}, u32[]{:S(2)}, u32[]{:S(2)}) collective-permute-start(f32[80,128]{1,0:T(8,128)S(1)} %get-tuple-element.71.refs_0_), channel_id=1, source_target_pairs={{0,24},{1,25},{2,26},{3,27},{4,28},{5,29},{6,30},{7,31},{8,16},{9,... | collective-permute-start | bytes 122888 | tf_op jit(solution)/shard_map/ppermute | solution.py:275
  57.4 6.0 %collective-permute-start.15 = (f32[272,128]{1,0:T(8,128)S(1)}, f32[272,128]{1,0:T(8,128)S(1)}, u32[]{:S(2)}, u32[]{:S(2)}) collective-permute-start(f32[272,128]{1,0:T(8,128)S(1)} %get-tuple-element.75), channel_id=1, source_target_pairs={{0,5},{1,7},{2,4},{3,6},{4,2},{5,0},{6,3},{7,1},{8,14},{9,12},{10,... | collective-permute-start | bytes 417800 | tf_op jit(solution)/shard_map/ppermute | solution.py:275
  63.4 6.5 %collective-permute-start.16 = (f32[272,128]{1,0:T(8,128)S(1)}, f32[272,128]{1,0:T(8,128)S(1)}, u32[]{:S(2)}, u32[]{:S(2)}) collective-permute-start(f32[272,128]{1,0:T(8,128)S(1)} %maximum_add_fusion.2.za_ref), channel_id=1, source_target_pairs={{0,6},{1,4},{2,7},{3,5},{4,1},{5,3},{6,0},{7,2},{8,13},{9,15},{10,... | collective-permute-start | bytes 417800 | tf_op jit(solution)/shard_map/ppermute | solution.py:275
  70.9 3.4 %collective-permute-start.17 = (f32[80,128]{1,0:T(8,128)S(1)}, f32[80,128]{1,0:T(8,128)S(1)}, u32[]{:S(2)}, u32[]{:S(2)}) collective-permute-start(f32[80,128]{1,0:T(8,128)S(1)} %get-tuple-element.80.refs_0_), channel_id=1, source_target_pairs={{0,12},{1,21},{2,22},{3,15},{4,16},{5,9},{6,10},{7,19},{8,28},{9,5... | collective-permute-start | bytes 122888 | tf_op jit(solution)/shard_map/ppermute | solution.py:275
  70.9 3.5 %collective-permute-start.18 = (f32[80,128]{1,0:T(8,128)S(1)}, f32[80,128]{1,0:T(8,128)S(1)}, u32[]{:S(2)}, u32[]{:S(2)}) collective-permute-start(f32[80,128]{1,0:T(8,128)S(1)} %get-tuple-element.80.refs_0_), channel_id=1, source_target_pairs={{0,20},{1,13},{2,14},{3,23},{4,8},{5,17},{6,18},{7,11},{8,4},{9,29... | collective-permute-start | bytes 122888 | tf_op jit(solution)/shard_map/ppermute | solution.py:275
  72.1 4.9 %collective-permute-start.19 = (f32[80,128]{1,0:T(8,128)S(1)}, f32[80,128]{1,0:T(8,128)S(1)}, u32[]{:S(2)}, u32[]{:S(2)}) collective-permute-start(f32[80,128]{1,0:T(8,128)S(1)} %get-tuple-element.80.refs_0_), channel_id=1, source_target_pairs={{0,24},{1,25},{2,26},{3,27},{4,28},{5,29},{6,30},{7,31},{8,16},{9,... | collective-permute-start | bytes 122888 | tf_op jit(solution)/shard_map/ppermute | solution.py:275
  77.8 6.0 %collective-permute-start.20 = (f32[272,128]{1,0:T(8,128)S(1)}, f32[272,128]{1,0:T(8,128)S(1)}, u32[]{:S(2)}, u32[]{:S(2)}) collective-permute-start(f32[272,128]{1,0:T(8,128)S(1)} %get-tuple-element.84), channel_id=1, source_target_pairs={{0,5},{1,7},{2,4},{3,6},{4,2},{5,0},{6,3},{7,1},{8,14},{9,12},{10,... | collective-permute-start | bytes 417800 | tf_op jit(solution)/shard_map/ppermute | solution.py:275
  83.9 6.8 %collective-permute-start.21 = (f32[272,128]{1,0:T(8,128)S(1)}, f32[272,128]{1,0:T(8,128)S(1)}, u32[]{:S(2)}, u32[]{:S(2)}) collective-permute-start(f32[272,128]{1,0:T(8,128)S(1)} %maximum_add_fusion.3.za_ref), channel_id=1, source_target_pairs={{0,6},{1,4},{2,7},{3,5},{4,1},{5,3},{6,0},{7,2},{8,13},{9,15},{10,... | collective-permute-start | bytes 417800 | tf_op jit(solution)/shard_map/ppermute | solution.py:275
  91.6 3.4 %collective-permute-start.22 = (f32[80,128]{1,0:T(8,128)S(1)}, f32[80,128]{1,0:T(8,128)S(1)}, u32[]{:S(2)}, u32[]{:S(2)}) collective-permute-start(f32[80,128]{1,0:T(8,128)S(1)} %get-tuple-element.89.refs_0_), channel_id=1, source_target_pairs={{0,12},{1,21},{2,22},{3,15},{4,16},{5,9},{6,10},{7,19},{8,28},{9,5... | collective-permute-start | bytes 122888 | tf_op jit(solution)/shard_map/ppermute | solution.py:275
  91.6 3.9 %collective-permute-start.23 = (f32[80,128]{1,0:T(8,128)S(1)}, f32[80,128]{1,0:T(8,128)S(1)}, u32[]{:S(2)}, u32[]{:S(2)}) collective-permute-start(f32[80,128]{1,0:T(8,128)S(1)} %get-tuple-element.89.refs_0_), channel_id=1, source_target_pairs={{0,20},{1,13},{2,14},{3,23},{4,8},{5,17},{6,18},{7,11},{8,4},{9,29... | collective-permute-start | bytes 122888 | tf_op jit(solution)/shard_map/ppermute | solution.py:275
  93.9 4.9 %collective-permute-start.24 = (f32[80,128]{1,0:T(8,128)S(1)}, f32[80,128]{1,0:T(8,128)S(1)}, u32[]{:S(2)}, u32[]{:S(2)}) collective-permute-start(f32[80,128]{1,0:T(8,128)S(1)} %get-tuple-element.89.refs_0_), channel_id=1, source_target_pairs={{0,24},{1,25},{2,26},{3,27},{4,28},{5,29},{6,30},{7,31},{8,16},{9,... | collective-permute-start | bytes 122888 | tf_op jit(solution)/shard_map/ppermute | solution.py:275
  102.3 4.0 %collective-permute-start.26 = (f32[16,128]{1,0:T(8,128)S(1)}, f32[16,128]{1,0:T(8,128)S(1)}, u32[]{:S(2)}, u32[]{:S(2)}) collective-permute-start(f32[16,128]{1,0:T(8,128)S(1)} %add.47.ca_ref), channel_id=1, source_target_pairs={{0,6},{1,4},{2,7},{3,5},{4,1},{5,3},{6,0},{7,2},{8,13},{9,15},{10,... | collective-permute-start | bytes 24584 | tf_op jit(solution)/shard_map/ppermute | solution.py:275
  (9 other events, 31.6 us)

commit v3 on v2

--- a/solution.py
+++ b/solution.py
@@ -46,6 +46,22 @@
     return lax.broadcasted_iota(jnp.int32, shape, 1)
 
 
+def pack(columns):
+    lane = lane_index((8, LANE))
+    block = jnp.zeros((8, LANE), F32)
+    at = 0
+    for column in columns:
+        for row in range(0, column.shape[0], 8):
+            block = jnp.where(lane == at, column[row:row + 8], block)
+            at += 1
+    return block
+
+
+def unpack(block, rows, index):
+    groups = rows // 8
+    return jnp.concatenate([block[:, index * groups + g:index * groups + g + 1] for g in range(groups)], axis=0)
+
+
 def convert_body(a_ref, high_ref, low_ref):
     for k in range(a_ref.shape[0]):
         high, low = split(a_ref[k])
@@ -64,9 +80,10 @@
 
 
 def to_lines(vector, mats):
-    rows, n = vector.shape[0], vector.shape[1] // 2
+    count = len(mats) // 2
+    rows, n = vector.shape[0], vector.shape[1] // count
     total = None
-    for half in range(2):
+    for half in range(count):
         pair = stacked(vector[:, half * n:(half + 1) * n])
         for part in range(2):
             out = dot(pair, mats[2 * half + part][...], 0)
@@ -114,44 +131,76 @@
     return call(fold_body, [shape, shape], "fold", *pair, w, f, out)
 
 
-def store_flows(vector, hess, previous, mats, payload_ref):
-    rows = vector.shape[0]
-    lines = to_lines(vector, mats)
+def store(lines, columns, payload_ref):
+    rows = lines.shape[0]
     conts = lines.shape[1] // LANE
     for k in range(conts):
         payload_ref[k * rows:(k + 1) * rows, :] = lines[:, k * LANE:(k + 1) * LANE]
-    scaled = hess * vector
-    first = jnp.sum(vector * vector, axis=1, keepdims=True)
-    second = jnp.sum(scaled * vector, axis=1, keepdims=True)
-    lane = lane_index((rows, LANE))
-    packed = jnp.where(lane == 0, first, 0.0) + jnp.where(lane == 1, second, 0.0)
-    if previous is not None:
-        third = jnp.sum(scaled * previous, axis=1, keepdims=True)
-        packed = packed + jnp.where(lane == 2, third, 0.0)
-    payload_ref[conts * rows:(conts + 1) * rows, :] = packed
-
-
-def first_body(r_ref, hess_ref, a0, a1, a2, a3, payload_ref):
-    store_flows(r_ref[...], hess_ref[...], None, (a0, a1, a2, a3), payload_ref)
-
-
-def merged(za_ref, zb_ref, rows, chunks):
-    def block(ref, at):
-        return ref[at * rows:(at + 1) * rows, :]
-
-    own = [block(za_ref, c) + block(zb_ref, chunks + c) for c in range(chunks)]
-    other = [block(za_ref, chunks + c) + block(zb_ref, c) for c in range(chunks)]
-    curved = block(za_ref, 2 * chunks) + block(zb_ref, 2 * chunks)
-    return jnp.concatenate(own + other, axis=1), curved
-
-
-def step_body(za_ref, zb_ref, r_ref, p_ref, x_ref, sc_ref, hess_ref, a0, a1, a2, a3,
+    payload_ref[conts * rows:, :] = pack(columns)
+
+
+def row_sum(value):
+    return jnp.sum(value, axis=1, keepdims=True)
+
+
+def half_of(s, b, bits=None):
+    if bits is None:
+        return (s.bit_count() + b.bit_count()) & 1
+    return sum((s >> i) + (b >> i) for i in range(bits)) & 1
+
+
+def prepare_body(a_hbm, b_hbm, hess_hbm, high_ref, low_ref, mine_ref, theirs_ref, own_ref, extra_ref,
+                 held_ref, b_ref, hess_ref, sems, *, bits):
+    conts = a_hbm.shape[0]
+    copies = [pltpu.make_async_copy(a_hbm.at[k], held_ref.at[k], sems.at[k]) for k in range(conts)]
+    first = pltpu.make_async_copy(b_hbm, b_ref, sems.at[conts])
+    second = pltpu.make_async_copy(hess_hbm, hess_ref, sems.at[conts + 1])
+    for copy in [first, second] + copies:
+        copy.start()
+    first.wait()
+    second.wait()
+    rows = b_ref.shape[0] // 2
+    upper = half_of(lax.axis_index("scen"), lax.axis_index("base"), bits) == 1
+    low, high = b_ref[:rows, :], b_ref[rows:, :]
+    own_ref[...] = jnp.where(upper, high, low)
+    extra_ref[:rows, :] = jnp.where(upper, low, high)
+    hess = hess_ref[...]
+    extra_ref[rows:, :] = jnp.broadcast_to(hess, (8, hess.shape[1]))
+    for k in range(conts):
+        copies[k].wait()
+        one, two = split(held_ref[k])
+        high_ref[:, k * LANE:(k + 1) * LANE] = one
+        low_ref[:, k * LANE:(k + 1) * LANE] = two
+    value = b_ref[...]
+    lines = to_lines(value, (high_ref, low_ref))
+    sums = row_sum(value * value), row_sum(hess * value * value)
+
+    def chosen(value, flip):
+        one, two = (value[:rows], value[rows:]) if flip else (value[rows:], value[:rows])
+        return jnp.where(upper, one, two)
+
+    for flip, ref in ((False, mine_ref), (True, theirs_ref)):
+        store(chosen(lines, flip), [chosen(value, flip) for value in sums], ref)
+
+
+def merged(refs, rows, chunks):
+    lower = (lax.axis_index("scen") & 1) == 0
+    sums = []
+    for one, two in (refs[0:2], refs[2:4]):
+        sums.append([one[c * rows:(c + 1) * rows, :] + two[c * rows:(c + 1) * rows, :] for c in range(chunks)])
+    own = [jnp.where(lower, one, two) for one, two in zip(*sums)]
+    other = [jnp.where(lower, two, one) for one, two in zip(*sums)]
+    top = chunks * rows
+    return jnp.concatenate(own + other, axis=1), unpack(refs[0][top:, :] + refs[1][top:, :], rows, 0)
+
+
+def step_body(za_ref, zb_ref, zc_ref, zd_ref, r_ref, p_ref, x_ref, sc_ref, hess_ref, a0, a1, a2, a3,
               payload_ref, rn_ref, pn_ref, xn_ref, alpha_ref, *, first):
     rows, n = r_ref.shape
     r = r_ref[...]
     hess = hess_ref[...]
-    image, curved = merged(za_ref, zb_ref, rows, n // 2 // LANE)
-    alpha = sc_ref[:, 0:1] / (curved[:, 0:1] + sc_ref[:, 1:2])
+    image, curved = merged((za_ref, zb_ref, zc_ref, zd_ref), rows, n // 2 // LANE)
+    alpha = sc_ref[:, 0:1] / (curved + sc_ref[:, 1:2])
     if first:
         p = r
         xn_ref[...] = alpha * p
@@ -162,7 +211,8 @@
     r = r - alpha * (image + hess * p)
     rn_ref[...] = r
     alpha_ref[...] = jnp.broadcast_to(alpha, alpha_ref.shape)
-    store_flows(r, hess, p, (a0, a1, a2, a3), payload_ref)
+    scaled = hess * r
+    store(to_lines(r, (a0, a1, a2, a3)), [row_sum(r * r), row_sum(scaled * r), row_sum(scaled * p)], payload_ref)
 
 
 def weigh(flows, k, w_ref, f_ref, out_ref):
@@ -177,21 +227,21 @@
     parts, refs = refs[:count], refs[count:]
     fp_ref, fx_ref, sc_ref, alpha_ref, w_ref, f_ref, out_ref = refs[:7]
     mats = () if last else refs[7:11]
-    z_ref, fpn_ref, fxn_ref, scn_ref = refs[7 if last else 11:]
+    *z_refs, fpn_ref, fxn_ref, scn_ref = refs[7 if last else 11:]
     conts = w_ref.shape[0]
-    rows = parts[0].shape[0] // (conts + 1)
-
-    def total(at):
-        values = [ref[at:at + rows, :] for ref in parts]
+    rows = parts[0].shape[0] // conts // 8 * 8
+
+    def total(at, size):
+        values = [ref[at:at + size, :] for ref in parts]
         while len(values) > 1:
             values = [values[i] + values[i + 1] for i in range(0, len(values), 2)]
         return values[0]
 
-    sums = total(conts * rows)
-    rr, base = sums[:, 0:1], sums[:, 1:2]
+    sums = total(conts * rows, 8)
+    rr, base = unpack(sums, rows, 0), unpack(sums, rows, 1)
     if not first:
         beta = rr / sc_ref[:, 0:1]
-        base = base + beta * (2.0 * sums[:, 2:3] + beta * sc_ref[:, 1:2])
+        base = base + beta * (2.0 * unpack(sums, rows, 2) + beta * sc_ref[:, 1:2])
         alpha = alpha_ref[:, 0:1]
     lane = lane_index((rows, LANE))
     packed = jnp.where(lane == 0, rr, 0.0) + jnp.where(lane == 1, base, 0.0)
@@ -202,7 +252,7 @@
     flat = []
     for k in range(conts):
         span = slice(k * rows, (k + 1) * rows)
-        flows = total(k * rows)
+        flows = total(k * rows, rows)
         if not first:
             before = fp_ref[span, :]
             fxn_ref[span, :] = fx_ref[span, :] + alpha * before
@@ -213,24 +263,25 @@
         post, weighted = weigh(flows, k, w_ref, f_ref, out_ref)
         curv = curv + post * weighted
         flat.append(flows)
-    curv = jnp.broadcast_to(jnp.sum(curv, axis=1, keepdims=True), (rows, LANE))
+    curv = pack([row_sum(curv)])
     if last:
-        z_ref[...] = curv
+        z_refs[0][...] = curv
     else:
         halves = from_lines(jnp.concatenate(flat, axis=1), mats)
-        chunks = halves[0].shape[1] // LANE
-        for half in range(2):
+        lower = (lax.axis_index("scen") & 1) == 0
+        own, other = halves
+        chunks = own.shape[1] // LANE
+        for z_ref, value in zip(z_refs, (jnp.where(lower, own, other), jnp.where(lower, other, own))):
             for c in range(chunks):
-                at = (half * chunks + c) * rows
-                z_ref[at:at + rows, :] = halves[half][:, c * LANE:(c + 1) * LANE]
-        z_ref[2 * chunks * rows:, :] = curv
+                z_ref[c * rows:(c + 1) * rows, :] = value[:, c * LANE:(c + 1) * LANE]
+        z_refs[0][chunks * rows:, :] = curv
 
 
 def finish_body(ca_ref, cb_ref, r_ref, p_ref, x_ref, sc_ref, fp_ref, fx_ref, w_ref, f_ref, out_ref,
                 own_ref, send_ref):
     n = r_ref.shape[1] // 2
     rows = r_ref.shape[0]
-    alpha = sc_ref[:, 0:1] / (ca_ref[:, 0:1] + cb_ref[:, 0:1] + sc_ref[:, 1:2])
+    alpha = sc_ref[:, 0:1] / (unpack(ca_ref[...] + cb_ref[...], rows, 0) + sc_ref[:, 1:2])
     p = r_ref[...] + sc_ref[:, 2:3] * p_ref[...]
     x = x_ref[...] + alpha * p
     own_ref[:, :n] = x[:, :n]
@@ -263,9 +314,6 @@
     half = n // LANE * rows
     spread = jnp.broadcast_to(outaged.astype(jnp.int32)[:, None], (conts, lines))
 
-    def half_of(s, b):
-        return (s.bit_count() + b.bit_count()) & 1
-
     def swap(value, *steps):
         pairs = []
         for s in range(scen):
@@ -284,36 +332,49 @@
             return [value, swap(value, one, two), swap(value, two, one), swap(value, (3 * bit, 0))]
         return [value, swap(value, (bit | 1, 0))]
 
-    def over_base(value):
-        bits = [1 << i for i in range((base - 1).bit_length())]
-        for i, bit in enumerate(bits):
-            got = swap(value, (1, bit), (1, bits[(i + 1) % len(bits)]))
-            if i + 1 == len(bits):
-                return value, got
-            if got.shape[0] > 2 * half:
-                got = jnp.concatenate([got[half:2 * half], got[:half], got[2 * half:]], axis=0)
-            value = value + got
-
-    place = lax.axis_index("scen") * base + lax.axis_index("base")
-    bits = (scen * base - 1).bit_length()
-    part = sum((place >> i) & 1 for i in range(bits)) & 1
-    other_a = swap(sensitivity, (1, 0))
-    mine = lax.dynamic_slice_in_dim(right_sides, part * rows, rows, 0)
-    theirs = lax.dynamic_slice_in_dim(right_sides, (1 - part) * rows, rows, 0)
-    extra = jnp.concatenate([theirs, jnp.broadcast_to(base_hessian[None, :], (8, n))], axis=0)
-    other = swap(extra, (1, 0))
-    r = jnp.concatenate([mine, other[:rows]], axis=1)
-    hess = jnp.concatenate([base_hessian[None, :], other[rows:rows + 1]], axis=1)
-    pairs = convert(sensitivity), convert(other_a)
-    mats = [*pairs[0], *pairs[1]]
-
+    def over_base(values):
+        order = [1 << i for i in range((base - 1).bit_length())]
+        for i in range(len(order)):
+            got = []
+            for value in values:
+                steps = [(1, order[(i + turn) % len(order)]) for turn in (0, 1)]
+                got.append(swap(value, *steps))
+            if i + 1 == len(order):
+                return [v for both in zip(values, got) for v in both]
+            values = [value + new for value, new in zip(values, got)]
+
+    bits = max(scen, base).bit_length()
+    part = half_of(lax.axis_index("scen"), lax.axis_index("base"), bits)
     flat = struct((conts * rows, LANE))
     state = struct((rows, 2 * n))
     scal = struct((rows, LANE))
-    payload = struct(((conts + 1) * rows, LANE))
-    wide = struct((2 * half + rows, LANE))
-
-    pay = call(first_body, payload, "first", r, hess, *mats)
+    payload = struct((conts * rows + 8, LANE))
+    wide = [struct((half + 8, LANE)), struct((half, LANE))]
+    block = struct((8, LANE))
+
+    other_a = swap(sensitivity, (1, 0))
+    matrix = struct((n, conts * lines), BF16)
+    high, low, mine, theirs, own, extra = pl.pallas_call(
+        functools.partial(prepare_body, bits=bits),
+        out_shape=[matrix, matrix, payload, payload, struct((rows, n)), struct((rows + 8, n))],
+        in_specs=[pl.BlockSpec(memory_space=pltpu.HBM)] * 3,
+        out_specs=[VM] * 6,
+        scratch_shapes=[
+            pltpu.VMEM(sensitivity.shape, F32),
+            pltpu.VMEM(right_sides.shape, F32),
+            pltpu.VMEM((1, n), F32),
+            pltpu.SemaphoreType.DMA((conts + 2,)),
+        ],
+        compiler_params=PARAMS,
+        name="prepare",
+    )(*[pltpu.with_memory_space_constraint(v, pltpu.HBM) for v in (sensitivity, right_sides, base_hessian.reshape(1, n))])
+    pay = mine + swap(theirs, (1, 0))
+    other = swap(extra, (1, 0))
+    r = jnp.concatenate([own, other[:rows]], axis=1)
+    hess = jnp.concatenate([base_hessian[None, :], other[rows:rows + 1]], axis=1)
+    pairs = (high, low), convert(other_a)
+    mats = [*pairs[0], *pairs[1]]
+
     table = (weights, outage_factors, spread)
     folded = [*fold(pairs[0], *table), *fold(pairs[1], *table)]
     p = x = r
@@ -323,18 +384,18 @@
         first, last = it == 0, it + 1 == ITERS
         sent = over_scen(pay)
         tail = () if last else tuple(folded)
-        z, fp, fx, sc = call(
+        *z, fp, fx, sc = call(
             functools.partial(lines_body, count=len(sent), first=first, last=last),
-            [scal if last else wide, flat, flat, scal], "lines",
+            [*([block] if last else wide), flat, flat, scal], "lines",
             *sent, fp, fx, sc, alpha, *table, *tail)
-        za, zb = over_base(z)
+        z = over_base(z)
         if not last:
             pay, r, p, x, alpha = call(
                 functools.partial(step_body, first=first),
                 [payload, state, state, state, scal], "step",
-                za, zb, r, p, x, sc, hess, *mats)
+                *z, r, p, x, sc, hess, *mats)
     both = struct((rows, n + conts * LANE))
-    own, send = call(finish_body, [both, both], "finish", za, zb, r, p, x, sc, fp, fx, *table)
+    own, send = call(finish_body, [both, both], "finish", *z, r, p, x, sc, fp, fx, *table)
     recv = swap(send, (1, 0))
     which = jnp.broadcast_to(part.astype(jnp.int32), (8, LANE))
     step, flow = call(place_body, [struct((rhs, n)), struct((conts, rhs, lines))], "place", own, recv, which)

time: 109 us -> 102 us (0.936)
  waiting for transfers between devices: 66.6 us -> 45.4 us
  starting transfers between devices: 25.7 us -> 42.4 us
  local copies, waits for them, and re-layouts: 3.32 us -> 0.11 us
  Pallas kernels: 12 us -> 13.2 us
    ppermute x28 -> x37, waiting for transfers between devices: 66.6 us -> 45.4 us  [swap(): return lax.ppermute(value, ('scen', 'base'), pairs)]
    ppermute x28 -> x37, starting transfers between devices: 25.7 us -> 42.4 us  [swap(): return lax.ppermute(value, ('scen', 'base'), pairs)]
    pallas_call x0 -> x1, Pallas kernels: none -> 2.15 us  [per_device(): pl.pallas_call(functools.partial(prepare_body, bits=bits), out_shape=[mat...]
    unnamed x10, local copies, waits for them, and re-layouts: 1.62 us -> 0.03 us
    pallas_call x16 -> x14, Pallas kernels: 12 us -> 11.1 us  [call(): pl.pallas_call(body, out_shape=out_shape, in_specs=[VM] * len(args), out_...]
  transfers between devices with their start and end apart: 28 -> 37, of which waited for: 25 -> 26; matrix products, arithmetic and copies ran while one was open for 2% -> 0% of each run, Pallas kernels for 2% -> 5%
where the time goes in v3:
time: 102 us
  waiting for transfers between devices  45.4 us (45%)
  starting transfers between devices  42.4 us (42%)
  Pallas kernels  13.2 us (13%)
    ppermute x37, waiting for transfers between devices, swap(): return lax.ppermute(value, ('scen', 'base'), pairs)  45.4 us
    ppermute x37, starting transfers between devices, swap(): return lax.ppermute(value, ('scen', 'base'), pairs)  42.4 us
    pallas_call x14, Pallas kernels, call(): pl.pallas_call(body, out_shape=out_shape, in_specs=[VM] * len(args), out_...  11.1 us
    pallas_call x1, Pallas kernels, per_device(): pl.pallas_call(functools.partial(prepare_body, bits=bits), out_shape=[mat...  2.15 us
  transfers between devices with their start and end apart: 37, of which 26 were waited for; matrix products, arithmetic and copies ran while one was open for 0% of the time, Pallas kernels for 5%

profile of v3, /device:TPU:0, one launch (start us, length us, event | category | flops | bytes accessed | tf_op | source)
XLA Modules:
  0.0 102.2 jit_solution(15267912484898552121)
XLA Ops:
  1.2 2.2 %prepare.1 = (bf16[1024,512]{1,0:T(8,128)(2,1)S(1)}, bf16[1024,512]{1,0:T(8,128)(2,1)S(1)}, f32[72,128]{1,0:T(8,128)S(1)}, f32[72,128]{1,0:T(8,128)S(1)}, f32[16...) custom-call(f32[4,1024,128]{2,1,0:T(8,128)} %a_hbm.1, f32[32,1024]{1,0:T(8,128)} %b_hbm.1, f32[1,1024]{1,0:T(1,128)} %bitcast.1), custom_call_target="tpu_custom_call" | custom-call | tf_op jit(solution)/shard_map/prepare/pallas_call | solution.py:357
  5.4 2.6 %collective-permute-start.1 = (f32[72,128]{1,0:T(8,128)S(1)}, f32[72,128]{1,0:T(8,128)S(1)}, u32[]{:S(2)}, u32[]{:S(2)}) collective-permute-start(f32[72,128]{1,0:T(8,128)S(1)} %add.51.refs_0_), channel_id=1, source_target_pairs={{0,12},{1,21},{2,22},{3,15},{4,16},{5,9},{6,10},{7,19},{8,28},{9,5... | collective-permute-start | bytes 110600 | tf_op jit(solution)/shard_map/ppermute | solution.py:323
  12.3 2.1 %collective-permute-done.3.refs_3_ = f32[72,128]{1,0:T(8,128)S(1)} collective-permute-done((f32[72,128]{1,0:T(8,128)S(1)}, f32[72,128]{1,0:T(8,128)S(1)}, u32[]{:S(2)}, u32[]{:S(2)}) %collective-permute-start.3) | collective-permute-done | bytes 36896 | tf_op jit(solution)/shard_map/ppermute | solution.py:323
  17.0 1.9 %collective-permute-done.7 = f32[128,128]{1,0:T(8,128)S(1)} collective-permute-done((f32[128,128]{1,0:T(8,128)S(1)}, f32[128,128]{1,0:T(8,128)S(1)}, u32[]{:S(2)}, u32[]{:S(2)}) %collective-permute-start.7) | collective-permute-done | bytes 65568 | tf_op jit(solution)/shard_map/ppermute | solution.py:323
  18.9 3.2 %collective-permute-start.8 = (f32[128,128]{1,0:T(8,128)S(1)}, f32[128,128]{1,0:T(8,128)S(1)}, u32[]{:S(2)}, u32[]{:S(2)}) collective-permute-start(f32[128,128]{1,0:T(8,128)S(1)} %add.53.zc_ref), channel_id=1, source_target_pairs={{0,6},{1,4},{2,7},{3,5},{4,1},{5,3},{6,0},{7,2},{8,13},{9,15},{10,... | collective-permute-start | bytes 196616 | tf_op jit(solution)/shard_map/ppermute | solution.py:323
  24.2 2.7 %collective-permute-done.6.zb_ref = f32[136,128]{1,0:T(8,128)S(1)} collective-permute-done((f32[136,128]{1,0:T(8,128)S(1)}, f32[136,128]{1,0:T(8,128)S(1)}, u32[]{:S(2)}, u32[]{:S(2)}) %collective-permute-start.6) | collective-permute-done | bytes 69664 | tf_op jit(solution)/shard_map/ppermute | solution.py:323
  28.7 2.4 %collective-permute-start.12 = (f32[72,128]{1,0:T(8,128)S(1)}, f32[72,128]{1,0:T(8,128)S(1)}, u32[]{:S(2)}, u32[]{:S(2)}) collective-permute-start(f32[72,128]{1,0:T(8,128)S(1)} %get-tuple-element.75.refs_0_), channel_id=1, source_target_pairs={{0,24},{1,25},{2,26},{3,27},{4,28},{5,29},{6,30},{7,31},{8,16},{9,... | collective-permute-start | bytes 110600 | tf_op jit(solution)/shard_map/ppermute | solution.py:323
  36.4 2.0 %collective-permute-done.13 = f32[136,128]{1,0:T(8,128)S(1)} collective-permute-done((f32[136,128]{1,0:T(8,128)S(1)}, f32[136,128]{1,0:T(8,128)S(1)}, u32[]{:S(2)}, u32[]{:S(2)}) %collective-permute-start.13) | collective-permute-done | bytes 69664 | tf_op jit(solution)/shard_map/ppermute | solution.py:323
  39.8 2.3 %collective-permute-start.16 = (f32[128,128]{1,0:T(8,128)S(1)}, f32[128,128]{1,0:T(8,128)S(1)}, u32[]{:S(2)}, u32[]{:S(2)}) collective-permute-start(f32[128,128]{1,0:T(8,128)S(1)} %add.55.zc_ref), channel_id=1, source_target_pairs={{0,6},{1,4},{2,7},{3,5},{4,1},{5,3},{6,0},{7,2},{8,13},{9,15},{10,... | collective-permute-start | bytes 196616 | tf_op jit(solution)/shard_map/ppermute | solution.py:323
  42.1 2.5 %collective-permute-done.16.zd_ref = f32[128,128]{1,0:T(8,128)S(1)} collective-permute-done((f32[128,128]{1,0:T(8,128)S(1)}, f32[128,128]{1,0:T(8,128)S(1)}, u32[]{:S(2)}, u32[]{:S(2)}) %collective-permute-start.16) | collective-permute-done | bytes 65568 | tf_op jit(solution)/shard_map/ppermute | solution.py:323
  45.5 2.0 %collective-permute-start.17 = (f32[72,128]{1,0:T(8,128)S(1)}, f32[72,128]{1,0:T(8,128)S(1)}, u32[]{:S(2)}, u32[]{:S(2)}) collective-permute-start(f32[72,128]{1,0:T(8,128)S(1)} %get-tuple-element.85.refs_0_), channel_id=1, source_target_pairs={{0,12},{1,21},{2,22},{3,15},{4,16},{5,9},{6,10},{7,19},{8,28},{9,5... | collective-permute-start | bytes 110600 | tf_op jit(solution)/shard_map/ppermute | solution.py:323
  50.9 3.1 %collective-permute-done.19.refs_3_ = f32[72,128]{1,0:T(8,128)S(1)} collective-permute-done((f32[72,128]{1,0:T(8,128)S(1)}, f32[72,128]{1,0:T(8,128)S(1)}, u32[]{:S(2)}, u32[]{:S(2)}) %collective-permute-start.19) | collective-permute-done | bytes 36896 | tf_op jit(solution)/shard_map/ppermute | solution.py:323
  56.6 2.2 %collective-permute-done.20 = f32[136,128]{1,0:T(8,128)S(1)} collective-permute-done((f32[136,128]{1,0:T(8,128)S(1)}, f32[136,128]{1,0:T(8,128)S(1)}, u32[]{:S(2)}, u32[]{:S(2)}) %collective-permute-start.20) | collective-permute-done | bytes 69664 | tf_op jit(solution)/shard_map/ppermute | solution.py:323
  58.9 2.1 %collective-permute-start.21 = (f32[136,128]{1,0:T(8,128)S(1)}, f32[136,128]{1,0:T(8,128)S(1)}, u32[]{:S(2)}, u32[]{:S(2)}) collective-permute-start(f32[136,128]{1,0:T(8,128)S(1)} %add.56.za_ref), channel_id=1, source_target_pairs={{0,6},{1,4},{2,7},{3,5},{4,1},{5,3},{6,0},{7,2},{8,13},{9,15},{10,... | collective-permute-start | bytes 208904 | tf_op jit(solution)/shard_map/ppermute | solution.py:323
  62.1 3.7 %collective-permute-done.23.zd_ref = f32[128,128]{1,0:T(8,128)S(1)} collective-permute-done((f32[128,128]{1,0:T(8,128)S(1)}, f32[128,128]{1,0:T(8,128)S(1)}, u32[]{:S(2)}, u32[]{:S(2)}) %collective-permute-start.23) | collective-permute-done | bytes 65568 | tf_op jit(solution)/shard_map/ppermute | solution.py:323
  67.1 2.8 %collective-permute-start.26 = (f32[72,128]{1,0:T(8,128)S(1)}, f32[72,128]{1,0:T(8,128)S(1)}, u32[]{:S(2)}, u32[]{:S(2)}) collective-permute-start(f32[72,128]{1,0:T(8,128)S(1)} %get-tuple-element.95.refs_0_), channel_id=1, source_target_pairs={{0,24},{1,25},{2,26},{3,27},{4,28},{5,29},{6,30},{7,31},{8,16},{9,... | collective-permute-start | bytes 110600 | tf_op jit(solution)/shard_map/ppermute | solution.py:323
  74.6 2.7 %collective-permute-done.27 = f32[136,128]{1,0:T(8,128)S(1)} collective-permute-done((f32[136,128]{1,0:T(8,128)S(1)}, f32[136,128]{1,0:T(8,128)S(1)}, u32[]{:S(2)}, u32[]{:S(2)}) %collective-permute-start.27) | collective-permute-done | bytes 69664 | tf_op jit(solution)/shard_map/ppermute | solution.py:323
  78.5 1.9 %collective-permute-start.30 = (f32[128,128]{1,0:T(8,128)S(1)}, f32[128,128]{1,0:T(8,128)S(1)}, u32[]{:S(2)}, u32[]{:S(2)}) collective-permute-start(f32[128,128]{1,0:T(8,128)S(1)} %add.59.zc_ref), channel_id=1, source_target_pairs={{0,6},{1,4},{2,7},{3,5},{4,1},{5,3},{6,0},{7,2},{8,13},{9,15},{10,... | collective-permute-start | bytes 196616 | tf_op jit(solution)/shard_map/ppermute | solution.py:323
  80.4 3.1 %collective-permute-done.30.zd_ref = f32[128,128]{1,0:T(8,128)S(1)} collective-permute-done((f32[128,128]{1,0:T(8,128)S(1)}, f32[128,128]{1,0:T(8,128)S(1)}, u32[]{:S(2)}, u32[]{:S(2)}) %collective-permute-start.30) | collective-permute-done | bytes 65568 | tf_op jit(solution)/shard_map/ppermute | solution.py:323
  84.5 2.3 %collective-permute-start.31 = (f32[72,128]{1,0:T(8,128)S(1)}, f32[72,128]{1,0:T(8,128)S(1)}, u32[]{:S(2)}, u32[]{:S(2)}) collective-permute-start(f32[72,128]{1,0:T(8,128)S(1)} %get-tuple-element.105.refs_0_), channel_id=1, source_target_pairs={{0,12},{1,21},{2,22},{3,15},{4,16},{5,9},{6,10},{7,19},{8,28},{9,5... | collective-permute-start | bytes 110600 | tf_op jit(solution)/shard_map/ppermute | solution.py:323
  88.5 2.1 %collective-permute-done.32.refs_2_ = f32[72,128]{1,0:T(8,128)S(1)} collective-permute-done((f32[72,128]{1,0:T(8,128)S(1)}, f32[72,128]{1,0:T(8,128)S(1)}, u32[]{:S(2)}, u32[]{:S(2)}) %collective-permute-start.32) | collective-permute-done | bytes 36896 | tf_op jit(solution)/shard_map/ppermute | solution.py:323
  90.6 1.8 %collective-permute-done.33.refs_3_ = f32[72,128]{1,0:T(8,128)S(1)} collective-permute-done((f32[72,128]{1,0:T(8,128)S(1)}, f32[72,128]{1,0:T(8,128)S(1)}, u32[]{:S(2)}, u32[]{:S(2)}) %collective-permute-start.33) | collective-permute-done | bytes 36896 | tf_op jit(solution)/shard_map/ppermute | solution.py:323
  93.2 2.6 %collective-permute-done.34 = f32[8,128]{1,0:T(8,128)S(1)} collective-permute-done((f32[8,128]{1,0:T(8,128)S(1)}, f32[8,128]{1,0:T(8,128)S(1)}, u32[]{:S(2)}, u32[]{:S(2)}) %collective-permute-start.34) | collective-permute-done | bytes 4128 | tf_op jit(solution)/shard_map/ppermute | solution.py:323
  97.7 2.1 %collective-permute-done.35.cb_ref = f32[8,128]{1,0:T(8,128)S(1)} collective-permute-done((f32[8,128]{1,0:T(8,128)S(1)}, f32[8,128]{1,0:T(8,128)S(1)}, u32[]{:S(2)}, u32[]{:S(2)}) %collective-permute-start.35) | collective-permute-done | bytes 4128 | tf_op jit(solution)/shard_map/ppermute | solution.py:323
  (95 shorter events, 42.8 us)
Async XLA Ops:
  0.7 10.1 %collective-permute-start.4 = (f32[4,1024,128]{2,1,0:T(8,128)}, f32[4,1024,128]{2,1,0:T(8,128)S(1)}, u32[]{:S(2)}, u32[]{:S(2)}) collective-permute-start(f32[4,1024,128]{2,1,0:T(8,128)} %a_hbm.1), channel_id=1, source_target_pairs={{0,4},{1,5},{2,6},{3,7},{4,0},{5,1},{6,2},{7,3},{8,12},{9,13},{10,... | collective-permute-start | bytes 6291464 | tf_op jit(solution)/shard_map/ppermute | solution.py:323
  3.4 7.3 %collective-permute-start.9 = (f32[24,1024]{1,0:T(8,128)S(1)}, f32[24,1024]{1,0:T(8,128)S(1)}, u32[]{:S(2)}, u32[]{:S(2)}) collective-permute-start(f32[24,1024]{1,0:T(8,128)S(1)} %get-tuple-element.73), channel_id=1, source_target_pairs={{0,4},{1,5},{2,6},{3,7},{4,0},{5,1},{6,2},{7,3},{8,12},{9,13},{10,... | collective-permute-start | bytes 294920 | tf_op jit(solution)/shard_map/ppermute | solution.py:323
  5.4 6.8 %collective-permute-start.1 = (f32[72,128]{1,0:T(8,128)S(1)}, f32[72,128]{1,0:T(8,128)S(1)}, u32[]{:S(2)}, u32[]{:S(2)}) collective-permute-start(f32[72,128]{1,0:T(8,128)S(1)} %add.51.refs_0_), channel_id=1, source_target_pairs={{0,12},{1,21},{2,22},{3,15},{4,16},{5,9},{6,10},{7,19},{8,28},{9,5... | collective-permute-start | bytes 110600 | tf_op jit(solution)/shard_map/ppermute | solution.py:323
  8.0 4.3 %collective-permute-start.2 = (f32[72,128]{1,0:T(8,128)S(1)}, f32[72,128]{1,0:T(8,128)S(1)}, u32[]{:S(2)}, u32[]{:S(2)}) collective-permute-start(f32[72,128]{1,0:T(8,128)S(1)} %add.51.refs_0_), channel_id=1, source_target_pairs={{0,20},{1,13},{2,14},{3,23},{4,8},{5,17},{6,18},{7,11},{8,4},{9,29... | collective-permute-start | bytes 110600 | tf_op jit(solution)/shard_map/ppermute | solution.py:323
  9.5 4.9 %collective-permute-start.3 = (f32[72,128]{1,0:T(8,128)S(1)}, f32[72,128]{1,0:T(8,128)S(1)}, u32[]{:S(2)}, u32[]{:S(2)}) collective-permute-start(f32[72,128]{1,0:T(8,128)S(1)} %add.51.refs_0_), channel_id=1, source_target_pairs={{0,24},{1,25},{2,26},{3,27},{4,28},{5,29},{6,30},{7,31},{8,16},{9,... | collective-permute-start | bytes 110600 | tf_op jit(solution)/shard_map/ppermute | solution.py:323
  15.4 6.7 %collective-permute-start.5 = (f32[136,128]{1,0:T(8,128)S(1)}, f32[136,128]{1,0:T(8,128)S(1)}, u32[]{:S(2)}, u32[]{:S(2)}) collective-permute-start(f32[136,128]{1,0:T(8,128)S(1)} %get-tuple-element.70), channel_id=1, source_target_pairs={{0,5},{1,7},{2,4},{3,6},{4,2},{5,0},{6,3},{7,1},{8,14},{9,12},{10,... | collective-permute-start | bytes 208904 | tf_op jit(solution)/shard_map/ppermute | solution.py:323
  18.9 5.3 %collective-permute-start.8 = (f32[128,128]{1,0:T(8,128)S(1)}, f32[128,128]{1,0:T(8,128)S(1)}, u32[]{:S(2)}, u32[]{:S(2)}) collective-permute-start(f32[128,128]{1,0:T(8,128)S(1)} %add.53.zc_ref), channel_id=1, source_target_pairs={{0,6},{1,4},{2,7},{3,5},{4,1},{5,3},{6,0},{7,2},{8,13},{9,15},{10,... | collective-permute-start | bytes 196616 | tf_op jit(solution)/shard_map/ppermute | solution.py:323
  22.1 4.8 %collective-permute-start.6 = (f32[136,128]{1,0:T(8,128)S(1)}, f32[136,128]{1,0:T(8,128)S(1)}, u32[]{:S(2)}, u32[]{:S(2)}) collective-permute-start(f32[136,128]{1,0:T(8,128)S(1)} %add.52.za_ref), channel_id=1, source_target_pairs={{0,6},{1,4},{2,7},{3,5},{4,1},{5,3},{6,0},{7,2},{8,13},{9,15},{10,... | collective-permute-start | bytes 208904 | tf_op jit(solution)/shard_map/ppermute | solution.py:323
  28.7 5.1 %collective-permute-start.12 = (f32[72,128]{1,0:T(8,128)S(1)}, f32[72,128]{1,0:T(8,128)S(1)}, u32[]{:S(2)}, u32[]{:S(2)}) collective-permute-start(f32[72,128]{1,0:T(8,128)S(1)} %get-tuple-element.75.refs_0_), channel_id=1, source_target_pairs={{0,24},{1,25},{2,26},{3,27},{4,28},{5,29},{6,30},{7,31},{8,16},{9,... | collective-permute-start | bytes 110600 | tf_op jit(solution)/shard_map/ppermute | solution.py:323
  34.6 5.2 %collective-permute-start.15 = (f32[128,128]{1,0:T(8,128)S(1)}, f32[128,128]{1,0:T(8,128)S(1)}, u32[]{:S(2)}, u32[]{:S(2)}) collective-permute-start(f32[128,128]{1,0:T(8,128)S(1)} %get-tuple-element.80), channel_id=1, source_target_pairs={{0,5},{1,7},{2,4},{3,6},{4,2},{5,0},{6,3},{7,1},{8,14},{9,12},{10,... | collective-permute-start | bytes 196616 | tf_op jit(solution)/shard_map/ppermute | solution.py:323
  38.4 6.2 %collective-permute-start.14 = (f32[136,128]{1,0:T(8,128)S(1)}, f32[136,128]{1,0:T(8,128)S(1)}, u32[]{:S(2)}, u32[]{:S(2)}) collective-permute-start(f32[136,128]{1,0:T(8,128)S(1)} %add.54.za_ref), channel_id=1, source_target_pairs={{0,6},{1,4},{2,7},{3,5},{4,1},{5,3},{6,0},{7,2},{8,13},{9,15},{10,... | collective-permute-start | bytes 208904 | tf_op jit(solution)/shard_map/ppermute | solution.py:323
  39.8 4.8 %collective-permute-start.16 = (f32[128,128]{1,0:T(8,128)S(1)}, f32[128,128]{1,0:T(8,128)S(1)}, u32[]{:S(2)}, u32[]{:S(2)}) collective-permute-start(f32[128,128]{1,0:T(8,128)S(1)} %add.55.zc_ref), channel_id=1, source_target_pairs={{0,6},{1,4},{2,7},{3,5},{4,1},{5,3},{6,0},{7,2},{8,13},{9,15},{10,... | collective-permute-start | bytes 196616 | tf_op jit(solution)/shard_map/ppermute | solution.py:323
  49.1 4.9 %collective-permute-start.19 = (f32[72,128]{1,0:T(8,128)S(1)}, f32[72,128]{1,0:T(8,128)S(1)}, u32[]{:S(2)}, u32[]{:S(2)}) collective-permute-start(f32[72,128]{1,0:T(8,128)S(1)} %get-tuple-element.85.refs_0_), channel_id=1, source_target_pairs={{0,24},{1,25},{2,26},{3,27},{4,28},{5,29},{6,30},{7,31},{8,16},{9,... | collective-permute-start | bytes 110600 | tf_op jit(solution)/shard_map/ppermute | solution.py:323
  54.9 4.0 %collective-permute-start.20 = (f32[136,128]{1,0:T(8,128)S(1)}, f32[136,128]{1,0:T(8,128)S(1)}, u32[]{:S(2)}, u32[]{:S(2)}) collective-permute-start(f32[136,128]{1,0:T(8,128)S(1)} %get-tuple-element.89), channel_id=1, source_target_pairs={{0,5},{1,7},{2,4},{3,6},{4,2},{5,0},{6,3},{7,1},{8,14},{9,12},{10,... | collective-permute-start | bytes 208904 | tf_op jit(solution)/shard_map/ppermute | solution.py:323
  55.0 5.9 %collective-permute-start.22 = (f32[128,128]{1,0:T(8,128)S(1)}, f32[128,128]{1,0:T(8,128)S(1)}, u32[]{:S(2)}, u32[]{:S(2)}) collective-permute-start(f32[128,128]{1,0:T(8,128)S(1)} %get-tuple-element.90), channel_id=1, source_target_pairs={{0,5},{1,7},{2,4},{3,6},{4,2},{5,0},{6,3},{7,1},{8,14},{9,12},{10,... | collective-permute-start | bytes 196616 | tf_op jit(solution)/shard_map/ppermute | solution.py:323
  58.9 6.9 %collective-permute-start.21 = (f32[136,128]{1,0:T(8,128)S(1)}, f32[136,128]{1,0:T(8,128)S(1)}, u32[]{:S(2)}, u32[]{:S(2)}) collective-permute-start(f32[136,128]{1,0:T(8,128)S(1)} %add.56.za_ref), channel_id=1, source_target_pairs={{0,6},{1,4},{2,7},{3,5},{4,1},{5,3},{6,0},{7,2},{8,13},{9,15},{10,... | collective-permute-start | bytes 208904 | tf_op jit(solution)/shard_map/ppermute | solution.py:323
  61.0 4.8 %collective-permute-start.23 = (f32[128,128]{1,0:T(8,128)S(1)}, f32[128,128]{1,0:T(8,128)S(1)}, u32[]{:S(2)}, u32[]{:S(2)}) collective-permute-start(f32[128,128]{1,0:T(8,128)S(1)} %add.57.zc_ref), channel_id=1, source_target_pairs={{0,6},{1,4},{2,7},{3,5},{4,1},{5,3},{6,0},{7,2},{8,13},{9,15},{10,... | collective-permute-start | bytes 196616 | tf_op jit(solution)/shard_map/ppermute | solution.py:323
  67.1 4.9 %collective-permute-start.26 = (f32[72,128]{1,0:T(8,128)S(1)}, f32[72,128]{1,0:T(8,128)S(1)}, u32[]{:S(2)}, u32[]{:S(2)}) collective-permute-start(f32[72,128]{1,0:T(8,128)S(1)} %get-tuple-element.95.refs_0_), channel_id=1, source_target_pairs={{0,24},{1,25},{2,26},{3,27},{4,28},{5,29},{6,30},{7,31},{8,16},{9,... | collective-permute-start | bytes 110600 | tf_op jit(solution)/shard_map/ppermute | solution.py:323
  72.9 4.5 %collective-permute-start.27 = (f32[136,128]{1,0:T(8,128)S(1)}, f32[136,128]{1,0:T(8,128)S(1)}, u32[]{:S(2)}, u32[]{:S(2)}) collective-permute-start(f32[136,128]{1,0:T(8,128)S(1)} %get-tuple-element.99), channel_id=1, source_target_pairs={{0,5},{1,7},{2,4},{3,6},{4,2},{5,0},{6,3},{7,1},{8,14},{9,12},{10,... | collective-permute-start | bytes 208904 | tf_op jit(solution)/shard_map/ppermute | solution.py:323
  73.3 5.3 %collective-permute-start.29 = (f32[128,128]{1,0:T(8,128)S(1)}, f32[128,128]{1,0:T(8,128)S(1)}, u32[]{:S(2)}, u32[]{:S(2)}) collective-permute-start(f32[128,128]{1,0:T(8,128)S(1)} %get-tuple-element.100), channel_id=1, source_target_pairs={{0,5},{1,7},{2,4},{3,6},{4,2},{5,0},{6,3},{7,1},{8,14},{9,12},{10,... | collective-permute-start | bytes 196616 | tf_op jit(solution)/shard_map/ppermute | solution.py:323
  77.4 6.2 %collective-permute-start.28 = (f32[136,128]{1,0:T(8,128)S(1)}, f32[136,128]{1,0:T(8,128)S(1)}, u32[]{:S(2)}, u32[]{:S(2)}) collective-permute-start(f32[136,128]{1,0:T(8,128)S(1)} %add.58.za_ref), channel_id=1, source_target_pairs={{0,6},{1,4},{2,7},{3,5},{4,1},{5,3},{6,0},{7,2},{8,13},{9,15},{10,... | collective-permute-start | bytes 208904 | tf_op jit(solution)/shard_map/ppermute | solution.py:323
  78.5 5.0 %collective-permute-start.30 = (f32[128,128]{1,0:T(8,128)S(1)}, f32[128,128]{1,0:T(8,128)S(1)}, u32[]{:S(2)}, u32[]{:S(2)}) collective-permute-start(f32[128,128]{1,0:T(8,128)S(1)} %add.59.zc_ref), channel_id=1, source_target_pairs={{0,6},{1,4},{2,7},{3,5},{4,1},{5,3},{6,0},{7,2},{8,13},{9,15},{10,... | collective-permute-start | bytes 196616 | tf_op jit(solution)/shard_map/ppermute | solution.py:323
  84.5 4.0 %collective-permute-start.31 = (f32[72,128]{1,0:T(8,128)S(1)}, f32[72,128]{1,0:T(8,128)S(1)}, u32[]{:S(2)}, u32[]{:S(2)}) collective-permute-start(f32[72,128]{1,0:T(8,128)S(1)} %get-tuple-element.105.refs_0_), channel_id=1, source_target_pairs={{0,12},{1,21},{2,22},{3,15},{4,16},{5,9},{6,10},{7,19},{8,28},{9,5... | collective-permute-start | bytes 110600 | tf_op jit(solution)/shard_map/ppermute | solution.py:323
  87.6 4.9 %collective-permute-start.33 = (f32[72,128]{1,0:T(8,128)S(1)}, f32[72,128]{1,0:T(8,128)S(1)}, u32[]{:S(2)}, u32[]{:S(2)}) collective-permute-start(f32[72,128]{1,0:T(8,128)S(1)} %get-tuple-element.105.refs_0_), channel_id=1, source_target_pairs={{0,24},{1,25},{2,26},{3,27},{4,28},{5,29},{6,30},{7,31},{8,16},{9,... | collective-permute-start | bytes 110600 | tf_op jit(solution)/shard_map/ppermute | solution.py:323
  (20 other events, 91.4 us)

commit v4 on v3

v4 whole, which is shorter than its diff:
```python
import functools

import jax
import jax.numpy as jnp
from jax import lax
from jax.experimental import pallas as pl
from jax.experimental.pallas import tpu as pltpu
from jax.sharding import PartitionSpec as P

ITERS = 5
LANE = 128
F32 = jnp.float32
BF16 = jnp.bfloat16
VM = pl.BlockSpec(memory_space=pltpu.VMEM)
PARAMS = pltpu.CompilerParams(vmem_limit_bytes=24 * 1024 * 1024)


def call(body, out_shape, name, *args):
    many = isinstance(out_shape, (list, tuple))
    return pl.pallas_call(
        body,
        out_shape=out_shape,
        in_specs=[VM] * len(args),
        out_specs=[VM] * len(out_shape) if many else VM,
        compiler_params=PARAMS,
        name=name,
    )(*args)


def struct(shape, dtype=F32):
    return jax.ShapeDtypeStruct(shape, dtype)


def split(value):
    high = value.astype(BF16)
    low = (value - high.astype(F32)).astype(BF16)
    return high, low


def stacked(value):
    high, low = split(value)
    return jnp.concatenate([high, low], axis=0)


def lane_index(shape):
    return lax.broadcasted_iota(jnp.int32, shape, 1)


def pack(columns):
    lane = lane_index((8, LANE))
    block = jnp.zeros((8, LANE), F32)
    at = 0
    for column in columns:
        for row in range(0, column.shape[0], 8):
            block = jnp.where(lane == at, column[row:row + 8], block)
            at += 1
    return block


def unpack(block, rows, index):
    groups = rows // 8
    return jnp.concatenate([block[:, index * groups + g:index * groups + g + 1] for g in range(groups)], axis=0)


def core():
    return lax.axis_index("scen") & 1


def with_slot(slot, refs, body):
    own = core() == slot

    @pl.when(own)
    def _():
        body(*refs[:2])

    @pl.when(jnp.logical_not(own))
    def _():
        body(*refs[2:])


def dot(lhs, rhs, rhs_dim):
    return lax.dot_general(lhs, rhs, (((1,), (rhs_dim,)), ((), ())), preferred_element_type=F32)


def to_lines(vector, high_ref, low_ref):
    rows = vector.shape[0]
    pair = stacked(vector)
    total = dot(pair, high_ref[...], 0) + dot(pair, low_ref[...], 0)
    return total[:rows] + total[rows:]


def from_lines(pair, z_ref, high_ref, low_ref):
    rows = pair.shape[0] // 2
    total = dot(pair, high_ref[...], 0) + dot(pair, low_ref[...], 0)
    image = total[:rows] + total[rows:]
    for c in range(image.shape[1] // LANE):
        z_ref[c * rows:(c + 1) * rows, :] = image[:, c * LANE:(c + 1) * LANE]


def operator(w, f, out):
    row = lax.broadcasted_iota(jnp.int32, (LANE, LANE), 0)
    col = lax.broadcasted_iota(jnp.int32, (LANE, LANE), 1)
    lane = lane_index((1, LANE))
    kept = jnp.where(lane == out, 0.0, f)
    gain = w * kept
    corner = jnp.sum(gain * kept, axis=1, keepdims=True)
    edge = jnp.where(row == out, gain, 0.0)
    inner = jnp.where(row == col, jnp.where(col == out, corner, w), 0.0)
    return inner + edge + edge.T


def fold_one(k, high_ref, low_ref, w_ref, f_ref, out_ref, bh_ref, bl_ref):
    span = slice(k * LANE, (k + 1) * LANE)
    op = operator(w_ref[k:k + 1, :], f_ref[k:k + 1, :], out_ref[k:k + 1, :])
    pair = stacked(op)
    main = dot(pair, high_ref[:, span], 1)
    rest = dot(pair[:LANE], low_ref[:, span], 1)
    high, low = split(main[:LANE] + (main[LANE:] + rest))
    bh_ref[span, :] = high
    bl_ref[span, :] = low


def fold_body(high_ref, low_ref, w_ref, f_ref, out_ref, bh_ref, bl_ref):
    for k in range(w_ref.shape[0]):
        fold_one(k, high_ref, low_ref, w_ref, f_ref, out_ref, bh_ref, bl_ref)


def reads(a_hbm, held_ref, sems):
    return [pltpu.make_async_copy(a_hbm.at[k], held_ref.at[k], sems.at[k]) for k in range(a_hbm.shape[0])]


def convert_one(k, held_ref, high_ref, low_ref):
    high, low = split(held_ref[k])
    high_ref[:, k * LANE:(k + 1) * LANE] = high
    low_ref[:, k * LANE:(k + 1) * LANE] = low


def absorb_body(a_hbm, w_ref, f_ref, out_ref, high_ref, low_ref, bh_ref, bl_ref, held_ref, sems):
    copies = reads(a_hbm, held_ref, sems)
    for copy in copies:
        copy.start()
    for k, copy in enumerate(copies):
        copy.wait()
        convert_one(k, held_ref, high_ref, low_ref)
        fold_one(k, high_ref, low_ref, w_ref, f_ref, out_ref, bh_ref, bl_ref)


def fold(pair, w, f, out):
    n, m = pair[0].shape
    shape = struct((m, n), BF16)
    return call(fold_body, [shape, shape], "fold", *pair, w, f, out)


def store(lines, columns, payload_ref):
    rows = lines.shape[0]
    conts = lines.shape[1] // LANE
    for k in range(conts):
        payload_ref[k * rows:(k + 1) * rows, :] = lines[:, k * LANE:(k + 1) * LANE]
    if columns is not None:
        payload_ref[conts * rows:, :] = pack(columns)


def row_sum(value):
    return jnp.sum(value, axis=1, keepdims=True)


def flips(step, scen):
    return (step & (scen // 2 - 1)).bit_count() & 1


def half_of(s, b, scen, bits):
    s = s & (scen // 2 - 1)
    return sum((s >> i) + (b >> i) for i in range(bits)) & 1


def prepare_body(a_hbm, b_hbm, hess_hbm, high_ref, low_ref, mine_ref, theirs_ref, own_ref, extra_ref,
                 held_ref, b_ref, hess_ref, sems, *, scen, bits):
    conts = a_hbm.shape[0]
    copies = reads(a_hbm, held_ref, sems)
    first = pltpu.make_async_copy(b_hbm, b_ref, sems.at[conts])
    second = pltpu.make_async_copy(hess_hbm, hess_ref, sems.at[conts + 1])
    for copy in [first, second] + copies:
        copy.start()
    first.wait()
    second.wait()
    rows = b_ref.shape[0] // 2
    upper = half_of(lax.axis_index("scen"), lax.axis_index("base"), scen, bits) == 1
    low, high = b_ref[:rows, :], b_ref[rows:, :]
    own_ref[...] = jnp.where(upper, high, low)
    extra_ref[:rows, :] = jnp.where(upper, low, high)
    hess = hess_ref[...]
    extra_ref[rows:, :] = jnp.broadcast_to(hess, (8, hess.shape[1]))
    for k in range(conts):
        copies[k].wait()
        convert_one(k, held_ref, high_ref, low_ref)
    value = b_ref[...]
    lines = to_lines(value, high_ref, low_ref)
    sums = row_sum(value * value), row_sum(hess * value * value)

    def chosen(value, flip):
        one, two = (value[:rows], value[rows:]) if flip else (value[rows:], value[:rows])
        return jnp.where(upper, one, two)

    for flip, ref in ((False, mine_ref), (True, theirs_ref)):
        store(chosen(lines, flip), [chosen(value, flip) for value in sums], ref)


def summed(za_ref, zb_ref, rows, n):
    blocks = [za_ref[c * rows:(c + 1) * rows, :] + zb_ref[c * rows:(c + 1) * rows, :] for c in range(n // LANE)]
    return jnp.concatenate(blocks, axis=1)


def step_body(*refs, slot, first):
    za_ref, zb_ref, r_ref, p_ref, x_ref, sc_ref, hess_ref = refs[:7]
    mats, refs = refs[7:11], refs[11:]
    rows, n = r_ref.shape
    r = r_ref[...]
    hess = hess_ref[...]
    if slot == 0:
        out_ref, sums_ref, rn_ref, pn_ref, xn_ref, alpha_ref = refs
        top = n // LANE * rows
        curved = unpack(za_ref[top:, :] + zb_ref[top:, :], rows, 0)
        alpha = sc_ref[:, 0:1] / (curved + sc_ref[:, 1:2])
        alpha_ref[...] = jnp.broadcast_to(alpha, alpha_ref.shape)
    else:
        alpha_in, share_ref, share_sums, out_ref, rn_ref, pn_ref, xn_ref = refs
        alpha = alpha_in[:, 0:1]
    if first:
        p = r
        xn_ref[...] = alpha * p
    else:
        p = r + sc_ref[:, 2:3] * p_ref[...]
        xn_ref[...] = x_ref[...] + alpha * p
    pn_ref[...] = p
    r = r - alpha * (summed(za_ref, zb_ref, rows, n) + hess * p)
    rn_ref[...] = r
    scaled = hess * r
    columns = [row_sum(r * r), row_sum(scaled * r), row_sum(scaled * p)]
    sums = pack(columns)
    if slot == 0:
        sums_ref[...] = sums

    def share(high_ref, low_ref):
        lines = to_lines(r, high_ref, low_ref)
        if slot == 0:
            out_ref[...] = lines
        else:
            store(lines + share_ref[...], None, out_ref)

    with_slot(slot, mats, share)
    if slot == 1:
        out_ref[out_ref.shape[0] - 8:, :] = sums + share_sums[...]


def weigh(flows, k, w_ref, f_ref, out_ref):
    chosen = lane_index((1, LANE)) == out_ref[k:k + 1, :]
    factors = jnp.where(chosen, -1.0, f_ref[k:k + 1, :])
    hit = jnp.sum(jnp.where(chosen, flows, 0.0), axis=1, keepdims=True)
    post = flows + factors * hit
    return post, w_ref[k:k + 1, :] * post


def lines_body(*refs, count, first, last):
    parts, refs = refs[:count], refs[count:]
    fp_ref, fx_ref, sc_ref, alpha_ref, w_ref, f_ref, out_ref = refs[:7]
    if last:
        z_ref, fpn_ref, fxn_ref, scn_ref = refs[7:]
    else:
        mats = refs[7:11]
        z_ref, pair_ref, fpn_ref, fxn_ref, scn_ref = refs[11:]
    conts = w_ref.shape[0]
    rows = parts[0].shape[0] // conts // 8 * 8

    def total(at, size):
        values = [ref[at:at + size, :] for ref in parts]
        if count == 4:
            values = [values[0], values[3], values[1], values[2]]
        while len(values) > 1:
            values = [values[i] + values[i + 1] for i in range(0, len(values), 2)]
        return values[0]

    sums = total(conts * rows, 8)
    rr, base = unpack(sums, rows, 0), unpack(sums, rows, 1)
    if not first:
        beta = rr / sc_ref[:, 0:1]
        base = base + beta * (2.0 * unpack(sums, rows, 2) + beta * sc_ref[:, 1:2])
        alpha = alpha_ref[:, 0:1]
    lane = lane_index((rows, LANE))
    packed = jnp.where(lane == 0, rr, 0.0) + jnp.where(lane == 1, base, 0.0)
    if not first:
        packed = packed + jnp.where(lane == 2, beta, 0.0)
    scn_ref[...] = packed
    curv = jnp.zeros((rows, LANE), F32)
    flat = []
    for k in range(conts):
        span = slice(k * rows, (k + 1) * rows)
        flows = total(k * rows, rows)
        if not first:
            before = fp_ref[span, :]
            fxn_ref[span, :] = fx_ref[span, :] + alpha * before
            flows = flows + beta * before
        else:
            fxn_ref[span, :] = jnp.zeros((rows, LANE), F32)
        fpn_ref[span, :] = flows
        post, weighted = weigh(flows, k, w_ref, f_ref, out_ref)
        curv = curv + post * weighted
        flat.append(flows)
    curv = pack([row_sum(curv)])
    if last:
        z_ref[...] = curv
    else:
        pair = stacked(jnp.concatenate(flat, axis=1))
        pair_ref[...] = pair
        z_ref[z_ref.shape[0] - 8:, :] = curv
        with_slot(0, mats, functools.partial(from_lines, pair, z_ref))


def image_body(pair_ref, b0, b1, b2, b3, z_ref):
    with_slot(1, (b0, b1, b2, b3), functools.partial(from_lines, pair_ref[...], z_ref))


def finish_body(ca_ref, cb_ref, r0, r1, p0, p1, x0, x1, sc_ref, fp_ref, fx_ref, w_ref, f_ref, out_ref,
                own_ref, send_ref):
    rows, n = r0.shape
    alpha = sc_ref[:, 0:1] / (unpack(ca_ref[...] + cb_ref[...], rows, 0) + sc_ref[:, 1:2])
    one, two = [x[...] + alpha * (r[...] + sc_ref[:, 2:3] * p[...]) for r, p, x in ((r0, p0, x0), (r1, p1, x1))]
    lower = core() == 0
    own_ref[:, :n] = jnp.where(lower, one, two)
    send_ref[:, :n] = jnp.where(lower, two, one)
    for k in range(w_ref.shape[0]):
        span = slice(k * rows, (k + 1) * rows)
        flows = fx_ref[span, :] + alpha * fp_ref[span, :]
        weighted = weigh(flows, k, w_ref, f_ref, out_ref)[1]
        own_ref[:, n + k * LANE:n + (k + 1) * LANE] = weighted
        send_ref[:, n + k * LANE:n + (k + 1) * LANE] = weighted


def place_body(own_ref, other_ref, part_ref, x_ref, w_ref):
    rows = own_ref.shape[0]
    n = x_ref.shape[1]
    upper = part_ref[0:1, 0:1] > 0
    for low in range(2):
        one, two = (other_ref, own_ref) if low == 0 else (own_ref, other_ref)
        value = jnp.where(upper, one[...], two[...])
        at = slice(low * rows, (low + 1) * rows)
        x_ref[at, :] = value[:, :n]
        for k in range(w_ref.shape[0]):
            w_ref[k, at, :] = value[:, n + k * LANE:n + (k + 1) * LANE]


def per_device(right_sides, base_hessian, sensitivity, weights, outage_factors, outaged, *, scen, base):
    conts, n, lines = sensitivity.shape
    rhs = right_sides.shape[0]
    rows = rhs // 2
    half = n // LANE * rows
    bits = max(scen, base).bit_length()
    spread = jnp.broadcast_to(outaged.astype(jnp.int32)[:, None], (conts, lines))

    def swap(value, *steps):
        pairs = []
        for s in range(scen):
            for b in range(base):
                along, across = steps[half_of(s, b, scen, bits) % len(steps)]
                pairs.append((s * base + b, (s ^ along) * base + (b ^ across)))
        return lax.ppermute(value, ("scen", "base"), pairs)

    def over_scen(value):
        bit = 2
        while 4 * bit < scen:
            value = value + swap(value, (bit | 1, 0))
            bit *= 2
        if 2 * bit < scen:
            one, two, both = (bit | 1, 0), (2 * bit, 0), (3 * bit | 1, 0)
            return [value, swap(value, both), swap(value, two), swap(value, one)]
        return [value, swap(value, (bit | 1, 0))]

    def over_base(values):
        order = [1 << i for i in range((base - 1).bit_length())]
        for i in range(len(order)):
            got = []
            for value in values:
                steps = [(1, order[(i + turn) % len(order)]) for turn in (0, 1)]
                got.append(swap(value, *steps))
            if i + 1 == len(order):
                return [v for both in zip(values, got) for v in both]
            values = [value + new for value, new in zip(values, got)]
            values[1:] = [lax.optimization_barrier((value, values[0]))[0] for value in values[1:]]

    part = half_of(lax.axis_index("scen"), lax.axis_index("base"), scen, bits)
    flat = struct((conts * rows, LANE))
    state = struct((rows, n))
    scal = struct((rows, LANE))
    payload = struct((conts * rows + 8, LANE))
    wide = [struct((half + 8, LANE)), struct((half, LANE))]
    share = struct((rows, conts * lines))
    pair = struct((2 * rows, conts * lines), BF16)
    block = struct((8, LANE))

    matrix = struct((n, conts * lines), BF16)
    high, low, mine, theirs, own, extra = pl.pallas_call(
        functools.partial(prepare_body, scen=scen, bits=bits),
        out_shape=[matrix, matrix, payload, payload, struct((rows, n)), struct((rows + 8, n))],
        in_specs=[pl.BlockSpec(memory_space=pltpu.HBM)] * 3,
        out_specs=[VM] * 6,
        scratch_shapes=[
            pltpu.VMEM(sensitivity.shape, F32),
            pltpu.VMEM(right_sides.shape, F32),
            pltpu.VMEM((1, n), F32),
            pltpu.SemaphoreType.DMA((conts + 2,)),
        ],
        compiler_params=PARAMS,
        name="prepare",
    )(*[pltpu.with_memory_space_constraint(v, pltpu.HBM) for v in (sensitivity, right_sides, base_hessian.reshape(1, n))])
    pay = mine + swap(theirs, (1, 0))
    held, late, pay = lax.optimization_barrier((sensitivity, extra, pay))
    other_a = swap(held, (1, 0))
    other = swap(late, (1, 0))
    lower = core() == 0

    def by_core(one, two):
        return [jnp.where(lower, one, two), jnp.where(lower, two, one)]

    r = by_core(own, other[:rows])
    hess = by_core(base_hessian[None, :], other[rows:rows + 1])
    table = (weights, outage_factors, spread)
    turned = struct((conts * lines, n), BF16)
    absorbed = pl.pallas_call(
        absorb_body,
        out_shape=[matrix, matrix, turned, turned],
        in_specs=[pl.BlockSpec(memory_space=pltpu.HBM)] + [VM] * 3,
        out_specs=[VM] * 4,
        scratch_shapes=[pltpu.VMEM(sensitivity.shape, F32), pltpu.SemaphoreType.DMA((conts,))],
        compiler_params=PARAMS,
        name="absorb",
    )(pltpu.with_memory_space_constraint(other_a, pltpu.HBM), *table)
    mats = [high, low, *absorbed[:2]]
    folded = [*fold(mats[:2], *table), *absorbed[2:]]
    p, x = list(r), list(r)
    fp = fx = jnp.zeros(flat.shape, F32)
    sc = alpha = jnp.zeros(scal.shape, F32)
    for it in range(ITERS):
        first, last = it == 0, it + 1 == ITERS
        sent = over_scen(pay)
        got = call(
            functools.partial(lines_body, count=len(sent), first=first, last=last),
            [*([block] if last else [wide[0], pair]), flat, flat, scal], "lines",
            *sent, fp, fx, sc, alpha, *table, *(() if last else folded))
        fp, fx, sc = got[-3:]
        if last:
            z = over_base(got[:1])
            break
        z = over_base([got[0], call(image_body, wide[1], "image", got[1], *folded)])
        share_lines, share_sums, r[0], p[0], x[0], alpha = call(
            functools.partial(step_body, slot=0, first=first),
            [share, block, state, state, state, scal], "step",
            *z[:2], r[0], p[0], x[0], sc, hess[0], *mats)
        pay, r[1], p[1], x[1] = call(
            functools.partial(step_body, slot=1, first=first),
            [payload, state, state, state], "step",
            *z[2:], r[1], p[1], x[1], sc, hess[1], *mats, alpha, share_lines, share_sums)
    both = struct((rows, n + conts * LANE))
    own, send = call(finish_body, [both, both], "finish", *z, *r, *p, *x, sc, fp, fx, *table)
    recv = swap(send, (1, 0))
    which = jnp.broadcast_to(part.astype(jnp.int32), (8, LANE))
    step, flow = call(place_body, [struct((rhs, n)), struct((conts, rhs, lines))], "place", own, recv, which)
    return step, flow


def solution(mesh):
    placed = (
        P(None, "scen"),
        P("scen"),
        P("base", "scen", None),
        P("base", None),
        P("base", None),
        P("base"),
    )
    body = functools.partial(per_device, scen=mesh.shape["scen"], base=mesh.shape["base"])
    return jax.shard_map(
        body,
        mesh=mesh,
        in_specs=placed,
        out_specs=(P(None, "scen"), P("base", None, None)),
        check_vma=False,
    )
```

time: 102 us -> 99 us (0.971)
  starting transfers between devices: 42.4 us -> 38.1 us
  Pallas kernels: 13.2 us -> 17.4 us
  waiting for transfers between devices: 45.4 us -> 42.3 us
    ppermute x37, starting transfers between devices: 42.4 us -> 38.1 us  [swap(): return lax.ppermute(value, ('scen', 'base'), pairs)]
    ppermute x37, waiting for transfers between devices: 45.4 us -> 42.3 us  [swap(): return lax.ppermute(value, ('scen', 'base'), pairs)]
    pallas_call x1 -> x2, Pallas kernels: 2.15 us -> 5.15 us  [the longest x1 3.01 us: per_device(): pl.pallas_call(absorb_body, out_shape=[matrix, matrix, turned, turned], i...]
    pallas_call x14 -> x20, Pallas kernels: 11.1 us -> 12.3 us  [call(): pl.pallas_call(body, out_shape=out_shape, in_specs=[VM] * len(args), out_...]
  transfers between devices with their start and end apart: 37 -> 37, of which waited for: 26 -> 26; matrix products, arithmetic and copies ran while one was open for 0% -> 0% of each run, Pallas kernels for 5% -> 9%
where the time goes in v4:
time: 99 us; the launch traced here: 98.9 us
  waiting for transfers between devices  42.3 us (43%)
  starting transfers between devices  38.1 us (38%)
  Pallas kernels  17.4 us (18%)
    ppermute x37, waiting for transfers between devices, swap(): return lax.ppermute(value, ('scen', 'base'), pairs)  42.3 us
    ppermute x37, starting transfers between devices, swap(): return lax.ppermute(value, ('scen', 'base'), pairs)  38.1 us
    pallas_call x20, Pallas kernels, call(): pl.pallas_call(body, out_shape=out_shape, in_specs=[VM] * len(args), out_...  12.3 us
    pallas_call x1, Pallas kernels, per_device(): pl.pallas_call(absorb_body, out_shape=[matrix, matrix, turned, turned], i...  3.01 us
    pallas_call x1, Pallas kernels, per_device(): pl.pallas_call(functools.partial(prepare_body, scen=scen, bits=bits), out...  2.14 us
  transfers between devices with their start and end apart: 37, of which 26 were waited for; matrix products, arithmetic and copies ran while one was open for 0% of the time, Pallas kernels for 9%

profile of v4, /device:TPU:0, one launch (start us, length us, event | category | flops | bytes accessed | tf_op | source)
XLA Modules:
  0.0 98.9 jit_solution(13569629237081308680)
XLA Ops:
  0.7 2.1 %prepare.1 = (bf16[1024,512]{1,0:T(8,128)(2,1)S(1)}, bf16[1024,512]{1,0:T(8,128)(2,1)S(1)}, f32[72,128]{1,0:T(8,128)S(1)}, f32[72,128]{1,0:T(8,128)S(1)}, f32[16...) custom-call(f32[4,1024,128]{2,1,0:T(8,128)} %a_hbm.1, f32[32,1024]{1,0:T(8,128)} %b_hbm.1, f32[1,1024]{1,0:T(1,128)} %bitcast.1), custom_call_target="tpu_custom_call" | custom-call | tf_op jit(solution)/shard_map/prepare/pallas_call | solution.py:400
  4.7 3.5 %collective-permute-start.1 = (f32[72,128]{1,0:T(8,128)S(1)}, f32[72,128]{1,0:T(8,128)S(1)}, u32[]{:S(2)}, u32[]{:S(2)}) collective-permute-start(f32[72,128]{1,0:T(8,128)S(1)} %add.51.refs_0_), channel_id=1, source_target_pairs={{0,28},{1,29},{2,30},{3,31},{4,24},{5,25},{6,26},{7,27},{8,20},{9,... | collective-permute-start | bytes 110600 | tf_op jit(solution)/shard_map/ppermute | solution.py:365
  10.0 3.0 %absorb.1 = (bf16[1024,512]{1,0:T(8,128)(2,1)S(1)}, bf16[1024,512]{1,0:T(8,128)(2,1)S(1)}, bf16[512,1024]{1,0:T(8,128)(2,1)S(1)}, bf16[512,1024]{1,0:T(8,128)(2,1)S(1)}) custom-call(f32[4,1024,128]{2,1,0:T(8,128)} %collective-permute-done.4.a_hbm, f32[4,128]{1,0:T(4,128)S(1)} %copy-done, f32[4,128]{1,0:T(4,128)S(1)} %copy-done.1, ...), custom_call_target="tpu_custom_call" | custom-call | tf_op jit(solution)/shard_map/absorb/pallas_call | solution.py:427
  13.7 1.8 %collective-permute-start.6 = (f32[136,128]{1,0:T(8,128)S(1)}, f32[136,128]{1,0:T(8,128)S(1)}, u32[]{:S(2)}, u32[]{:S(2)}) collective-permute-start(f32[136,128]{1,0:T(8,128)S(1)} %get-tuple-element.99), channel_id=1, source_target_pairs={{0,5},{1,7},{2,4},{3,6},{4,2},{5,0},{6,3},{7,1},{8,14},{9,12},{10,... | collective-permute-start | bytes 208904 | tf_op jit(solution)/shard_map/ppermute | solution.py:365
  16.0 3.7 %collective-permute-done.5 = f32[128,128]{1,0:T(8,128)S(1)} collective-permute-done((f32[128,128]{1,0:T(8,128)S(1)}, f32[128,128]{1,0:T(8,128)S(1)}, u32[]{:S(2)}, u32[]{:S(2)}) %collective-permute-start.5) | collective-permute-done | bytes 65568 | tf_op jit(solution)/shard_map/ppermute | solution.py:365
  19.7 2.6 %collective-permute-start.9 = (f32[136,128]{1,0:T(8,128)S(1)}, f32[136,128]{1,0:T(8,128)S(1)}, u32[]{:S(2)}, u32[]{:S(2)}) collective-permute-start(f32[136,128]{1,0:T(8,128)S(1)} %add.53.refs_0_), channel_id=1, source_target_pairs={{0,6},{1,4},{2,7},{3,5},{4,1},{5,3},{6,0},{7,2},{8,13},{9,15},{10,... | collective-permute-start | bytes 208904 | tf_op jit(solution)/shard_map/ppermute | solution.py:365
  22.4 2.1 %collective-permute-done.9.refs_1_ = f32[136,128]{1,0:T(8,128)S(1)} collective-permute-done((f32[136,128]{1,0:T(8,128)S(1)}, f32[136,128]{1,0:T(8,128)S(1)}, u32[]{:S(2)}, u32[]{:S(2)}) %collective-permute-start.9) | collective-permute-done | bytes 69664 | tf_op jit(solution)/shard_map/ppermute | solution.py:365
  25.2 2.4 %collective-permute-done.7.refs_1_ = f32[128,128]{1,0:T(8,128)S(1)} collective-permute-done((f32[128,128]{1,0:T(8,128)S(1)}, f32[128,128]{1,0:T(8,128)S(1)}, u32[]{:S(2)}, u32[]{:S(2)}) %collective-permute-start.7) | collective-permute-done | bytes 65568 | tf_op jit(solution)/shard_map/ppermute | solution.py:365
  28.2 2.1 %collective-permute-start.10 = (f32[72,128]{1,0:T(8,128)S(1)}, f32[72,128]{1,0:T(8,128)S(1)}, u32[]{:S(2)}, u32[]{:S(2)}) collective-permute-start(f32[72,128]{1,0:T(8,128)S(1)} %get-tuple-element.109.refs_0_), channel_id=1, source_target_pairs={{0,28},{1,29},{2,30},{3,31},{4,24},{5,25},{6,26},{7,27},{8,20},{9,... | collective-permute-start | bytes 110600 | tf_op jit(solution)/shard_map/ppermute | solution.py:365
  31.2 1.7 %collective-permute-done.10.refs_1_ = f32[72,128]{1,0:T(8,128)S(1)} collective-permute-done((f32[72,128]{1,0:T(8,128)S(1)}, f32[72,128]{1,0:T(8,128)S(1)}, u32[]{:S(2)}, u32[]{:S(2)}) %collective-permute-start.10) | collective-permute-done | bytes 36896 | tf_op jit(solution)/shard_map/ppermute | solution.py:365
  37.4 2.3 %collective-permute-done.14 = f32[136,128]{1,0:T(8,128)S(1)} collective-permute-done((f32[136,128]{1,0:T(8,128)S(1)}, f32[136,128]{1,0:T(8,128)S(1)}, u32[]{:S(2)}, u32[]{:S(2)}) %collective-permute-start.14) | collective-permute-done | bytes 69664 | tf_op jit(solution)/shard_map/ppermute | solution.py:365
  42.5 2.3 %collective-permute-done.16.refs_1_ = f32[136,128]{1,0:T(8,128)S(1)} collective-permute-done((f32[136,128]{1,0:T(8,128)S(1)}, f32[136,128]{1,0:T(8,128)S(1)}, u32[]{:S(2)}, u32[]{:S(2)}) %collective-permute-start.16) | collective-permute-done | bytes 69664 | tf_op jit(solution)/shard_map/ppermute | solution.py:365
  48.5 1.6 %collective-permute-start.19 = (f32[72,128]{1,0:T(8,128)S(1)}, f32[72,128]{1,0:T(8,128)S(1)}, u32[]{:S(2)}, u32[]{:S(2)}) collective-permute-start(f32[72,128]{1,0:T(8,128)S(1)} %get-tuple-element.125.refs_0_), channel_id=1, source_target_pairs={{0,12},{1,13},{2,14},{3,15},{4,8},{5,9},{6,10},{7,11},{8,4},{9,5},... | collective-permute-start | bytes 110600 | tf_op jit(solution)/shard_map/ppermute | solution.py:365
  50.1 1.7 %collective-permute-done.17.refs_1_ = f32[72,128]{1,0:T(8,128)S(1)} collective-permute-done((f32[72,128]{1,0:T(8,128)S(1)}, f32[72,128]{1,0:T(8,128)S(1)}, u32[]{:S(2)}, u32[]{:S(2)}) %collective-permute-start.17) | collective-permute-done | bytes 36896 | tf_op jit(solution)/shard_map/ppermute | solution.py:365
  56.9 1.8 %collective-permute-start.23 = (f32[136,128]{1,0:T(8,128)S(1)}, f32[136,128]{1,0:T(8,128)S(1)}, u32[]{:S(2)}, u32[]{:S(2)}) collective-permute-start(f32[136,128]{1,0:T(8,128)S(1)} %add.57.refs_0_), channel_id=1, source_target_pairs={{0,6},{1,4},{2,7},{3,5},{4,1},{5,3},{6,0},{7,2},{8,13},{9,15},{10,... | collective-permute-start | bytes 208904 | tf_op jit(solution)/shard_map/ppermute | solution.py:365
  58.7 2.0 %collective-permute-start.22 = (f32[128,128]{1,0:T(8,128)S(1)}, f32[128,128]{1,0:T(8,128)S(1)}, u32[]{:S(2)}, u32[]{:S(2)}) collective-permute-start(f32[128,128]{1,0:T(8,128)S(1)} %add.56.refs_0_), channel_id=1, source_target_pairs={{0,6},{1,4},{2,7},{3,5},{4,1},{5,3},{6,0},{7,2},{8,13},{9,15},{10,... | collective-permute-start | bytes 196616 | tf_op jit(solution)/shard_map/ppermute | solution.py:365
  62.3 1.8 %collective-permute-done.22.refs_1_ = f32[128,128]{1,0:T(8,128)S(1)} collective-permute-done((f32[128,128]{1,0:T(8,128)S(1)}, f32[128,128]{1,0:T(8,128)S(1)}, u32[]{:S(2)}, u32[]{:S(2)}) %collective-permute-start.22) | collective-permute-done | bytes 65568 | tf_op jit(solution)/shard_map/ppermute | solution.py:365
  64.7 1.9 %collective-permute-start.24 = (f32[72,128]{1,0:T(8,128)S(1)}, f32[72,128]{1,0:T(8,128)S(1)}, u32[]{:S(2)}, u32[]{:S(2)}) collective-permute-start(f32[72,128]{1,0:T(8,128)S(1)} %get-tuple-element.141.refs_0_), channel_id=1, source_target_pairs={{0,28},{1,29},{2,30},{3,31},{4,24},{5,25},{6,26},{7,27},{8,20},{9,... | collective-permute-start | bytes 110600 | tf_op jit(solution)/shard_map/ppermute | solution.py:365
  74.2 2.3 %collective-permute-done.28 = f32[136,128]{1,0:T(8,128)S(1)} collective-permute-done((f32[136,128]{1,0:T(8,128)S(1)}, f32[136,128]{1,0:T(8,128)S(1)}, u32[]{:S(2)}, u32[]{:S(2)}) %collective-permute-start.28) | collective-permute-done | bytes 69664 | tf_op jit(solution)/shard_map/ppermute | solution.py:365
  77.2 2.1 %collective-permute-start.29 = (f32[128,128]{1,0:T(8,128)S(1)}, f32[128,128]{1,0:T(8,128)S(1)}, u32[]{:S(2)}, u32[]{:S(2)}) collective-permute-start(f32[128,128]{1,0:T(8,128)S(1)} %add.58.refs_0_), channel_id=1, source_target_pairs={{0,6},{1,4},{2,7},{3,5},{4,1},{5,3},{6,0},{7,2},{8,13},{9,15},{10,... | collective-permute-start | bytes 196616 | tf_op jit(solution)/shard_map/ppermute | solution.py:365
  79.2 1.9 %collective-permute-done.30.refs_1_ = f32[136,128]{1,0:T(8,128)S(1)} collective-permute-done((f32[136,128]{1,0:T(8,128)S(1)}, f32[136,128]{1,0:T(8,128)S(1)}, u32[]{:S(2)}, u32[]{:S(2)}) %collective-permute-start.30) | collective-permute-done | bytes 69664 | tf_op jit(solution)/shard_map/ppermute | solution.py:365
  83.6 1.8 %collective-permute-start.32 = (f32[72,128]{1,0:T(8,128)S(1)}, f32[72,128]{1,0:T(8,128)S(1)}, u32[]{:S(2)}, u32[]{:S(2)}) collective-permute-start(f32[72,128]{1,0:T(8,128)S(1)} %get-tuple-element.157.refs_0_), channel_id=1, source_target_pairs={{0,16},{1,17},{2,18},{3,19},{4,20},{5,21},{6,22},{7,23},{8,24},{9,... | collective-permute-start | bytes 110600 | tf_op jit(solution)/shard_map/ppermute | solution.py:365
  90.2 2.4 %collective-permute-done.34 = f32[8,128]{1,0:T(8,128)S(1)} collective-permute-done((f32[8,128]{1,0:T(8,128)S(1)}, f32[8,128]{1,0:T(8,128)S(1)}, u32[]{:S(2)}, u32[]{:S(2)}) %collective-permute-start.34) | collective-permute-done | bytes 4128 | tf_op jit(solution)/shard_map/ppermute | solution.py:365
  93.5 3.0 %collective-permute-done.35.cb_ref = f32[8,128]{1,0:T(8,128)S(1)} collective-permute-done((f32[8,128]{1,0:T(8,128)S(1)}, f32[8,128]{1,0:T(8,128)S(1)}, u32[]{:S(2)}, u32[]{:S(2)}) %collective-permute-start.35) | collective-permute-done | bytes 4128 | tf_op jit(solution)/shard_map/ppermute | solution.py:365
  (96 shorter events, 44.0 us)
Async XLA Ops:
  4.2 5.7 %collective-permute-start.4 = (f32[4,1024,128]{2,1,0:T(8,128)}, f32[4,1024,128]{2,1,0:T(8,128)}, u32[]{:S(2)}, u32[]{:S(2)}) collective-permute-start(f32[4,1024,128]{2,1,0:T(8,128)} %a_hbm.1), channel_id=1, source_target_pairs={{0,4},{1,5},{2,6},{3,7},{4,0},{5,1},{6,2},{7,3},{8,12},{9,13},{10,... | collective-permute-start | bytes 6291464 | tf_op jit(solution)/shard_map/ppermute | solution.py:365
  4.6 11.4 %collective-permute-start.8 = (f32[24,1024]{1,0:T(8,128)S(1)}, f32[24,1024]{1,0:T(8,128)S(1)}, u32[]{:S(2)}, u32[]{:S(2)}) collective-permute-start(f32[24,1024]{1,0:T(8,128)S(1)} %get-tuple-element.101), channel_id=1, source_target_pairs={{0,4},{1,5},{2,6},{3,7},{4,0},{5,1},{6,2},{7,3},{8,12},{9,13},{10,... | collective-permute-start | bytes 294920 | tf_op jit(solution)/shard_map/ppermute | solution.py:365
  4.7 8.2 %collective-permute-start.1 = (f32[72,128]{1,0:T(8,128)S(1)}, f32[72,128]{1,0:T(8,128)S(1)}, u32[]{:S(2)}, u32[]{:S(2)}) collective-permute-start(f32[72,128]{1,0:T(8,128)S(1)} %add.51.refs_0_), channel_id=1, source_target_pairs={{0,28},{1,29},{2,30},{3,31},{4,24},{5,25},{6,26},{7,27},{8,20},{9,... | collective-permute-start | bytes 110600 | tf_op jit(solution)/shard_map/ppermute | solution.py:365
  8.3 4.7 %collective-permute-start.2 = (f32[72,128]{1,0:T(8,128)S(1)}, f32[72,128]{1,0:T(8,128)S(1)}, u32[]{:S(2)}, u32[]{:S(2)}) collective-permute-start(f32[72,128]{1,0:T(8,128)S(1)} %add.51.refs_0_), channel_id=1, source_target_pairs={{0,16},{1,17},{2,18},{3,19},{4,20},{5,21},{6,22},{7,23},{8,24},{9,... | collective-permute-start | bytes 110600 | tf_op jit(solution)/shard_map/ppermute | solution.py:365
  13.7 6.0 %collective-permute-start.6 = (f32[136,128]{1,0:T(8,128)S(1)}, f32[136,128]{1,0:T(8,128)S(1)}, u32[]{:S(2)}, u32[]{:S(2)}) collective-permute-start(f32[136,128]{1,0:T(8,128)S(1)} %get-tuple-element.99), channel_id=1, source_target_pairs={{0,5},{1,7},{2,4},{3,6},{4,2},{5,0},{6,3},{7,1},{8,14},{9,12},{10,... | collective-permute-start | bytes 208904 | tf_op jit(solution)/shard_map/ppermute | solution.py:365
  19.7 4.8 %collective-permute-start.9 = (f32[136,128]{1,0:T(8,128)S(1)}, f32[136,128]{1,0:T(8,128)S(1)}, u32[]{:S(2)}, u32[]{:S(2)}) collective-permute-start(f32[136,128]{1,0:T(8,128)S(1)} %add.53.refs_0_), channel_id=1, source_target_pairs={{0,6},{1,4},{2,7},{3,5},{4,1},{5,3},{6,0},{7,2},{8,13},{9,15},{10,... | collective-permute-start | bytes 208904 | tf_op jit(solution)/shard_map/ppermute | solution.py:365
  22.3 5.3 %collective-permute-start.7 = (f32[128,128]{1,0:T(8,128)S(1)}, f32[128,128]{1,0:T(8,128)S(1)}, u32[]{:S(2)}, u32[]{:S(2)}) collective-permute-start(f32[128,128]{1,0:T(8,128)S(1)} %add.52.refs_0_), channel_id=1, source_target_pairs={{0,6},{1,4},{2,7},{3,5},{4,1},{5,3},{6,0},{7,2},{8,13},{9,15},{10,... | collective-permute-start | bytes 196616 | tf_op jit(solution)/shard_map/ppermute | solution.py:365
  28.2 4.7 %collective-permute-start.10 = (f32[72,128]{1,0:T(8,128)S(1)}, f32[72,128]{1,0:T(8,128)S(1)}, u32[]{:S(2)}, u32[]{:S(2)}) collective-permute-start(f32[72,128]{1,0:T(8,128)S(1)} %get-tuple-element.109.refs_0_), channel_id=1, source_target_pairs={{0,28},{1,29},{2,30},{3,31},{4,24},{5,25},{6,26},{7,27},{8,20},{9,... | collective-permute-start | bytes 110600 | tf_op jit(solution)/shard_map/ppermute | solution.py:365
  35.2 4.5 %collective-permute-start.14 = (f32[136,128]{1,0:T(8,128)S(1)}, f32[136,128]{1,0:T(8,128)S(1)}, u32[]{:S(2)}, u32[]{:S(2)}) collective-permute-start(f32[136,128]{1,0:T(8,128)S(1)} %get-tuple-element.113), channel_id=1, source_target_pairs={{0,5},{1,7},{2,4},{3,6},{4,2},{5,0},{6,3},{7,1},{8,14},{9,12},{10,... | collective-permute-start | bytes 208904 | tf_op jit(solution)/shard_map/ppermute | solution.py:365
  35.9 5.0 %collective-permute-start.13 = (f32[128,128]{1,0:T(8,128)S(1)}, f32[128,128]{1,0:T(8,128)S(1)}, u32[]{:S(2)}, u32[]{:S(2)}) collective-permute-start(f32[128,128]{1,0:T(8,128)S(1)} %image.5), channel_id=1, source_target_pairs={{0,5},{1,7},{2,4},{3,6},{4,2},{5,0},{6,3},{7,1},{8,14},{9,12},{10,... | collective-permute-start | bytes 196616 | tf_op jit(solution)/shard_map/ppermute | solution.py:365
  39.7 5.1 %collective-permute-start.16 = (f32[136,128]{1,0:T(8,128)S(1)}, f32[136,128]{1,0:T(8,128)S(1)}, u32[]{:S(2)}, u32[]{:S(2)}) collective-permute-start(f32[136,128]{1,0:T(8,128)S(1)} %add.55.refs_0_), channel_id=1, source_target_pairs={{0,6},{1,4},{2,7},{3,5},{4,1},{5,3},{6,0},{7,2},{8,13},{9,15},{10,... | collective-permute-start | bytes 208904 | tf_op jit(solution)/shard_map/ppermute | solution.py:365
  41.0 5.6 %collective-permute-start.15 = (f32[128,128]{1,0:T(8,128)S(1)}, f32[128,128]{1,0:T(8,128)S(1)}, u32[]{:S(2)}, u32[]{:S(2)}) collective-permute-start(f32[128,128]{1,0:T(8,128)S(1)} %add.54.refs_0_), channel_id=1, source_target_pairs={{0,6},{1,4},{2,7},{3,5},{4,1},{5,3},{6,0},{7,2},{8,13},{9,15},{10,... | collective-permute-start | bytes 196616 | tf_op jit(solution)/shard_map/ppermute | solution.py:365
  47.2 4.6 %collective-permute-start.17 = (f32[72,128]{1,0:T(8,128)S(1)}, f32[72,128]{1,0:T(8,128)S(1)}, u32[]{:S(2)}, u32[]{:S(2)}) collective-permute-start(f32[72,128]{1,0:T(8,128)S(1)} %get-tuple-element.125.refs_0_), channel_id=1, source_target_pairs={{0,28},{1,29},{2,30},{3,31},{4,24},{5,25},{6,26},{7,27},{8,20},{9,... | collective-permute-start | bytes 110600 | tf_op jit(solution)/shard_map/ppermute | solution.py:365
  47.2 5.2 %collective-permute-start.18 = (f32[72,128]{1,0:T(8,128)S(1)}, f32[72,128]{1,0:T(8,128)S(1)}, u32[]{:S(2)}, u32[]{:S(2)}) collective-permute-start(f32[72,128]{1,0:T(8,128)S(1)} %get-tuple-element.125.refs_0_), channel_id=1, source_target_pairs={{0,16},{1,17},{2,18},{3,19},{4,20},{5,21},{6,22},{7,23},{8,24},{9,... | collective-permute-start | bytes 110600 | tf_op jit(solution)/shard_map/ppermute | solution.py:365
  54.2 4.5 %collective-permute-start.20 = (f32[128,128]{1,0:T(8,128)S(1)}, f32[128,128]{1,0:T(8,128)S(1)}, u32[]{:S(2)}, u32[]{:S(2)}) collective-permute-start(f32[128,128]{1,0:T(8,128)S(1)} %image.6), channel_id=1, source_target_pairs={{0,5},{1,7},{2,4},{3,6},{4,2},{5,0},{6,3},{7,1},{8,14},{9,12},{10,... | collective-permute-start | bytes 196616 | tf_op jit(solution)/shard_map/ppermute | solution.py:365
  56.9 4.7 %collective-permute-start.23 = (f32[136,128]{1,0:T(8,128)S(1)}, f32[136,128]{1,0:T(8,128)S(1)}, u32[]{:S(2)}, u32[]{:S(2)}) collective-permute-start(f32[136,128]{1,0:T(8,128)S(1)} %add.57.refs_0_), channel_id=1, source_target_pairs={{0,6},{1,4},{2,7},{3,5},{4,1},{5,3},{6,0},{7,2},{8,13},{9,15},{10,... | collective-permute-start | bytes 208904 | tf_op jit(solution)/shard_map/ppermute | solution.py:365
  58.7 5.4 %collective-permute-start.22 = (f32[128,128]{1,0:T(8,128)S(1)}, f32[128,128]{1,0:T(8,128)S(1)}, u32[]{:S(2)}, u32[]{:S(2)}) collective-permute-start(f32[128,128]{1,0:T(8,128)S(1)} %add.56.refs_0_), channel_id=1, source_target_pairs={{0,6},{1,4},{2,7},{3,5},{4,1},{5,3},{6,0},{7,2},{8,13},{9,15},{10,... | collective-permute-start | bytes 196616 | tf_op jit(solution)/shard_map/ppermute | solution.py:365
  64.7 4.4 %collective-permute-start.24 = (f32[72,128]{1,0:T(8,128)S(1)}, f32[72,128]{1,0:T(8,128)S(1)}, u32[]{:S(2)}, u32[]{:S(2)}) collective-permute-start(f32[72,128]{1,0:T(8,128)S(1)} %get-tuple-element.141.refs_0_), channel_id=1, source_target_pairs={{0,28},{1,29},{2,30},{3,31},{4,24},{5,25},{6,26},{7,27},{8,20},{9,... | collective-permute-start | bytes 110600 | tf_op jit(solution)/shard_map/ppermute | solution.py:365
  72.0 4.5 %collective-permute-start.28 = (f32[136,128]{1,0:T(8,128)S(1)}, f32[136,128]{1,0:T(8,128)S(1)}, u32[]{:S(2)}, u32[]{:S(2)}) collective-permute-start(f32[136,128]{1,0:T(8,128)S(1)} %get-tuple-element.145), channel_id=1, source_target_pairs={{0,5},{1,7},{2,4},{3,6},{4,2},{5,0},{6,3},{7,1},{8,14},{9,12},{10,... | collective-permute-start | bytes 208904 | tf_op jit(solution)/shard_map/ppermute | solution.py:365
  72.9 4.2 %collective-permute-start.27 = (f32[128,128]{1,0:T(8,128)S(1)}, f32[128,128]{1,0:T(8,128)S(1)}, u32[]{:S(2)}, u32[]{:S(2)}) collective-permute-start(f32[128,128]{1,0:T(8,128)S(1)} %image.7), channel_id=1, source_target_pairs={{0,5},{1,7},{2,4},{3,6},{4,2},{5,0},{6,3},{7,1},{8,14},{9,12},{10,... | collective-permute-start | bytes 196616 | tf_op jit(solution)/shard_map/ppermute | solution.py:365
  76.5 4.7 %collective-permute-start.30 = (f32[136,128]{1,0:T(8,128)S(1)}, f32[136,128]{1,0:T(8,128)S(1)}, u32[]{:S(2)}, u32[]{:S(2)}) collective-permute-start(f32[136,128]{1,0:T(8,128)S(1)} %add.59.refs_0_), channel_id=1, source_target_pairs={{0,6},{1,4},{2,7},{3,5},{4,1},{5,3},{6,0},{7,2},{8,13},{9,15},{10,... | collective-permute-start | bytes 208904 | tf_op jit(solution)/shard_map/ppermute | solution.py:365
  77.2 5.5 %collective-permute-start.29 = (f32[128,128]{1,0:T(8,128)S(1)}, f32[128,128]{1,0:T(8,128)S(1)}, u32[]{:S(2)}, u32[]{:S(2)}) collective-permute-start(f32[128,128]{1,0:T(8,128)S(1)} %add.58.refs_0_), channel_id=1, source_target_pairs={{0,6},{1,4},{2,7},{3,5},{4,1},{5,3},{6,0},{7,2},{8,13},{9,15},{10,... | collective-permute-start | bytes 196616 | tf_op jit(solution)/shard_map/ppermute | solution.py:365
  83.3 4.3 %collective-permute-start.31 = (f32[72,128]{1,0:T(8,128)S(1)}, f32[72,128]{1,0:T(8,128)S(1)}, u32[]{:S(2)}, u32[]{:S(2)}) collective-permute-start(f32[72,128]{1,0:T(8,128)S(1)} %get-tuple-element.157.refs_0_), channel_id=1, source_target_pairs={{0,28},{1,29},{2,30},{3,31},{4,24},{5,25},{6,26},{7,27},{8,20},{9,... | collective-permute-start | bytes 110600 | tf_op jit(solution)/shard_map/ppermute | solution.py:365
  83.6 5.1 %collective-permute-start.32 = (f32[72,128]{1,0:T(8,128)S(1)}, f32[72,128]{1,0:T(8,128)S(1)}, u32[]{:S(2)}, u32[]{:S(2)}) collective-permute-start(f32[72,128]{1,0:T(8,128)S(1)} %get-tuple-element.157.refs_0_), channel_id=1, source_target_pairs={{0,16},{1,17},{2,18},{3,19},{4,20},{5,21},{6,22},{7,23},{8,24},{9,... | collective-permute-start | bytes 110600 | tf_op jit(solution)/shard_map/ppermute | solution.py:365
  (17 other events, 75.3 us)

commit v5 on v4

--- a/solution.py
+++ b/solution.py
@@ -135,10 +135,13 @@
     low_ref[:, k * LANE:(k + 1) * LANE] = low
 
 
-def absorb_body(a_hbm, w_ref, f_ref, out_ref, high_ref, low_ref, bh_ref, bl_ref, held_ref, sems):
+def absorb_body(a_hbm, own_high, own_low, w_ref, f_ref, out_ref, oh_ref, ol_ref,
+                high_ref, low_ref, bh_ref, bl_ref, held_ref, sems):
     copies = reads(a_hbm, held_ref, sems)
     for copy in copies:
         copy.start()
+    for k in range(len(copies)):
+        fold_one(k, own_high, own_low, w_ref, f_ref, out_ref, oh_ref, ol_ref)
     for k, copy in enumerate(copies):
         copy.wait()
         convert_one(k, held_ref, high_ref, low_ref)
@@ -211,8 +214,11 @@
 
 
 def step_body(*refs, slot, first):
-    za_ref, zb_ref, r_ref, p_ref, x_ref, sc_ref, hess_ref = refs[:7]
-    mats, refs = refs[7:11], refs[11:]
+    with_slot(slot, refs[7:11], functools.partial(step_work, refs[:7], refs[11:], slot, first))
+
+
+def step_work(ins, refs, slot, first, high_ref, low_ref):
+    za_ref, zb_ref, r_ref, p_ref, x_ref, sc_ref, hess_ref = ins
     rows, n = r_ref.shape
     r = r_ref[...]
     hess = hess_ref[...]
@@ -237,18 +243,12 @@
     scaled = hess * r
     columns = [row_sum(r * r), row_sum(scaled * r), row_sum(scaled * p)]
     sums = pack(columns)
+    lines = to_lines(r, high_ref, low_ref)
     if slot == 0:
         sums_ref[...] = sums
-
-    def share(high_ref, low_ref):
-        lines = to_lines(r, high_ref, low_ref)
-        if slot == 0:
-            out_ref[...] = lines
-        else:
-            store(lines + share_ref[...], None, out_ref)
-
-    with_slot(slot, mats, share)
-    if slot == 1:
+        out_ref[...] = lines
+    else:
+        store(lines + share_ref[...], None, out_ref)
         out_ref[out_ref.shape[0] - 8:, :] = sums + share_sums[...]
 
 
@@ -260,24 +260,33 @@
     return post, w_ref[k:k + 1, :] * post
 
 
+def tree(refs, span):
+    values = [ref[span, :] for ref in refs]
+    if len(values) == 4:
+        return (values[0] + values[3]) + (values[1] + values[2])
+    return values[0] + values[1]
+
+
 def lines_body(*refs, count, first, last):
     parts, refs = refs[:count], refs[count:]
-    fp_ref, fx_ref, sc_ref, alpha_ref, w_ref, f_ref, out_ref = refs[:7]
     if last:
-        z_ref, fpn_ref, fxn_ref, scn_ref = refs[7:]
-    else:
-        mats = refs[7:11]
-        z_ref, pair_ref, fpn_ref, fxn_ref, scn_ref = refs[11:]
+        lines_work(parts, refs[:7], refs[7:], first)
+    else:
+        with_slot(0, refs[7:11], functools.partial(lines_work, parts, refs[:7], refs[11:], first))
+
+
+def lines_work(parts, ins, outs, first, *mats):
+    fp_ref, fx_ref, sc_ref, alpha_ref, w_ref, f_ref, out_ref = ins
+    last = not mats
+    if last:
+        z_ref, fpn_ref, fxn_ref, scn_ref = outs
+    else:
+        z_ref, pair_ref, fpn_ref, fxn_ref, scn_ref = outs
     conts = w_ref.shape[0]
     rows = parts[0].shape[0] // conts // 8 * 8
 
     def total(at, size):
-        values = [ref[at:at + size, :] for ref in parts]
-        if count == 4:
-            values = [values[0], values[3], values[1], values[2]]
-        while len(values) > 1:
-            values = [values[i] + values[i + 1] for i in range(0, len(values), 2)]
-        return values[0]
+        return tree(parts, slice(at, at + size))
 
     sums = total(conts * rows, 8)
     rr, base = unpack(sums, rows, 0), unpack(sums, rows, 1)
@@ -312,17 +321,18 @@
         pair = stacked(jnp.concatenate(flat, axis=1))
         pair_ref[...] = pair
         z_ref[z_ref.shape[0] - 8:, :] = curv
-        with_slot(0, mats, functools.partial(from_lines, pair, z_ref))
+        from_lines(pair, z_ref, *mats)
 
 
 def image_body(pair_ref, b0, b1, b2, b3, z_ref):
     with_slot(1, (b0, b1, b2, b3), functools.partial(from_lines, pair_ref[...], z_ref))
 
 
-def finish_body(ca_ref, cb_ref, r0, r1, p0, p1, x0, x1, sc_ref, fp_ref, fx_ref, w_ref, f_ref, out_ref,
-                own_ref, send_ref):
+def finish_body(*refs, count):
+    parts, refs = refs[:count], refs[count:]
+    r0, r1, p0, p1, x0, x1, sc_ref, fp_ref, fx_ref, w_ref, f_ref, out_ref, own_ref, send_ref = refs
     rows, n = r0.shape
-    alpha = sc_ref[:, 0:1] / (unpack(ca_ref[...] + cb_ref[...], rows, 0) + sc_ref[:, 1:2])
+    alpha = sc_ref[:, 0:1] / (unpack(tree(parts, slice(None)), rows, 0) + sc_ref[:, 1:2])
     one, two = [x[...] + alpha * (r[...] + sc_ref[:, 2:3] * p[...]) for r, p, x in ((r0, p0, x0), (r1, p1, x1))]
     lower = core() == 0
     own_ref[:, :n] = jnp.where(lower, one, two)
@@ -376,6 +386,9 @@
 
     def over_base(values):
         order = [1 << i for i in range((base - 1).bit_length())]
+        if len(values) == 1 and len(order) == 2:
+            value, = values
+            return [value, swap(value, (0, 3)), swap(value, (1, 2)), swap(value, (1, 1))]
         for i in range(len(order)):
             got = []
             for value in values:
@@ -426,15 +439,15 @@
     turned = struct((conts * lines, n), BF16)
     absorbed = pl.pallas_call(
         absorb_body,
-        out_shape=[matrix, matrix, turned, turned],
-        in_specs=[pl.BlockSpec(memory_space=pltpu.HBM)] + [VM] * 3,
-        out_specs=[VM] * 4,
+        out_shape=[turned, turned, matrix, matrix, turned, turned],
+        in_specs=[pl.BlockSpec(memory_space=pltpu.HBM)] + [VM] * 5,
+        out_specs=[VM] * 6,
         scratch_shapes=[pltpu.VMEM(sensitivity.shape, F32), pltpu.SemaphoreType.DMA((conts,))],
         compiler_params=PARAMS,
         name="absorb",
-    )(pltpu.with_memory_space_constraint(other_a, pltpu.HBM), *table)
-    mats = [high, low, *absorbed[:2]]
-    folded = [*fold(mats[:2], *table), *absorbed[2:]]
+    )(pltpu.with_memory_space_constraint(other_a, pltpu.HBM), high, low, *table)
+    mats = [high, low, *absorbed[2:4]]
+    folded = [*absorbed[:2], *absorbed[4:]]
     p, x = list(r), list(r)
     fp = fx = jnp.zeros(flat.shape, F32)
     sc = alpha = jnp.zeros(scal.shape, F32)
@@ -459,7 +472,7 @@
             [payload, state, state, state], "step",
             *z[2:], r[1], p[1], x[1], sc, hess[1], *mats, alpha, share_lines, share_sums)
     both = struct((rows, n + conts * LANE))
-    own, send = call(finish_body, [both, both], "finish", *z, *r, *p, *x, sc, fp, fx, *table)
+    own, send = call(functools.partial(finish_body, count=len(z)), [both, both], "finish", *z, *r, *p, *x, sc, fp, fx, *table)
     recv = swap(send, (1, 0))
     which = jnp.broadcast_to(part.astype(jnp.int32), (8, LANE))
     step, flow = call(place_body, [struct((rhs, n)), struct((conts, rhs, lines))], "place", own, recv, which)

time: 99 us -> 96.6 us (0.976)
  starting transfers between devices: 38.1 us -> 42.9 us
  waiting for transfers between devices: 42.3 us -> 37.7 us
  Pallas kernels: 17.4 us -> 14.7 us
    ppermute x37 -> x38, starting transfers between devices: 38.1 us -> 42.9 us  [swap(): return lax.ppermute(value, ('scen', 'base'), pairs)]
    ppermute x37 -> x38, waiting for transfers between devices: 42.3 us -> 37.7 us  [swap(): return lax.ppermute(value, ('scen', 'base'), pairs)]
    pallas_call x20 -> x19, Pallas kernels: 12.3 us -> 9.54 us  [call(): pl.pallas_call(body, out_shape=out_shape, in_specs=[VM] * len(args), out_...]
  transfers between devices with their start and end apart: 37 -> 38, of which waited for: 26 -> 28; matrix products, arithmetic and copies ran while one was open for 0% -> 0% of each run, Pallas kernels for 9% -> 8%
where the time goes in v5:
time: 96.6 us; the launch traced here: 96.4 us
  starting transfers between devices  42.9 us (44%)
  waiting for transfers between devices  37.7 us (39%)
  Pallas kernels  14.7 us (15%)
    ppermute x38, starting transfers between devices, swap(): return lax.ppermute(value, ('scen', 'base'), pairs)  42.9 us
    ppermute x38, waiting for transfers between devices, swap(): return lax.ppermute(value, ('scen', 'base'), pairs)  37.7 us
    pallas_call x19, Pallas kernels, call(): pl.pallas_call(body, out_shape=out_shape, in_specs=[VM] * len(args), out_...  9.54 us
    pallas_call x1, Pallas kernels, per_device(): pl.pallas_call(absorb_body, out_shape=[turned, turned, matrix, matrix, tu...  3.03 us
    pallas_call x1, Pallas kernels, per_device(): pl.pallas_call(functools.partial(prepare_body, scen=scen, bits=bits), out...  2.14 us
  transfers between devices with their start and end apart: 38, of which 28 were waited for; matrix products, arithmetic and copies ran while one was open for 0% of the time, Pallas kernels for 8%

profile of v5, /device:TPU:0, one launch (start us, length us, event | category | flops | bytes accessed | tf_op | source)
XLA Modules:
  0.0 96.4 jit_solution(13499651945365230354)
XLA Ops:
  0.7 2.1 %prepare.1 = (bf16[1024,512]{1,0:T(8,128)(2,1)S(1)}, bf16[1024,512]{1,0:T(8,128)(2,1)S(1)}, f32[72,128]{1,0:T(8,128)S(1)}, f32[72,128]{1,0:T(8,128)S(1)}, f32[16...) custom-call(f32[4,1024,128]{2,1,0:T(8,128)} %a_hbm.1, f32[32,1024]{1,0:T(8,128)} %b_hbm.1, f32[1,1024]{1,0:T(1,128)} %bitcast.1), custom_call_target="tpu_custom_call" | custom-call | tf_op jit(solution)/shard_map/prepare/pallas_call | solution.py:413
  4.7 3.5 %collective-permute-start.1 = (f32[72,128]{1,0:T(8,128)S(1)}, f32[72,128]{1,0:T(8,128)S(1)}, u32[]{:S(2)}, u32[]{:S(2)}) collective-permute-start(f32[72,128]{1,0:T(8,128)S(1)} %add.48.refs_0_), channel_id=1, source_target_pairs={{0,28},{1,29},{2,30},{3,31},{4,24},{5,25},{6,26},{7,27},{8,20},{9,... | collective-permute-start | bytes 110600 | tf_op jit(solution)/shard_map/ppermute | solution.py:375
  8.9 3.0 %absorb.1 = (bf16[512,1024]{1,0:T(8,128)(2,1)S(1)}, bf16[512,1024]{1,0:T(8,128)(2,1)S(1)}, bf16[1024,512]{1,0:T(8,128)(2,1)S(1)}, bf16[1024,512]{1,0:T(8,128)(2,...) custom-call(f32[4,1024,128]{2,1,0:T(8,128)} %collective-permute-done.4.a_hbm, ...), custom_call_target="tpu_custom_call" | custom-call | tf_op jit(solution)/shard_map/absorb/pallas_call | solution.py:440
  12.8 2.3 %collective-permute-start.6 = (f32[136,128]{1,0:T(8,128)S(1)}, f32[136,128]{1,0:T(8,128)S(1)}, u32[]{:S(2)}, u32[]{:S(2)}) collective-permute-start(f32[136,128]{1,0:T(8,128)S(1)} %get-tuple-element.99), channel_id=1, source_target_pairs={{0,5},{1,7},{2,4},{3,6},{4,2},{5,0},{6,3},{7,1},{8,14},{9,12},{10,... | collective-permute-start | bytes 208904 | tf_op jit(solution)/shard_map/ppermute | solution.py:375
  15.5 3.8 %collective-permute-done.5 = f32[128,128]{1,0:T(8,128)S(1)} collective-permute-done((f32[128,128]{1,0:T(8,128)S(1)}, f32[128,128]{1,0:T(8,128)S(1)}, u32[]{:S(2)}, u32[]{:S(2)}) %collective-permute-start.5) | collective-permute-done | bytes 65568 | tf_op jit(solution)/shard_map/ppermute | solution.py:375
  19.3 2.9 %collective-permute-start.9 = (f32[136,128]{1,0:T(8,128)S(1)}, f32[136,128]{1,0:T(8,128)S(1)}, u32[]{:S(2)}, u32[]{:S(2)}) collective-permute-start(f32[136,128]{1,0:T(8,128)S(1)} %add.50.refs_0_), channel_id=1, source_target_pairs={{0,6},{1,4},{2,7},{3,5},{4,1},{5,3},{6,0},{7,2},{8,13},{9,15},{10,... | collective-permute-start | bytes 208904 | tf_op jit(solution)/shard_map/ppermute | solution.py:375
  22.3 2.2 %collective-permute-done.9.refs_1_ = f32[136,128]{1,0:T(8,128)S(1)} collective-permute-done((f32[136,128]{1,0:T(8,128)S(1)}, f32[136,128]{1,0:T(8,128)S(1)}, u32[]{:S(2)}, u32[]{:S(2)}) %collective-permute-start.9) | collective-permute-done | bytes 69664 | tf_op jit(solution)/shard_map/ppermute | solution.py:375
  25.1 2.5 %collective-permute-done.7.refs_1_ = f32[128,128]{1,0:T(8,128)S(1)} collective-permute-done((f32[128,128]{1,0:T(8,128)S(1)}, f32[128,128]{1,0:T(8,128)S(1)}, u32[]{:S(2)}, u32[]{:S(2)}) %collective-permute-start.7) | collective-permute-done | bytes 65568 | tf_op jit(solution)/shard_map/ppermute | solution.py:375
  28.1 1.8 %collective-permute-start.10 = (f32[72,128]{1,0:T(8,128)S(1)}, f32[72,128]{1,0:T(8,128)S(1)}, u32[]{:S(2)}, u32[]{:S(2)}) collective-permute-start(f32[72,128]{1,0:T(8,128)S(1)} %get-tuple-element.109.refs_0_), channel_id=1, source_target_pairs={{0,28},{1,29},{2,30},{3,31},{4,24},{5,25},{6,26},{7,27},{8,20},{9,... | collective-permute-start | bytes 110600 | tf_op jit(solution)/shard_map/ppermute | solution.py:375
  31.0 1.7 %collective-permute-done.10.refs_1_ = f32[72,128]{1,0:T(8,128)S(1)} collective-permute-done((f32[72,128]{1,0:T(8,128)S(1)}, f32[72,128]{1,0:T(8,128)S(1)}, u32[]{:S(2)}, u32[]{:S(2)}) %collective-permute-start.10) | collective-permute-done | bytes 36896 | tf_op jit(solution)/shard_map/ppermute | solution.py:375
  35.1 1.7 %collective-permute-start.13 = (f32[128,128]{1,0:T(8,128)S(1)}, f32[128,128]{1,0:T(8,128)S(1)}, u32[]{:S(2)}, u32[]{:S(2)}) collective-permute-start(f32[128,128]{1,0:T(8,128)S(1)} %image.5), channel_id=1, source_target_pairs={{0,5},{1,7},{2,4},{3,6},{4,2},{5,0},{6,3},{7,1},{8,14},{9,12},{10,... | collective-permute-start | bytes 196616 | tf_op jit(solution)/shard_map/ppermute | solution.py:375
  38.4 1.8 %collective-permute-start.16 = (f32[136,128]{1,0:T(8,128)S(1)}, f32[136,128]{1,0:T(8,128)S(1)}, u32[]{:S(2)}, u32[]{:S(2)}) collective-permute-start(f32[136,128]{1,0:T(8,128)S(1)} %add.52.refs_0_), channel_id=1, source_target_pairs={{0,6},{1,4},{2,7},{3,5},{4,1},{5,3},{6,0},{7,2},{8,13},{9,15},{10,... | collective-permute-start | bytes 208904 | tf_op jit(solution)/shard_map/ppermute | solution.py:375
  45.6 1.7 %collective-permute-start.17 = (f32[72,128]{1,0:T(8,128)S(1)}, f32[72,128]{1,0:T(8,128)S(1)}, u32[]{:S(2)}, u32[]{:S(2)}) collective-permute-start(f32[72,128]{1,0:T(8,128)S(1)} %get-tuple-element.125.refs_0_), channel_id=1, source_target_pairs={{0,28},{1,29},{2,30},{3,31},{4,24},{5,25},{6,26},{7,27},{8,20},{9,... | collective-permute-start | bytes 110600 | tf_op jit(solution)/shard_map/ppermute | solution.py:375
  52.6 1.7 %collective-permute-start.20 = (f32[128,128]{1,0:T(8,128)S(1)}, f32[128,128]{1,0:T(8,128)S(1)}, u32[]{:S(2)}, u32[]{:S(2)}) collective-permute-start(f32[128,128]{1,0:T(8,128)S(1)} %image.6), channel_id=1, source_target_pairs={{0,5},{1,7},{2,4},{3,6},{4,2},{5,0},{6,3},{7,1},{8,14},{9,12},{10,... | collective-permute-start | bytes 196616 | tf_op jit(solution)/shard_map/ppermute | solution.py:375
  55.9 1.6 %collective-permute-start.23 = (f32[136,128]{1,0:T(8,128)S(1)}, f32[136,128]{1,0:T(8,128)S(1)}, u32[]{:S(2)}, u32[]{:S(2)}) collective-permute-start(f32[136,128]{1,0:T(8,128)S(1)} %add.54.refs_0_), channel_id=1, source_target_pairs={{0,6},{1,4},{2,7},{3,5},{4,1},{5,3},{6,0},{7,2},{8,13},{9,15},{10,... | collective-permute-start | bytes 208904 | tf_op jit(solution)/shard_map/ppermute | solution.py:375
  57.6 2.1 %collective-permute-start.22 = (f32[128,128]{1,0:T(8,128)S(1)}, f32[128,128]{1,0:T(8,128)S(1)}, u32[]{:S(2)}, u32[]{:S(2)}) collective-permute-start(f32[128,128]{1,0:T(8,128)S(1)} %add.53.refs_0_), channel_id=1, source_target_pairs={{0,6},{1,4},{2,7},{3,5},{4,1},{5,3},{6,0},{7,2},{8,13},{9,15},{10,... | collective-permute-start | bytes 196616 | tf_op jit(solution)/shard_map/ppermute | solution.py:375
  59.7 1.7 %collective-permute-done.23.refs_1_ = f32[136,128]{1,0:T(8,128)S(1)} collective-permute-done((f32[136,128]{1,0:T(8,128)S(1)}, f32[136,128]{1,0:T(8,128)S(1)}, u32[]{:S(2)}, u32[]{:S(2)}) %collective-permute-start.23) | collective-permute-done | bytes 69664 | tf_op jit(solution)/shard_map/ppermute | solution.py:375
  69.1 1.9 %collective-permute-start.28 = (f32[136,128]{1,0:T(8,128)S(1)}, f32[136,128]{1,0:T(8,128)S(1)}, u32[]{:S(2)}, u32[]{:S(2)}) collective-permute-start(f32[136,128]{1,0:T(8,128)S(1)} %get-tuple-element.145), channel_id=1, source_target_pairs={{0,5},{1,7},{2,4},{3,6},{4,2},{5,0},{6,3},{7,1},{8,14},{9,12},{10,... | collective-permute-start | bytes 208904 | tf_op jit(solution)/shard_map/ppermute | solution.py:375
  71.5 2.1 %collective-permute-done.28 = f32[136,128]{1,0:T(8,128)S(1)} collective-permute-done((f32[136,128]{1,0:T(8,128)S(1)}, f32[136,128]{1,0:T(8,128)S(1)}, u32[]{:S(2)}, u32[]{:S(2)}) %collective-permute-start.28) | collective-permute-done | bytes 69664 | tf_op jit(solution)/shard_map/ppermute | solution.py:375
  73.6 2.3 %collective-permute-start.30 = (f32[136,128]{1,0:T(8,128)S(1)}, f32[136,128]{1,0:T(8,128)S(1)}, u32[]{:S(2)}, u32[]{:S(2)}) collective-permute-start(f32[136,128]{1,0:T(8,128)S(1)} %add.56.refs_0_), channel_id=1, source_target_pairs={{0,6},{1,4},{2,7},{3,5},{4,1},{5,3},{6,0},{7,2},{8,13},{9,15},{10,... | collective-permute-start | bytes 208904 | tf_op jit(solution)/shard_map/ppermute | solution.py:375
  78.9 2.5 %collective-permute-done.29.refs_1_ = f32[128,128]{1,0:T(8,128)S(1)} collective-permute-done((f32[128,128]{1,0:T(8,128)S(1)}, f32[128,128]{1,0:T(8,128)S(1)}, u32[]{:S(2)}, u32[]{:S(2)}) %collective-permute-start.29) | collective-permute-done | bytes 65568 | tf_op jit(solution)/shard_map/ppermute | solution.py:375
  81.9 1.6 %collective-permute-start.31 = (f32[72,128]{1,0:T(8,128)S(1)}, f32[72,128]{1,0:T(8,128)S(1)}, u32[]{:S(2)}, u32[]{:S(2)}) collective-permute-start(f32[72,128]{1,0:T(8,128)S(1)} %get-tuple-element.157.refs_0_), channel_id=1, source_target_pairs={{0,28},{1,29},{2,30},{3,31},{4,24},{5,25},{6,26},{7,27},{8,20},{9,... | collective-permute-start | bytes 110600 | tf_op jit(solution)/shard_map/ppermute | solution.py:375
  87.8 2.3 %collective-permute-start.34 = (f32[8,128]{1,0:T(8,128)S(1)}, f32[8,128]{1,0:T(8,128)S(1)}, u32[]{:S(2)}, u32[]{:S(2)}) collective-permute-start(f32[8,128]{1,0:T(8,128)S(1)} %get-tuple-element.160.refs_0_), channel_id=1, source_target_pairs={{0,3},{1,2},{2,1},{3,0},{4,7},{5,6},{6,5},{7,4},{8,11},{9,10},{10,... | collective-permute-start | bytes 12296 | tf_op jit(solution)/shard_map/ppermute | solution.py:375
  90.1 1.9 %collective-permute-start.36 = (f32[8,128]{1,0:T(8,128)S(1)}, f32[8,128]{1,0:T(8,128)S(1)}, u32[]{:S(2)}, u32[]{:S(2)}) collective-permute-start(f32[8,128]{1,0:T(8,128)S(1)} %get-tuple-element.160.refs_0_), channel_id=1, source_target_pairs={{0,5},{1,4},{2,7},{3,6},{4,1},{5,0},{6,3},{7,2},{8,13},{9,12},{10,... | collective-permute-start | bytes 12296 | tf_op jit(solution)/shard_map/ppermute | solution.py:375
  (96 shorter events, 42.8 us)
Async XLA Ops:
  4.2 4.6 %collective-permute-start.4 = (f32[4,1024,128]{2,1,0:T(8,128)}, f32[4,1024,128]{2,1,0:T(8,128)}, u32[]{:S(2)}, u32[]{:S(2)}) collective-permute-start(f32[4,1024,128]{2,1,0:T(8,128)} %a_hbm.1), channel_id=1, source_target_pairs={{0,4},{1,5},{2,6},{3,7},{4,0},{5,1},{6,2},{7,3},{8,12},{9,13},{10,... | collective-permute-start | bytes 6291464 | tf_op jit(solution)/shard_map/ppermute | solution.py:375
  4.6 10.9 %collective-permute-start.8 = (f32[24,1024]{1,0:T(8,128)S(1)}, f32[24,1024]{1,0:T(8,128)S(1)}, u32[]{:S(2)}, u32[]{:S(2)}) collective-permute-start(f32[24,1024]{1,0:T(8,128)S(1)} %get-tuple-element.101), channel_id=1, source_target_pairs={{0,4},{1,5},{2,6},{3,7},{4,0},{5,1},{6,2},{7,3},{8,12},{9,13},{10,... | collective-permute-start | bytes 294920 | tf_op jit(solution)/shard_map/ppermute | solution.py:375
  4.7 7.2 %collective-permute-start.1 = (f32[72,128]{1,0:T(8,128)S(1)}, f32[72,128]{1,0:T(8,128)S(1)}, u32[]{:S(2)}, u32[]{:S(2)}) collective-permute-start(f32[72,128]{1,0:T(8,128)S(1)} %add.48.refs_0_), channel_id=1, source_target_pairs={{0,28},{1,29},{2,30},{3,31},{4,24},{5,25},{6,26},{7,27},{8,20},{9,... | collective-permute-start | bytes 110600 | tf_op jit(solution)/shard_map/ppermute | solution.py:375
  8.3 4.0 %collective-permute-start.2 = (f32[72,128]{1,0:T(8,128)S(1)}, f32[72,128]{1,0:T(8,128)S(1)}, u32[]{:S(2)}, u32[]{:S(2)}) collective-permute-start(f32[72,128]{1,0:T(8,128)S(1)} %add.48.refs_0_), channel_id=1, source_target_pairs={{0,16},{1,17},{2,18},{3,19},{4,20},{5,21},{6,22},{7,23},{8,24},{9,... | collective-permute-start | bytes 110600 | tf_op jit(solution)/shard_map/ppermute | solution.py:375
  12.8 6.6 %collective-permute-start.6 = (f32[136,128]{1,0:T(8,128)S(1)}, f32[136,128]{1,0:T(8,128)S(1)}, u32[]{:S(2)}, u32[]{:S(2)}) collective-permute-start(f32[136,128]{1,0:T(8,128)S(1)} %get-tuple-element.99), channel_id=1, source_target_pairs={{0,5},{1,7},{2,4},{3,6},{4,2},{5,0},{6,3},{7,1},{8,14},{9,12},{10,... | collective-permute-start | bytes 208904 | tf_op jit(solution)/shard_map/ppermute | solution.py:375
  19.3 5.2 %collective-permute-start.9 = (f32[136,128]{1,0:T(8,128)S(1)}, f32[136,128]{1,0:T(8,128)S(1)}, u32[]{:S(2)}, u32[]{:S(2)}) collective-permute-start(f32[136,128]{1,0:T(8,128)S(1)} %add.50.refs_0_), channel_id=1, source_target_pairs={{0,6},{1,4},{2,7},{3,5},{4,1},{5,3},{6,0},{7,2},{8,13},{9,15},{10,... | collective-permute-start | bytes 208904 | tf_op jit(solution)/shard_map/ppermute | solution.py:375
  22.2 5.4 %collective-permute-start.7 = (f32[128,128]{1,0:T(8,128)S(1)}, f32[128,128]{1,0:T(8,128)S(1)}, u32[]{:S(2)}, u32[]{:S(2)}) collective-permute-start(f32[128,128]{1,0:T(8,128)S(1)} %add.49.refs_0_), channel_id=1, source_target_pairs={{0,6},{1,4},{2,7},{3,5},{4,1},{5,3},{6,0},{7,2},{8,13},{9,15},{10,... | collective-permute-start | bytes 196616 | tf_op jit(solution)/shard_map/ppermute | solution.py:375
  28.1 4.6 %collective-permute-start.10 = (f32[72,128]{1,0:T(8,128)S(1)}, f32[72,128]{1,0:T(8,128)S(1)}, u32[]{:S(2)}, u32[]{:S(2)}) collective-permute-start(f32[72,128]{1,0:T(8,128)S(1)} %get-tuple-element.109.refs_0_), channel_id=1, source_target_pairs={{0,28},{1,29},{2,30},{3,31},{4,24},{5,25},{6,26},{7,27},{8,20},{9,... | collective-permute-start | bytes 110600 | tf_op jit(solution)/shard_map/ppermute | solution.py:375
  29.9 4.0 %collective-permute-start.11 = (f32[72,128]{1,0:T(8,128)S(1)}, f32[72,128]{1,0:T(8,128)S(1)}, u32[]{:S(2)}, u32[]{:S(2)}) collective-permute-start(f32[72,128]{1,0:T(8,128)S(1)} %get-tuple-element.109.refs_0_), channel_id=1, source_target_pairs={{0,16},{1,17},{2,18},{3,19},{4,20},{5,21},{6,22},{7,23},{8,24},{9,... | collective-permute-start | bytes 110600 | tf_op jit(solution)/shard_map/ppermute | solution.py:375
  35.1 5.0 %collective-permute-start.13 = (f32[128,128]{1,0:T(8,128)S(1)}, f32[128,128]{1,0:T(8,128)S(1)}, u32[]{:S(2)}, u32[]{:S(2)}) collective-permute-start(f32[128,128]{1,0:T(8,128)S(1)} %image.5), channel_id=1, source_target_pairs={{0,5},{1,7},{2,4},{3,6},{4,2},{5,0},{6,3},{7,1},{8,14},{9,12},{10,... | collective-permute-start | bytes 196616 | tf_op jit(solution)/shard_map/ppermute | solution.py:375
  38.4 4.7 %collective-permute-start.16 = (f32[136,128]{1,0:T(8,128)S(1)}, f32[136,128]{1,0:T(8,128)S(1)}, u32[]{:S(2)}, u32[]{:S(2)}) collective-permute-start(f32[136,128]{1,0:T(8,128)S(1)} %add.52.refs_0_), channel_id=1, source_target_pairs={{0,6},{1,4},{2,7},{3,5},{4,1},{5,3},{6,0},{7,2},{8,13},{9,15},{10,... | collective-permute-start | bytes 208904 | tf_op jit(solution)/shard_map/ppermute | solution.py:375
  40.2 4.9 %collective-permute-start.15 = (f32[128,128]{1,0:T(8,128)S(1)}, f32[128,128]{1,0:T(8,128)S(1)}, u32[]{:S(2)}, u32[]{:S(2)}) collective-permute-start(f32[128,128]{1,0:T(8,128)S(1)} %add.51.refs_0_), channel_id=1, source_target_pairs={{0,6},{1,4},{2,7},{3,5},{4,1},{5,3},{6,0},{7,2},{8,13},{9,15},{10,... | collective-permute-start | bytes 196616 | tf_op jit(solution)/shard_map/ppermute | solution.py:375
  45.6 4.3 %collective-permute-start.17 = (f32[72,128]{1,0:T(8,128)S(1)}, f32[72,128]{1,0:T(8,128)S(1)}, u32[]{:S(2)}, u32[]{:S(2)}) collective-permute-start(f32[72,128]{1,0:T(8,128)S(1)} %get-tuple-element.125.refs_0_), channel_id=1, source_target_pairs={{0,28},{1,29},{2,30},{3,31},{4,24},{5,25},{6,26},{7,27},{8,20},{9,... | collective-permute-start | bytes 110600 | tf_op jit(solution)/shard_map/ppermute | solution.py:375
  52.6 4.9 %collective-permute-start.20 = (f32[128,128]{1,0:T(8,128)S(1)}, f32[128,128]{1,0:T(8,128)S(1)}, u32[]{:S(2)}, u32[]{:S(2)}) collective-permute-start(f32[128,128]{1,0:T(8,128)S(1)} %image.6), channel_id=1, source_target_pairs={{0,5},{1,7},{2,4},{3,6},{4,2},{5,0},{6,3},{7,1},{8,14},{9,12},{10,... | collective-permute-start | bytes 196616 | tf_op jit(solution)/shard_map/ppermute | solution.py:375
  55.9 5.4 %collective-permute-start.23 = (f32[136,128]{1,0:T(8,128)S(1)}, f32[136,128]{1,0:T(8,128)S(1)}, u32[]{:S(2)}, u32[]{:S(2)}) collective-permute-start(f32[136,128]{1,0:T(8,128)S(1)} %add.54.refs_0_), channel_id=1, source_target_pairs={{0,6},{1,4},{2,7},{3,5},{4,1},{5,3},{6,0},{7,2},{8,13},{9,15},{10,... | collective-permute-start | bytes 208904 | tf_op jit(solution)/shard_map/ppermute | solution.py:375
  57.6 4.7 %collective-permute-start.22 = (f32[128,128]{1,0:T(8,128)S(1)}, f32[128,128]{1,0:T(8,128)S(1)}, u32[]{:S(2)}, u32[]{:S(2)}) collective-permute-start(f32[128,128]{1,0:T(8,128)S(1)} %add.53.refs_0_), channel_id=1, source_target_pairs={{0,6},{1,4},{2,7},{3,5},{4,1},{5,3},{6,0},{7,2},{8,13},{9,15},{10,... | collective-permute-start | bytes 196616 | tf_op jit(solution)/shard_map/ppermute | solution.py:375
  62.7 4.3 %collective-permute-start.24 = (f32[72,128]{1,0:T(8,128)S(1)}, f32[72,128]{1,0:T(8,128)S(1)}, u32[]{:S(2)}, u32[]{:S(2)}) collective-permute-start(f32[72,128]{1,0:T(8,128)S(1)} %get-tuple-element.141.refs_0_), channel_id=1, source_target_pairs={{0,28},{1,29},{2,30},{3,31},{4,24},{5,25},{6,26},{7,27},{8,20},{9,... | collective-permute-start | bytes 110600 | tf_op jit(solution)/shard_map/ppermute | solution.py:375
  64.2 4.3 %collective-permute-start.25 = (f32[72,128]{1,0:T(8,128)S(1)}, f32[72,128]{1,0:T(8,128)S(1)}, u32[]{:S(2)}, u32[]{:S(2)}) collective-permute-start(f32[72,128]{1,0:T(8,128)S(1)} %get-tuple-element.141.refs_0_), channel_id=1, source_target_pairs={{0,16},{1,17},{2,18},{3,19},{4,20},{5,21},{6,22},{7,23},{8,24},{9,... | collective-permute-start | bytes 110600 | tf_op jit(solution)/shard_map/ppermute | solution.py:375
  69.1 4.5 %collective-permute-start.28 = (f32[136,128]{1,0:T(8,128)S(1)}, f32[136,128]{1,0:T(8,128)S(1)}, u32[]{:S(2)}, u32[]{:S(2)}) collective-permute-start(f32[136,128]{1,0:T(8,128)S(1)} %get-tuple-element.145), channel_id=1, source_target_pairs={{0,5},{1,7},{2,4},{3,6},{4,2},{5,0},{6,3},{7,1},{8,14},{9,12},{10,... | collective-permute-start | bytes 208904 | tf_op jit(solution)/shard_map/ppermute | solution.py:375
  71.5 4.5 %collective-permute-start.27 = (f32[128,128]{1,0:T(8,128)S(1)}, f32[128,128]{1,0:T(8,128)S(1)}, u32[]{:S(2)}, u32[]{:S(2)}) collective-permute-start(f32[128,128]{1,0:T(8,128)S(1)} %image.7), channel_id=1, source_target_pairs={{0,5},{1,7},{2,4},{3,6},{4,2},{5,0},{6,3},{7,1},{8,14},{9,12},{10,... | collective-permute-start | bytes 196616 | tf_op jit(solution)/shard_map/ppermute | solution.py:375
  73.6 4.7 %collective-permute-start.30 = (f32[136,128]{1,0:T(8,128)S(1)}, f32[136,128]{1,0:T(8,128)S(1)}, u32[]{:S(2)}, u32[]{:S(2)}) collective-permute-start(f32[136,128]{1,0:T(8,128)S(1)} %add.56.refs_0_), channel_id=1, source_target_pairs={{0,6},{1,4},{2,7},{3,5},{4,1},{5,3},{6,0},{7,2},{8,13},{9,15},{10,... | collective-permute-start | bytes 208904 | tf_op jit(solution)/shard_map/ppermute | solution.py:375
  76.0 5.5 %collective-permute-start.29 = (f32[128,128]{1,0:T(8,128)S(1)}, f32[128,128]{1,0:T(8,128)S(1)}, u32[]{:S(2)}, u32[]{:S(2)}) collective-permute-start(f32[128,128]{1,0:T(8,128)S(1)} %add.55.refs_0_), channel_id=1, source_target_pairs={{0,6},{1,4},{2,7},{3,5},{4,1},{5,3},{6,0},{7,2},{8,13},{9,15},{10,... | collective-permute-start | bytes 196616 | tf_op jit(solution)/shard_map/ppermute | solution.py:375
  81.9 4.4 %collective-permute-start.31 = (f32[72,128]{1,0:T(8,128)S(1)}, f32[72,128]{1,0:T(8,128)S(1)}, u32[]{:S(2)}, u32[]{:S(2)}) collective-permute-start(f32[72,128]{1,0:T(8,128)S(1)} %get-tuple-element.157.refs_0_), channel_id=1, source_target_pairs={{0,28},{1,29},{2,30},{3,31},{4,24},{5,25},{6,26},{7,27},{8,20},{9,... | collective-permute-start | bytes 110600 | tf_op jit(solution)/shard_map/ppermute | solution.py:375
  87.8 5.5 %collective-permute-start.34 = (f32[8,128]{1,0:T(8,128)S(1)}, f32[8,128]{1,0:T(8,128)S(1)}, u32[]{:S(2)}, u32[]{:S(2)}) collective-permute-start(f32[8,128]{1,0:T(8,128)S(1)} %get-tuple-element.160.refs_0_), channel_id=1, source_target_pairs={{0,3},{1,2},{2,1},{3,0},{4,7},{5,6},{6,5},{7,4},{8,11},{9,10},{10,... | collective-permute-start | bytes 12296 | tf_op jit(solution)/shard_map/ppermute | solution.py:375
  (18 other events, 79.4 us)

commit v6 on v5

--- a/solution.py
+++ b/solution.py
@@ -85,14 +85,14 @@
 def to_lines(vector, high_ref, low_ref):
     rows = vector.shape[0]
     pair = stacked(vector)
-    total = dot(pair, high_ref[...], 0) + dot(pair, low_ref[...], 0)
-    return total[:rows] + total[rows:]
+    main, rest = dot(pair, high_ref[...], 0), dot(pair[:rows], low_ref[...], 0)
+    return main[:rows] + (main[rows:] + rest)
 
 
 def from_lines(pair, z_ref, high_ref, low_ref):
     rows = pair.shape[0] // 2
-    total = dot(pair, high_ref[...], 0) + dot(pair, low_ref[...], 0)
-    image = total[:rows] + total[rows:]
+    main, rest = dot(pair, high_ref[...], 0), dot(pair[:rows], low_ref[...], 0)
+    image = main[:rows] + (main[rows:] + rest)
     for c in range(image.shape[1] // LANE):
         z_ref[c * rows:(c + 1) * rows, :] = image[:, c * LANE:(c + 1) * LANE]
 

time: 96.6 us -> 96.5 us (level)
  starting transfers between devices: 42.9 us -> 43.9 us
  transfers between devices with their start and end apart: 38 -> 38, of which waited for: 28 -> 30; matrix products, arithmetic and copies ran while one was open for 0% -> 0% of each run, Pallas kernels for 8% -> 8%
where the time goes in v6:
time: 96.5 us; the launch traced here: 96.3 us
  starting transfers between devices  43.9 us (45%)
  waiting for transfers between devices  37.1 us (38%)
  Pallas kernels  14.3 us (15%)
    ppermute x38, starting transfers between devices, swap(): return lax.ppermute(value, ('scen', 'base'), pairs)  43.9 us
    ppermute x38, waiting for transfers between devices, swap(): return lax.ppermute(value, ('scen', 'base'), pairs)  37.1 us
    pallas_call x19, Pallas kernels, call(): pl.pallas_call(body, out_shape=out_shape, in_specs=[VM] * len(args), out_...  9.13 us
    pallas_call x1, Pallas kernels, per_device(): pl.pallas_call(absorb_body, out_shape=[turned, turned, matrix, matrix, tu...  3.03 us
    pallas_call x1, Pallas kernels, per_device(): pl.pallas_call(functools.partial(prepare_body, scen=scen, bits=bits), out...  2.13 us
  transfers between devices with their start and end apart: 38, of which 30 were waited for; matrix products, arithmetic and copies ran while one was open for 0% of the time, Pallas kernels for 8%

profile of v6, /device:TPU:0, one launch (start us, length us, event | category | flops | bytes accessed | tf_op | source)
XLA Modules:
  0.0 96.3 jit_solution(3560395173016605867)
XLA Ops:
  0.7 2.1 %prepare.1 = (bf16[1024,512]{1,0:T(8,128)(2,1)S(1)}, bf16[1024,512]{1,0:T(8,128)(2,1)S(1)}, f32[72,128]{1,0:T(8,128)S(1)}, f32[72,128]{1,0:T(8,128)S(1)}, f32[16...) custom-call(f32[4,1024,128]{2,1,0:T(8,128)} %a_hbm.1, f32[32,1024]{1,0:T(8,128)} %b_hbm.1, f32[1,1024]{1,0:T(1,128)} %bitcast.1), custom_call_target="tpu_custom_call" | custom-call | tf_op jit(solution)/shard_map/prepare/pallas_call | solution.py:413
  4.7 3.5 %collective-permute-start.1 = (f32[72,128]{1,0:T(8,128)S(1)}, f32[72,128]{1,0:T(8,128)S(1)}, u32[]{:S(2)}, u32[]{:S(2)}) collective-permute-start(f32[72,128]{1,0:T(8,128)S(1)} %add.48.refs_0_), channel_id=1, source_target_pairs={{0,28},{1,29},{2,30},{3,31},{4,24},{5,25},{6,26},{7,27},{8,20},{9,... | collective-permute-start | bytes 110600 | tf_op jit(solution)/shard_map/ppermute | solution.py:375
  8.9 3.0 %absorb.1 = (bf16[512,1024]{1,0:T(8,128)(2,1)S(1)}, bf16[512,1024]{1,0:T(8,128)(2,1)S(1)}, bf16[1024,512]{1,0:T(8,128)(2,1)S(1)}, bf16[1024,512]{1,0:T(8,128)(2,...) custom-call(f32[4,1024,128]{2,1,0:T(8,128)} %collective-permute-done.4.a_hbm, ...), custom_call_target="tpu_custom_call" | custom-call | tf_op jit(solution)/shard_map/absorb/pallas_call | solution.py:440
  12.7 2.3 %collective-permute-start.6 = (f32[136,128]{1,0:T(8,128)S(1)}, f32[136,128]{1,0:T(8,128)S(1)}, u32[]{:S(2)}, u32[]{:S(2)}) collective-permute-start(f32[136,128]{1,0:T(8,128)S(1)} %get-tuple-element.99), channel_id=1, source_target_pairs={{0,5},{1,7},{2,4},{3,6},{4,2},{5,0},{6,3},{7,1},{8,14},{9,12},{10,... | collective-permute-start | bytes 208904 | tf_op jit(solution)/shard_map/ppermute | solution.py:375
  15.5 3.8 %collective-permute-done.5 = f32[128,128]{1,0:T(8,128)S(1)} collective-permute-done((f32[128,128]{1,0:T(8,128)S(1)}, f32[128,128]{1,0:T(8,128)S(1)}, u32[]{:S(2)}, u32[]{:S(2)}) %collective-permute-start.5) | collective-permute-done | bytes 65568 | tf_op jit(solution)/shard_map/ppermute | solution.py:375
  19.3 2.9 %collective-permute-start.9 = (f32[136,128]{1,0:T(8,128)S(1)}, f32[136,128]{1,0:T(8,128)S(1)}, u32[]{:S(2)}, u32[]{:S(2)}) collective-permute-start(f32[136,128]{1,0:T(8,128)S(1)} %add.50.refs_0_), channel_id=1, source_target_pairs={{0,6},{1,4},{2,7},{3,5},{4,1},{5,3},{6,0},{7,2},{8,13},{9,15},{10,... | collective-permute-start | bytes 208904 | tf_op jit(solution)/shard_map/ppermute | solution.py:375
  22.3 2.2 %collective-permute-done.9.refs_1_ = f32[136,128]{1,0:T(8,128)S(1)} collective-permute-done((f32[136,128]{1,0:T(8,128)S(1)}, f32[136,128]{1,0:T(8,128)S(1)}, u32[]{:S(2)}, u32[]{:S(2)}) %collective-permute-start.9) | collective-permute-done | bytes 69664 | tf_op jit(solution)/shard_map/ppermute | solution.py:375
  25.1 2.5 %collective-permute-done.7.refs_1_ = f32[128,128]{1,0:T(8,128)S(1)} collective-permute-done((f32[128,128]{1,0:T(8,128)S(1)}, f32[128,128]{1,0:T(8,128)S(1)}, u32[]{:S(2)}, u32[]{:S(2)}) %collective-permute-start.7) | collective-permute-done | bytes 65568 | tf_op jit(solution)/shard_map/ppermute | solution.py:375
  28.0 1.7 %collective-permute-start.10 = (f32[72,128]{1,0:T(8,128)S(1)}, f32[72,128]{1,0:T(8,128)S(1)}, u32[]{:S(2)}, u32[]{:S(2)}) collective-permute-start(f32[72,128]{1,0:T(8,128)S(1)} %get-tuple-element.109.refs_0_), channel_id=1, source_target_pairs={{0,28},{1,29},{2,30},{3,31},{4,24},{5,25},{6,26},{7,27},{8,20},{9,... | collective-permute-start | bytes 110600 | tf_op jit(solution)/shard_map/ppermute | solution.py:375
  31.0 1.6 %collective-permute-done.10.refs_1_ = f32[72,128]{1,0:T(8,128)S(1)} collective-permute-done((f32[72,128]{1,0:T(8,128)S(1)}, f32[72,128]{1,0:T(8,128)S(1)}, u32[]{:S(2)}, u32[]{:S(2)}) %collective-permute-start.10) | collective-permute-done | bytes 36896 | tf_op jit(solution)/shard_map/ppermute | solution.py:375
  35.0 1.7 %collective-permute-start.13 = (f32[128,128]{1,0:T(8,128)S(1)}, f32[128,128]{1,0:T(8,128)S(1)}, u32[]{:S(2)}, u32[]{:S(2)}) collective-permute-start(f32[128,128]{1,0:T(8,128)S(1)} %image.5), channel_id=1, source_target_pairs={{0,5},{1,7},{2,4},{3,6},{4,2},{5,0},{6,3},{7,1},{8,14},{9,12},{10,... | collective-permute-start | bytes 196616 | tf_op jit(solution)/shard_map/ppermute | solution.py:375
  38.3 1.8 %collective-permute-start.16 = (f32[136,128]{1,0:T(8,128)S(1)}, f32[136,128]{1,0:T(8,128)S(1)}, u32[]{:S(2)}, u32[]{:S(2)}) collective-permute-start(f32[136,128]{1,0:T(8,128)S(1)} %add.52.refs_0_), channel_id=1, source_target_pairs={{0,6},{1,4},{2,7},{3,5},{4,1},{5,3},{6,0},{7,2},{8,13},{9,15},{10,... | collective-permute-start | bytes 208904 | tf_op jit(solution)/shard_map/ppermute | solution.py:375
  45.5 1.7 %collective-permute-start.17 = (f32[72,128]{1,0:T(8,128)S(1)}, f32[72,128]{1,0:T(8,128)S(1)}, u32[]{:S(2)}, u32[]{:S(2)}) collective-permute-start(f32[72,128]{1,0:T(8,128)S(1)} %get-tuple-element.125.refs_0_), channel_id=1, source_target_pairs={{0,28},{1,29},{2,30},{3,31},{4,24},{5,25},{6,26},{7,27},{8,20},{9,... | collective-permute-start | bytes 110600 | tf_op jit(solution)/shard_map/ppermute | solution.py:375
  52.4 1.7 %collective-permute-start.20 = (f32[128,128]{1,0:T(8,128)S(1)}, f32[128,128]{1,0:T(8,128)S(1)}, u32[]{:S(2)}, u32[]{:S(2)}) collective-permute-start(f32[128,128]{1,0:T(8,128)S(1)} %image.6), channel_id=1, source_target_pairs={{0,5},{1,7},{2,4},{3,6},{4,2},{5,0},{6,3},{7,1},{8,14},{9,12},{10,... | collective-permute-start | bytes 196616 | tf_op jit(solution)/shard_map/ppermute | solution.py:375
  54.2 1.6 %collective-permute-done.21 = f32[136,128]{1,0:T(8,128)S(1)} collective-permute-done((f32[136,128]{1,0:T(8,128)S(1)}, f32[136,128]{1,0:T(8,128)S(1)}, u32[]{:S(2)}, u32[]{:S(2)}) %collective-permute-start.21) | collective-permute-done | bytes 69664 | tf_op jit(solution)/shard_map/ppermute | solution.py:375
  55.8 1.6 %collective-permute-start.23 = (f32[136,128]{1,0:T(8,128)S(1)}, f32[136,128]{1,0:T(8,128)S(1)}, u32[]{:S(2)}, u32[]{:S(2)}) collective-permute-start(f32[136,128]{1,0:T(8,128)S(1)} %add.54.refs_0_), channel_id=1, source_target_pairs={{0,6},{1,4},{2,7},{3,5},{4,1},{5,3},{6,0},{7,2},{8,13},{9,15},{10,... | collective-permute-start | bytes 208904 | tf_op jit(solution)/shard_map/ppermute | solution.py:375
  57.4 2.1 %collective-permute-start.22 = (f32[128,128]{1,0:T(8,128)S(1)}, f32[128,128]{1,0:T(8,128)S(1)}, u32[]{:S(2)}, u32[]{:S(2)}) collective-permute-start(f32[128,128]{1,0:T(8,128)S(1)} %add.53.refs_0_), channel_id=1, source_target_pairs={{0,6},{1,4},{2,7},{3,5},{4,1},{5,3},{6,0},{7,2},{8,13},{9,15},{10,... | collective-permute-start | bytes 196616 | tf_op jit(solution)/shard_map/ppermute | solution.py:375
  59.5 1.7 %collective-permute-done.23.refs_1_ = f32[136,128]{1,0:T(8,128)S(1)} collective-permute-done((f32[136,128]{1,0:T(8,128)S(1)}, f32[136,128]{1,0:T(8,128)S(1)}, u32[]{:S(2)}, u32[]{:S(2)}) %collective-permute-start.23) | collective-permute-done | bytes 69664 | tf_op jit(solution)/shard_map/ppermute | solution.py:375
  71.2 1.7 %collective-permute-done.28 = f32[136,128]{1,0:T(8,128)S(1)} collective-permute-done((f32[136,128]{1,0:T(8,128)S(1)}, f32[136,128]{1,0:T(8,128)S(1)}, u32[]{:S(2)}, u32[]{:S(2)}) %collective-permute-start.28) | collective-permute-done | bytes 69664 | tf_op jit(solution)/shard_map/ppermute | solution.py:375
  72.9 2.7 %collective-permute-start.30 = (f32[136,128]{1,0:T(8,128)S(1)}, f32[136,128]{1,0:T(8,128)S(1)}, u32[]{:S(2)}, u32[]{:S(2)}) collective-permute-start(f32[136,128]{1,0:T(8,128)S(1)} %add.56.refs_0_), channel_id=1, source_target_pairs={{0,6},{1,4},{2,7},{3,5},{4,1},{5,3},{6,0},{7,2},{8,13},{9,15},{10,... | collective-permute-start | bytes 208904 | tf_op jit(solution)/shard_map/ppermute | solution.py:375
  75.6 2.0 %collective-permute-start.29 = (f32[128,128]{1,0:T(8,128)S(1)}, f32[128,128]{1,0:T(8,128)S(1)}, u32[]{:S(2)}, u32[]{:S(2)}) collective-permute-start(f32[128,128]{1,0:T(8,128)S(1)} %add.55.refs_0_), channel_id=1, source_target_pairs={{0,6},{1,4},{2,7},{3,5},{4,1},{5,3},{6,0},{7,2},{8,13},{9,15},{10,... | collective-permute-start | bytes 196616 | tf_op jit(solution)/shard_map/ppermute | solution.py:375
  78.6 2.4 %collective-permute-done.29.refs_1_ = f32[128,128]{1,0:T(8,128)S(1)} collective-permute-done((f32[128,128]{1,0:T(8,128)S(1)}, f32[128,128]{1,0:T(8,128)S(1)}, u32[]{:S(2)}, u32[]{:S(2)}) %collective-permute-start.29) | collective-permute-done | bytes 65568 | tf_op jit(solution)/shard_map/ppermute | solution.py:375
  88.0 2.0 %collective-permute-start.34 = (f32[8,128]{1,0:T(8,128)S(1)}, f32[8,128]{1,0:T(8,128)S(1)}, u32[]{:S(2)}, u32[]{:S(2)}) collective-permute-start(f32[8,128]{1,0:T(8,128)S(1)} %get-tuple-element.160.refs_0_), channel_id=1, source_target_pairs={{0,3},{1,2},{2,1},{3,0},{4,7},{5,6},{6,5},{7,4},{8,11},{9,10},{10,... | collective-permute-start | bytes 12296 | tf_op jit(solution)/shard_map/ppermute | solution.py:375
  90.0 2.2 %collective-permute-start.36 = (f32[8,128]{1,0:T(8,128)S(1)}, f32[8,128]{1,0:T(8,128)S(1)}, u32[]{:S(2)}, u32[]{:S(2)}) collective-permute-start(f32[8,128]{1,0:T(8,128)S(1)} %get-tuple-element.160.refs_0_), channel_id=1, source_target_pairs={{0,5},{1,4},{2,7},{3,6},{4,1},{5,0},{6,3},{7,2},{8,13},{9,12},{10,... | collective-permute-start | bytes 12296 | tf_op jit(solution)/shard_map/ppermute | solution.py:375
  (96 shorter events, 43.0 us)
Async XLA Ops:
  4.2 4.6 %collective-permute-start.4 = (f32[4,1024,128]{2,1,0:T(8,128)}, f32[4,1024,128]{2,1,0:T(8,128)}, u32[]{:S(2)}, u32[]{:S(2)}) collective-permute-start(f32[4,1024,128]{2,1,0:T(8,128)} %a_hbm.1), channel_id=1, source_target_pairs={{0,4},{1,5},{2,6},{3,7},{4,0},{5,1},{6,2},{7,3},{8,12},{9,13},{10,... | collective-permute-start | bytes 6291464 | tf_op jit(solution)/shard_map/ppermute | solution.py:375
  4.6 10.9 %collective-permute-start.8 = (f32[24,1024]{1,0:T(8,128)S(1)}, f32[24,1024]{1,0:T(8,128)S(1)}, u32[]{:S(2)}, u32[]{:S(2)}) collective-permute-start(f32[24,1024]{1,0:T(8,128)S(1)} %get-tuple-element.101), channel_id=1, source_target_pairs={{0,4},{1,5},{2,6},{3,7},{4,0},{5,1},{6,2},{7,3},{8,12},{9,13},{10,... | collective-permute-start | bytes 294920 | tf_op jit(solution)/shard_map/ppermute | solution.py:375
  4.7 7.2 %collective-permute-start.1 = (f32[72,128]{1,0:T(8,128)S(1)}, f32[72,128]{1,0:T(8,128)S(1)}, u32[]{:S(2)}, u32[]{:S(2)}) collective-permute-start(f32[72,128]{1,0:T(8,128)S(1)} %add.48.refs_0_), channel_id=1, source_target_pairs={{0,28},{1,29},{2,30},{3,31},{4,24},{5,25},{6,26},{7,27},{8,20},{9,... | collective-permute-start | bytes 110600 | tf_op jit(solution)/shard_map/ppermute | solution.py:375
  8.3 4.0 %collective-permute-start.2 = (f32[72,128]{1,0:T(8,128)S(1)}, f32[72,128]{1,0:T(8,128)S(1)}, u32[]{:S(2)}, u32[]{:S(2)}) collective-permute-start(f32[72,128]{1,0:T(8,128)S(1)} %add.48.refs_0_), channel_id=1, source_target_pairs={{0,16},{1,17},{2,18},{3,19},{4,20},{5,21},{6,22},{7,23},{8,24},{9,... | collective-permute-start | bytes 110600 | tf_op jit(solution)/shard_map/ppermute | solution.py:375
  12.7 6.5 %collective-permute-start.6 = (f32[136,128]{1,0:T(8,128)S(1)}, f32[136,128]{1,0:T(8,128)S(1)}, u32[]{:S(2)}, u32[]{:S(2)}) collective-permute-start(f32[136,128]{1,0:T(8,128)S(1)} %get-tuple-element.99), channel_id=1, source_target_pairs={{0,5},{1,7},{2,4},{3,6},{4,2},{5,0},{6,3},{7,1},{8,14},{9,12},{10,... | collective-permute-start | bytes 208904 | tf_op jit(solution)/shard_map/ppermute | solution.py:375
  19.3 5.2 %collective-permute-start.9 = (f32[136,128]{1,0:T(8,128)S(1)}, f32[136,128]{1,0:T(8,128)S(1)}, u32[]{:S(2)}, u32[]{:S(2)}) collective-permute-start(f32[136,128]{1,0:T(8,128)S(1)} %add.50.refs_0_), channel_id=1, source_target_pairs={{0,6},{1,4},{2,7},{3,5},{4,1},{5,3},{6,0},{7,2},{8,13},{9,15},{10,... | collective-permute-start | bytes 208904 | tf_op jit(solution)/shard_map/ppermute | solution.py:375
  22.2 5.3 %collective-permute-start.7 = (f32[128,128]{1,0:T(8,128)S(1)}, f32[128,128]{1,0:T(8,128)S(1)}, u32[]{:S(2)}, u32[]{:S(2)}) collective-permute-start(f32[128,128]{1,0:T(8,128)S(1)} %add.49.refs_0_), channel_id=1, source_target_pairs={{0,6},{1,4},{2,7},{3,5},{4,1},{5,3},{6,0},{7,2},{8,13},{9,15},{10,... | collective-permute-start | bytes 196616 | tf_op jit(solution)/shard_map/ppermute | solution.py:375
  28.0 4.6 %collective-permute-start.10 = (f32[72,128]{1,0:T(8,128)S(1)}, f32[72,128]{1,0:T(8,128)S(1)}, u32[]{:S(2)}, u32[]{:S(2)}) collective-permute-start(f32[72,128]{1,0:T(8,128)S(1)} %get-tuple-element.109.refs_0_), channel_id=1, source_target_pairs={{0,28},{1,29},{2,30},{3,31},{4,24},{5,25},{6,26},{7,27},{8,20},{9,... | collective-permute-start | bytes 110600 | tf_op jit(solution)/shard_map/ppermute | solution.py:375
  29.8 4.0 %collective-permute-start.11 = (f32[72,128]{1,0:T(8,128)S(1)}, f32[72,128]{1,0:T(8,128)S(1)}, u32[]{:S(2)}, u32[]{:S(2)}) collective-permute-start(f32[72,128]{1,0:T(8,128)S(1)} %get-tuple-element.109.refs_0_), channel_id=1, source_target_pairs={{0,16},{1,17},{2,18},{3,19},{4,20},{5,21},{6,22},{7,23},{8,24},{9,... | collective-permute-start | bytes 110600 | tf_op jit(solution)/shard_map/ppermute | solution.py:375
  35.0 5.0 %collective-permute-start.13 = (f32[128,128]{1,0:T(8,128)S(1)}, f32[128,128]{1,0:T(8,128)S(1)}, u32[]{:S(2)}, u32[]{:S(2)}) collective-permute-start(f32[128,128]{1,0:T(8,128)S(1)} %image.5), channel_id=1, source_target_pairs={{0,5},{1,7},{2,4},{3,6},{4,2},{5,0},{6,3},{7,1},{8,14},{9,12},{10,... | collective-permute-start | bytes 196616 | tf_op jit(solution)/shard_map/ppermute | solution.py:375
  38.3 4.7 %collective-permute-start.16 = (f32[136,128]{1,0:T(8,128)S(1)}, f32[136,128]{1,0:T(8,128)S(1)}, u32[]{:S(2)}, u32[]{:S(2)}) collective-permute-start(f32[136,128]{1,0:T(8,128)S(1)} %add.52.refs_0_), channel_id=1, source_target_pairs={{0,6},{1,4},{2,7},{3,5},{4,1},{5,3},{6,0},{7,2},{8,13},{9,15},{10,... | collective-permute-start | bytes 208904 | tf_op jit(solution)/shard_map/ppermute | solution.py:375
  40.1 4.9 %collective-permute-start.15 = (f32[128,128]{1,0:T(8,128)S(1)}, f32[128,128]{1,0:T(8,128)S(1)}, u32[]{:S(2)}, u32[]{:S(2)}) collective-permute-start(f32[128,128]{1,0:T(8,128)S(1)} %add.51.refs_0_), channel_id=1, source_target_pairs={{0,6},{1,4},{2,7},{3,5},{4,1},{5,3},{6,0},{7,2},{8,13},{9,15},{10,... | collective-permute-start | bytes 196616 | tf_op jit(solution)/shard_map/ppermute | solution.py:375
  45.5 4.3 %collective-permute-start.17 = (f32[72,128]{1,0:T(8,128)S(1)}, f32[72,128]{1,0:T(8,128)S(1)}, u32[]{:S(2)}, u32[]{:S(2)}) collective-permute-start(f32[72,128]{1,0:T(8,128)S(1)} %get-tuple-element.125.refs_0_), channel_id=1, source_target_pairs={{0,28},{1,29},{2,30},{3,31},{4,24},{5,25},{6,26},{7,27},{8,20},{9,... | collective-permute-start | bytes 110600 | tf_op jit(solution)/shard_map/ppermute | solution.py:375
  47.2 4.0 %collective-permute-start.18 = (f32[72,128]{1,0:T(8,128)S(1)}, f32[72,128]{1,0:T(8,128)S(1)}, u32[]{:S(2)}, u32[]{:S(2)}) collective-permute-start(f32[72,128]{1,0:T(8,128)S(1)} %get-tuple-element.125.refs_0_), channel_id=1, source_target_pairs={{0,16},{1,17},{2,18},{3,19},{4,20},{5,21},{6,22},{7,23},{8,24},{9,... | collective-permute-start | bytes 110600 | tf_op jit(solution)/shard_map/ppermute | solution.py:375
  52.4 4.9 %collective-permute-start.20 = (f32[128,128]{1,0:T(8,128)S(1)}, f32[128,128]{1,0:T(8,128)S(1)}, u32[]{:S(2)}, u32[]{:S(2)}) collective-permute-start(f32[128,128]{1,0:T(8,128)S(1)} %image.6), channel_id=1, source_target_pairs={{0,5},{1,7},{2,4},{3,6},{4,2},{5,0},{6,3},{7,1},{8,14},{9,12},{10,... | collective-permute-start | bytes 196616 | tf_op jit(solution)/shard_map/ppermute | solution.py:375
  55.8 5.4 %collective-permute-start.23 = (f32[136,128]{1,0:T(8,128)S(1)}, f32[136,128]{1,0:T(8,128)S(1)}, u32[]{:S(2)}, u32[]{:S(2)}) collective-permute-start(f32[136,128]{1,0:T(8,128)S(1)} %add.54.refs_0_), channel_id=1, source_target_pairs={{0,6},{1,4},{2,7},{3,5},{4,1},{5,3},{6,0},{7,2},{8,13},{9,15},{10,... | collective-permute-start | bytes 208904 | tf_op jit(solution)/shard_map/ppermute | solution.py:375
  57.4 4.7 %collective-permute-start.22 = (f32[128,128]{1,0:T(8,128)S(1)}, f32[128,128]{1,0:T(8,128)S(1)}, u32[]{:S(2)}, u32[]{:S(2)}) collective-permute-start(f32[128,128]{1,0:T(8,128)S(1)} %add.53.refs_0_), channel_id=1, source_target_pairs={{0,6},{1,4},{2,7},{3,5},{4,1},{5,3},{6,0},{7,2},{8,13},{9,15},{10,... | collective-permute-start | bytes 196616 | tf_op jit(solution)/shard_map/ppermute | solution.py:375
  62.5 4.3 %collective-permute-start.24 = (f32[72,128]{1,0:T(8,128)S(1)}, f32[72,128]{1,0:T(8,128)S(1)}, u32[]{:S(2)}, u32[]{:S(2)}) collective-permute-start(f32[72,128]{1,0:T(8,128)S(1)} %get-tuple-element.141.refs_0_), channel_id=1, source_target_pairs={{0,28},{1,29},{2,30},{3,31},{4,24},{5,25},{6,26},{7,27},{8,20},{9,... | collective-permute-start | bytes 110600 | tf_op jit(solution)/shard_map/ppermute | solution.py:375
  64.0 4.1 %collective-permute-start.25 = (f32[72,128]{1,0:T(8,128)S(1)}, f32[72,128]{1,0:T(8,128)S(1)}, u32[]{:S(2)}, u32[]{:S(2)}) collective-permute-start(f32[72,128]{1,0:T(8,128)S(1)} %get-tuple-element.141.refs_0_), channel_id=1, source_target_pairs={{0,16},{1,17},{2,18},{3,19},{4,20},{5,21},{6,22},{7,23},{8,24},{9,... | collective-permute-start | bytes 110600 | tf_op jit(solution)/shard_map/ppermute | solution.py:375
  70.9 4.8 %collective-permute-start.27 = (f32[128,128]{1,0:T(8,128)S(1)}, f32[128,128]{1,0:T(8,128)S(1)}, u32[]{:S(2)}, u32[]{:S(2)}) collective-permute-start(f32[128,128]{1,0:T(8,128)S(1)} %image.7), channel_id=1, source_target_pairs={{0,5},{1,7},{2,4},{3,6},{4,2},{5,0},{6,3},{7,1},{8,14},{9,12},{10,... | collective-permute-start | bytes 196616 | tf_op jit(solution)/shard_map/ppermute | solution.py:375
  72.9 5.1 %collective-permute-start.30 = (f32[136,128]{1,0:T(8,128)S(1)}, f32[136,128]{1,0:T(8,128)S(1)}, u32[]{:S(2)}, u32[]{:S(2)}) collective-permute-start(f32[136,128]{1,0:T(8,128)S(1)} %add.56.refs_0_), channel_id=1, source_target_pairs={{0,6},{1,4},{2,7},{3,5},{4,1},{5,3},{6,0},{7,2},{8,13},{9,15},{10,... | collective-permute-start | bytes 208904 | tf_op jit(solution)/shard_map/ppermute | solution.py:375
  75.6 5.4 %collective-permute-start.29 = (f32[128,128]{1,0:T(8,128)S(1)}, f32[128,128]{1,0:T(8,128)S(1)}, u32[]{:S(2)}, u32[]{:S(2)}) collective-permute-start(f32[128,128]{1,0:T(8,128)S(1)} %add.55.refs_0_), channel_id=1, source_target_pairs={{0,6},{1,4},{2,7},{3,5},{4,1},{5,3},{6,0},{7,2},{8,13},{9,15},{10,... | collective-permute-start | bytes 196616 | tf_op jit(solution)/shard_map/ppermute | solution.py:375
  81.5 4.5 %collective-permute-start.31 = (f32[72,128]{1,0:T(8,128)S(1)}, f32[72,128]{1,0:T(8,128)S(1)}, u32[]{:S(2)}, u32[]{:S(2)}) collective-permute-start(f32[72,128]{1,0:T(8,128)S(1)} %get-tuple-element.157.refs_0_), channel_id=1, source_target_pairs={{0,28},{1,29},{2,30},{3,31},{4,24},{5,25},{6,26},{7,27},{8,20},{9,... | collective-permute-start | bytes 110600 | tf_op jit(solution)/shard_map/ppermute | solution.py:375
  88.0 5.5 %collective-permute-start.34 = (f32[8,128]{1,0:T(8,128)S(1)}, f32[8,128]{1,0:T(8,128)S(1)}, u32[]{:S(2)}, u32[]{:S(2)}) collective-permute-start(f32[8,128]{1,0:T(8,128)S(1)} %get-tuple-element.160.refs_0_), channel_id=1, source_target_pairs={{0,3},{1,2},{2,1},{3,0},{4,7},{5,6},{6,5},{7,4},{8,11},{9,10},{10,... | collective-permute-start | bytes 12296 | tf_op jit(solution)/shard_map/ppermute | solution.py:375
  (18 other events, 79.5 us)
